TPU v7x, 768 devices: a whole 4x8x12 slice. The times are simulated.
768 devices in a mesh: wall: 64 (over x, y, core), span: 12 (over z).
Axes of the slice: x: 4, y: 8, z: 12, core: 2. Of those that a mesh axis runs over, the one named last changes fastest.
Arguments:
- velocity_old: float32 [3, 1024, 192, 128], P(None, 'wall', 'span'), may hold values from -12 to 12, as said below
- heights: float32 [16], replicated, may hold values from 0.04 to 0.25
- owner_device: int32 [393216, 1], P(('wall', 'span')), may hold values from 0 to 63, as said below
- owner_element: int32 [393216, 1], P(('wall', 'span')), may hold values from 0 to 63, as said below
- ref_coords: float32 [3, 393216], P(None, ('wall', 'span')), may hold values from -1 to 1
- roughness: float32 [393216], P(('wall', 'span')), may hold values from 0.0001 to 0.01
Outputs:
- velocity_new: float32 [3, 1024, 192, 128], P(None, 'wall', 'span')
- neumann: float32 [2, 393216], P(None, ('wall', 'span'))
Inputs may be any that keep to these rules, and one draw needn't show every extreme that they name: `velocity_old`: values at coinciding nodes of neighbouring elements are equal. `owner_device`: the owner is the streamwise index w of the point's own device, or w + 1 or w - 1 modulo 64. Among the rows of one device at most 128 name w + 1 and at most 128 name w - 1; some device has exactly 128 for w + 1 and some device exactly 128 for w - 1. `owner_element`: the element index is (ex * 2 + ez) * 16 + ey with ex = i // 8 and ez = j // 8 of the wall point; ey < 2 for points of the first wall, ey >= 14 for the second.
All inputs are finite; a program needn't handle non-finite values.
Results may differ from a plain program's by a relative error of at most 0.0003.
Values sent between devices are 32-bit elements; how exact they have to be, the bound alone decides.
A program may use at most 128 MiB of HBM per device.

v0:
```python
import math

import jax
import jax.numpy as jnp
import numpy as np
from jax import lax
from jax.sharding import Mesh
from jax.sharding import PartitionSpec as P

ITERS = 3
WALL_SPAN = ("wall_0", "wall_1", "wall_2", "span")
WALL = ("wall_0", "wall_1", "wall_2")


GLL_NODES = (
    -1.0,
    -0.8717401485096066,
    -0.5917001814331423,
    -0.2092992179024789,
    0.2092992179024789,
    0.5917001814331423,
    0.8717401485096066,
    1.0,
)
GLL_WEIGHTS = (
    0.03571428571428571,
    0.2107042271435061,
    0.3411226924835044,
    0.4124587946587038,
    0.4124587946587038,
    0.3411226924835044,
    0.2107042271435061,
    0.03571428571428571,
)
viscosity = 0.02
inverse_step = 20.0
karman = 0.41
sample_height = 0.1
speed_floor = 0.01
element_dx = 0.05
element_dz = 0.13
precise = lax.Precision.HIGHEST


def with_halo(cells, sides, width):
    for axis, dim in sides:
        count = lax.axis_size(axis)
        head = lax.slice_in_dim(cells, 0, width, axis=dim)
        tail = lax.slice_in_dim(cells, cells.shape[dim] - width, cells.shape[dim], axis=dim)
        cells = jnp.concatenate(
            [
                lax.ppermute(tail, axis, [(i, (i + 1) % count) for i in range(count)]),
                cells,
                lax.ppermute(head, axis, [((i + 1) % count, i) for i in range(count)]),
            ],
            axis=dim,
        )
    return cells


def one_axis_at_a_time(x, axes):
    for axis in axes:
        x = lax.psum(x, axis)
    return x


def shifted(value, axis, steps):
    count = lax.axis_size(axis)
    pairs = [(source, (source + steps) % count) for source in range(count)]
    return lax.ppermute(value, axis, pairs)


def stiffness_table():
    points = np.array(GLL_NODES)
    weights = np.array(GLL_WEIGHTS)
    previous = np.ones(8)
    current = points.copy()
    for degree in range(1, 7):
        previous, current = (
            current,
            ((2 * degree + 1) * points * current - degree * previous) / (degree + 1),
        )
    derivative = np.zeros((8, 8))
    for target in range(8):
        for source in range(8):
            if target != source:
                derivative[target, source] = (
                    current[target] / current[source] / (points[target] - points[source])
                )
    derivative[0, 0] = -14.0
    derivative[7, 7] = 14.0
    return derivative.T @ (weights[:, None] * derivative)


def lagrange(coord):
    points = np.array(GLL_NODES)
    gaps_table = points[:, None] - points[None, :] + np.eye(8)
    scale_row = jnp.asarray(1.0 / np.prod(gaps_table, axis=1), jnp.float32)
    gaps = coord[:, None] - jnp.asarray(points, jnp.float32)[None, :]
    filled = jnp.where(jnp.asarray(np.eye(8) > 0.5)[None], jnp.float32(1.0), gaps[:, None, :])
    return jnp.prod(filled, axis=2) * scale_row[None, :]


def face_weights(length, open_ends):
    values = np.ones(length)
    position = np.arange(length) % 8
    values[(position == 0) | (position == 7)] = 0.5
    if open_ends:
        values[0] = 1.0
        values[-1] = 1.0
    return values


def join_faces(core, before, after, axis):
    count = core.shape[axis] // 8
    blocks = core.reshape(core.shape[:axis] + (count, 8) + core.shape[axis + 1 :])
    first = lax.slice_in_dim(blocks, 0, 1, axis=axis + 1)
    last = lax.slice_in_dim(blocks, 7, 8, axis=axis + 1)
    before_b = jnp.expand_dims(before, axis + 1)
    after_b = jnp.expand_dims(after, axis + 1)
    prev_last = jnp.concatenate([before_b, lax.slice_in_dim(last, 0, count - 1, axis=axis)], axis)
    next_first = jnp.concatenate([lax.slice_in_dim(first, 1, count, axis=axis), after_b], axis)
    middle = lax.slice_in_dim(blocks, 1, 7, axis=axis + 1)
    joined = jnp.concatenate([first + prev_last, middle, last + next_first], axis + 1)
    return joined.reshape(core.shape)


def assemble(local):
    padded = with_halo(local, ((WALL, 1), ("span", 2)), 1)
    joined_x = join_faces(padded[:, 1:-1], padded[:, :1], padded[:, -1:], 1)
    joined_z = join_faces(joined_x[:, :, 1:-1], joined_x[:, :, :1], joined_x[:, :, -1:], 2)
    border = jnp.zeros(joined_z.shape[:3] + (1,), jnp.float32)
    return join_faces(joined_z, border, border, 3)


def paired_total(first, second):
    return (one_axis_at_a_time(first, WALL_SPAN), one_axis_at_a_time(second, WALL_SPAN))


def spread(values):
    return values[:, None, None, None]


def slot_numbers(selected, capacity):
    ranking = jnp.cumsum(selected.astype(jnp.int32)) - 1
    return jnp.where(selected, ranking, capacity)


def body(velocity_old, heights, owner_device, owner_element, ref_coords, roughness):
    weights = np.array(GLL_WEIGHTS)
    stiffness = stiffness_table()
    length_x, length_z, length_y = (
        velocity_old.shape[1],
        velocity_old.shape[2],
        velocity_old.shape[3],
    )
    count_x, count_z, count_y = (length_x // 8, length_z // 8, length_y // 8)
    stiff_x = jnp.asarray(np.kron(np.eye(count_x), stiffness * (2.0 / element_dx)), jnp.float32)
    stiff_z = jnp.asarray(np.kron(np.eye(count_z), stiffness * (2.0 / element_dz)), jnp.float32)
    blocks = (2.0 / heights)[:, None, None] * jnp.asarray(stiffness, jnp.float32)[None]
    stiff_y = jnp.einsum("ef,eab->eafb", jnp.eye(count_y, dtype=jnp.float32), blocks).reshape(
        length_y, length_y
    )
    mass_x = jnp.asarray(np.tile(0.5 * element_dx * weights, count_x), jnp.float32)
    mass_z = jnp.asarray(np.tile(0.5 * element_dz * weights, count_z), jnp.float32)
    mass_y = (0.5 * heights[:, None] * jnp.asarray(weights, jnp.float32)[None, :]).reshape(length_y)
    mass_xb = mass_x[None, :, None, None]
    mass_zb = mass_z[None, None, :, None]
    mass_yb = mass_y[None, None, None, :]
    mass_all = mass_xb * mass_zb * mass_yb
    inverse_count = jnp.asarray(
        face_weights(length_x, False)[:, None, None]
        * face_weights(length_z, False)[None, :, None]
        * face_weights(length_y, True)[None, None, :],
        jnp.float32,
    )

    def operate(field):
        along_x = jnp.einsum("ab,cbzy->cazy", stiff_x, field, precision=precise)
        along_z = jnp.einsum("ab,cxby->cxay", stiff_z, field, precision=precise)
        along_y = jnp.einsum("cxzb,ab->cxza", field, stiff_y, precision=precise)
        local = (
            viscosity
            * (
                along_x * mass_zb * mass_yb
                + mass_xb * along_z * mass_yb
                + mass_xb * mass_zb * along_y
            )
            + inverse_step * mass_all * field
        )
        return assemble(local)

    def weighted(first, second):
        return jnp.sum(first * second * inverse_count[None], axis=(1, 2, 3))

    element_rows = (
        velocity_old.reshape(3, count_x, 8, count_z, 8, count_y, 8)
        .transpose(1, 3, 5, 0, 2, 4, 6)
        .reshape(count_x * count_z * count_y, 3 * 512)
    )

    def interpolate(ids_in, coords_in):
        point_total = ids_in.shape[0]
        groups = math.gcd(point_total, 8)
        grouped_ids = ids_in.reshape(groups, point_total // groups)
        grouped_coords = coords_in.T.reshape(groups, point_total // groups, 3)

        def evaluate(pieces):
            row_ids, coords = pieces
            values = element_rows[row_ids].reshape(row_ids.shape[0], 3, 8, 8, 8)
            return jnp.einsum(
                "gcabd,ga,gb,gd->gc",
                values,
                lagrange(coords[:, 0]),
                lagrange(coords[:, 1]),
                lagrange(coords[:, 2]),
                precision=precise,
            )

        result = lax.map(evaluate, (grouped_ids, grouped_coords))
        return result.reshape(point_total, 3).T

    wall_count = lax.axis_size(WALL)
    point_count = owner_device.shape[0]
    capacity = point_count // 4
    own_wall = lax.axis_index(WALL)
    distance = (owner_device[:, 0] - own_wall + wall_count) % wall_count
    to_next = distance == 1
    to_prev = distance == wall_count - 1
    slot_next = slot_numbers(to_next, capacity)
    slot_prev = slot_numbers(to_prev, capacity)
    packed = jnp.concatenate([owner_element[:, 0].astype(jnp.float32)[None], ref_coords], axis=0)
    empty_buffer = jnp.zeros((4, capacity + 1), jnp.float32)
    send_next = empty_buffer.at[:, slot_next].set(packed)[:, :capacity]
    send_prev = empty_buffer.at[:, slot_prev].set(packed)[:, :capacity]
    got_next = shifted(send_next, WALL, 1)
    got_prev = shifted(send_prev, WALL, -1)
    answer_next = interpolate(got_next[0].astype(jnp.int32), got_next[1:])
    answer_prev = interpolate(got_prev[0].astype(jnp.int32), got_prev[1:])
    back_next = shifted(answer_next, WALL, -1)
    back_prev = shifted(answer_prev, WALL, 1)
    own_values = interpolate(owner_element[:, 0], ref_coords)
    zero_column = jnp.zeros((3, 1), jnp.float32)
    from_next = jnp.concatenate([back_next, zero_column], axis=1)[:, slot_next]
    from_prev = jnp.concatenate([back_prev, zero_column], axis=1)[:, slot_prev]
    velocity_pts = jnp.where(
        to_next[None], from_next, jnp.where(to_prev[None], from_prev, own_values)
    )
    stream = velocity_pts[0]
    spanwise = velocity_pts[2]
    wall_speed = jnp.sqrt(stream * stream + spanwise * spanwise + speed_floor)
    drag_coeff = (karman / jnp.log(sample_height / roughness)) ** 2
    neumann = -(drag_coeff * wall_speed / viscosity)[None, :] * jnp.stack([stream, spanwise])
    traction = (viscosity * neumann).reshape(2, 2, length_x, length_z) * (
        mass_x[:, None] * mass_z[None, :]
    )[None, None]
    zero_plane = jnp.zeros((1, length_x, length_z), jnp.float32)
    bottom = jnp.concatenate([traction[0:1, 0], zero_plane, traction[1:2, 0]], axis=0)
    top_wall = jnp.concatenate([traction[0:1, 1], zero_plane, traction[1:2, 1]], axis=0)
    forcing = inverse_step * mass_all * velocity_old
    forcing = forcing.at[:, :, :, 0].add(bottom).at[:, :, :, -1].add(top_wall)
    right_side = assemble(forcing)
    solution = jnp.zeros_like(right_side)
    residual = right_side
    applied = operate(residual)
    norm_now, product = paired_total(weighted(residual, residual), weighted(residual, applied))
    step_size = norm_now / product
    direction = residual
    along_dir = applied
    for sweep in range(ITERS):
        solution = solution + spread(step_size) * direction
        residual = residual - spread(step_size) * along_dir
        if sweep + 1 < ITERS:
            applied = operate(residual)
            norm_next, product = paired_total(
                weighted(residual, residual), weighted(residual, applied)
            )
            growth = norm_next / norm_now
            step_size = norm_next / (product - growth * norm_next / step_size)
            direction = residual + spread(growth) * direction
            along_dir = applied + spread(growth) * along_dir
            norm_now = norm_next
    return (solution, neumann)


def solution(mesh):
    torus = Mesh(
        mesh.devices.reshape(4, 8, 2, mesh.shape["span"]), ("wall_0", "wall_1", "wall_2", "span")
    )
    return jax.shard_map(
        body,
        mesh=torus,
        in_specs=(
            P(None, WALL, "span", None),
            P(),
            P(WALL_SPAN, None),
            P(WALL_SPAN, None),
            P(None, WALL_SPAN),
            P(WALL_SPAN),
        ),
        out_specs=(P(None, WALL, "span", None), P(None, WALL_SPAN)),
        check_vma=False,
    )
```

profile of v0, /device:TPU:10, one launch (start us, length us, event | category | flops | bytes accessed | tf_op | source)
XLA Modules:
  0.0 494.7 jit_solution(15787831424144379020)
XLA Ops:
  16.2 5.9 %reshape.740 = f32[3,2,8,2,8,16,8]{6,5,4,3,2,1,0:T(8,128)} reshape(f32[3,16,16,128]{3,2,1,0:T(8,128)} %param.50) | data formatting | bytes 786432 | tf_op jit(solution)/shard_map/reshape | solution.py:197
  23.1 6.7 %copy.466 = f32[2,2,16,3,8,8,8]{2,1,0,6,5,4,3:T(2,128)} copy(f32[2,2,16,3,8,8,8]{6,2,5,1,4,0,3:T(8,128)} %bitcast.359) | data formatting | bytes 786432 | tf_op jit(solution)/shard_map/transpose | solution.py:198
  29.9 4.0 reshape.741
  34.2 18.7 %while.40 = (s32[]{:T(128)}, f32[8,64,3]{1,0,2:T(8,128)S(1)}, f32[8,64,3]{1,0,2:T(8,128)S(1)}, s32[8,64]{1,0:T(8,128)S(1)}, f32[64,1536]{1,0:T(8,128)S(1)}, /*in...) while((s32[]{:T(128)}, f32[8,64,3]{1,0,2:T(8,128)S(1)}, ...), condition=%wide.region_20.21_spmd.clone.clone, body=%wide.region_16.20_spmd.sunk.clone.clone.sunk | while | flops 229378 | bytes 2121465 | solution.py:220
  53.8 15.5 %while.39 = (s32[]{:T(128)}, f32[8,16,3]{1,2,0:T(4,128)S(1)}, f32[8,16,3]{1,2,0:T(4,128)S(1)}, s32[8,16]{1,0:T(8,128)S(1)}, f32[64,1536]{1,0:T(8,128)S(1)}, /*in...) while((s32[]{:T(128)}, f32[8,16,3]{1,2,0:T(4,128)S(1)}, ...), condition=%wide.region_15.16_spmd.clone.clone, body=%wide.region_11.15_spmd.sunk.clone.clone.sunk | while | flops 58114 | bytes 536561 | solution.py:220
  69.3 15.5 %while.38 = (s32[]{:T(128)}, f32[8,16,3]{1,2,0:T(4,128)S(1)}, f32[8,16,3]{1,2,0:T(4,128)S(1)}, s32[8,16]{1,0:T(8,128)S(1)}, f32[64,1536]{1,0:T(8,128)S(1)}, /*in...) while((s32[]{:T(128)}, f32[8,16,3]{1,2,0:T(4,128)S(1)}, ...), condition=%wide.region_7.8_spmd.clone.clone, body=%wide.region_3.7_spmd.sunk.clone.clone.sunk | while | flops 58114 | bytes 536561 | solution.py:220
  85.1 3.1 collective-permute-start.3
  100.4 6.2 %scatter-add.9 = f32[3,16,16,128]{3,1,2,0:T(8,128)S(1)} dynamic-update-slice(f32[3,16,16,128]{3,1,2,0:T(8,128)S(1)} %scatter-add.6, f32[3,16,16,1]{3,1,2,0:T(8,128)S(1)} %slice_add_fusion.8, s32[]{:T(128)} %constant.188.clone.1, s32[]{:T(128)} %constant.188.clone.1, s32[]{:T(128)} %constant.188.clone.1, s32[]{:T(128)} %constant.198.clone.1) | dynamic-update-slice | bytes 6148 | tf_op jit(solution)/shard_map/scatter-add | solution.py:261
  106.6 3.6 collective-permute-start.4
  114.1 4.3 collective-permute-start.6
  118.3 12.2 %collective-permute-start.7 = (f32[3,18,1,128]{3,1,2,0:T(8,128)S(1)}, f32[3,18,1,128]{3,1,2,0:T(8,128)S(1)}, u32[]{:S(2)}, u32[]{:S(2)}) collective-permute-start(f32[3,18,1,128]{3,1,2,0:T(8,128)S(1)} %get-tuple-element.679), channel_id=1, source_target_pairs={{1,0},{2,1},{3,2},{4,3},{5,4},{6,5},{7,6},{8,7},{9,8},{10,9},{11,1... | collective-permute-start | bytes 82952 | tf_op jit(solution)/shard_map/ppermute | solution.py:54
  138.4 3.9 slice_add_fusion.7
  149.0 5.7 %copy.591 = f32[3,16,16,128]{2,3,1,0:T(8,128)} copy(f32[3,16,16,128]{1,3,2,0:T(8,128)} %fusion.52) | data formatting | bytes 786432 | tf_op jit(solution)/shard_map/reshape | solution.py:125
  154.7 7.0 %fusion.38 = f32[3,16,16,128]{3,2,1,0:T(8,128)S(1)} fusion(f32[3,16,16,128]{2,3,1,0:T(8,128)} %copy.591, f32[128,128,1,1]{1,0,2,3:T(8,128)} %reshape.854), kind=kOutput, calls=%fused_computation.161 | convolution fusion | flops 150994944 | bytes 851968 | tf_op jit(solution)/shard_map/cxzb,ab->cxza/dot_general | solution.py:181
  161.8 3.6 fusion.14
  165.4 4.1 fusion.20
  169.6 3.3 collective-permute-start.8
  178.6 5.4 %collective-permute-start.11 = (f32[3,18,1,128]{3,1,2,0:T(8,128)S(1)}, f32[3,18,1,128]{3,1,2,0:T(8,128)S(1)}, u32[]{:S(2)}, u32[]{:S(2)}) collective-permute-start(f32[3,18,1,128]{3,1,2,0:T(8,128)S(1)} %get-tuple-element.671), channel_id=1, source_target_pairs={{1,0},{2,1},{3,2},{4,3},{5,4},{6,5},{7,6},{8,7},{9,8},{10,9},{11,1... | collective-permute-start | bytes 82952 | tf_op jit(solution)/shard_map/ppermute | solution.py:54
  187.3 3.2 copy.509
  190.5 3.2 fusion.56
  196.3 5.1 %slice_add_fusion.5 = (f32[3,16,16,16,1]{1,4,3,2,0:T(1,128)S(1)}, f32[3,16,16,16,1]{1,4,3,2,0:T(1,128)S(1)}) fusion(f32[3,16,16,16,8]{1,4,3,2,0:T(8,128)} %bitcast.365, f32[3,16,16,15,1]{1,4,3,2,0:T(1,128)S(1)} %get-tuple-element.634, f32[3,16,16,15,1]{1,4,3,2,0:T(1,128)S(1)} %get-tuple-element.635), kind=kLoop, calls=%fused_computation.121 | loop fusion | flops 24576 | bytes 288768 | tf_op jit(solution)/shard_map/add | solution.py:124
  201.4 4.3 multiply_reduce_fusion.6
  205.7 11.8 %all-reduce.18 = (f32[3]{0:T(128)}, f32[3]{0:T(128)}) all-reduce(f32[3]{0:T(128)} %get-tuple-element.523, f32[3]{0:T(128)} %get-tuple-element.522), channel_id=1, replica_groups=mesh['wall_0'=4,'wall_1'=8,'wall_2'=2,'span'=12] {'wall_0'}, use_global_device_ids=true, to_apply=%region_22.23 | all-reduce | flops 6 | bytes 48 | tf_op jit(solution)/shard_map/psum | solution.py:63
  217.5 26.5 %all-reduce.15 = (f32[3]{0:T(128)}, f32[3]{0:T(128)}) all-reduce(f32[3]{0:T(128)} %get-tuple-element.576, f32[3]{0:T(128)} %get-tuple-element.577), channel_id=1, replica_groups=mesh['wall_0'=4,'wall_1'=8,'wall_2'=2,'span'=12] {'wall_1'}, use_global_device_ids=true, to_apply=%region_23.24 | all-reduce | flops 6 | bytes 48 | tf_op jit(solution)/shard_map/psum | solution.py:63
  244.0 3.1 all-reduce.21
  247.1 24.8 %all-reduce.12 = (f32[3]{0:T(128)}, f32[3]{0:T(128)}) all-reduce(f32[3]{0:T(128)} %get-tuple-element.582, f32[3]{0:T(128)} %get-tuple-element.583), channel_id=1, replica_groups=mesh['wall_0'=4,'wall_1'=8,'wall_2'=2,'span'=12] {'span'}, use_global_device_ids=true, to_apply=%region_25.26 | all-reduce | flops 6 | bytes 48 | tf_op jit(solution)/shard_map/psum | solution.py:63
  272.7 5.9 %multiply_subtract_fusion.1 = (f32[3,16,16,16,8]{1,4,3,2,0:T(8,128)}, f32[3,16,16,128]{1,3,2,0:T(8,128)}) fusion(f32[3]{0:T(128)S(1)} %div.49, f32[3,16,16,16,1]{1,4,3,2,0:T(1,128)} %copy-done.17, f32[3,16,16,16,6]{1,4,3,2,0:T(8,128)} %copy-done, f32[3,16,16,16,1]{1,4,3,2,0:T(1,128)} %copy-done.16, f32[3,16,16,16,1]{1,4,3,2,0:T(1,128)} %copy-done.8, ...), kind=kLoop, calls=%fused_computation.84 | loop fusion | flops 589824 | bytes 1572876 | tf_op jit(solution)/shard_map/sub | solution.py:272
  278.6 3.2 copy.512
  285.6 4.1 copy.595
  289.7 7.0 %fusion.36 = f32[3,16,16,128]{3,2,1,0:T(8,128)S(1)} fusion(f32[3,16,16,128]{2,3,1,0:T(8,128)} %copy.595, f32[128,128,1,1]{1,0,2,3:T(8,128)} %reshape.854), kind=kOutput, calls=%fused_computation.159 | convolution fusion | flops 150994944 | bytes 851968 | tf_op jit(solution)/shard_map/cxzb,ab->cxza/dot_general | solution.py:181
  299.0 3.6 collective-permute-start.13
  306.1 5.1 %collective-permute-start.15 = (f32[3,18,1,128]{3,1,2,0:T(8,128)S(1)}, f32[3,18,1,128]{3,1,2,0:T(8,128)S(1)}, u32[]{:S(2)}, u32[]{:S(2)}) collective-permute-start(f32[3,18,1,128]{3,1,2,0:T(8,128)S(1)} %get-tuple-element.663), channel_id=1, source_target_pairs={{1,0},{2,1},{3,2},{4,3},{5,4},{6,5},{7,6},{8,7},{9,8},{10,9},{11,1... | collective-permute-start | bytes 82952 | tf_op jit(solution)/shard_map/ppermute | solution.py:54
  323.6 8.3 %all-reduce.17 = (f32[3]{0:T(128)}, f32[3]{0:T(128)}) all-reduce(f32[3]{0:T(128)} %get-tuple-element.527, f32[3]{0:T(128)} %get-tuple-element.526), channel_id=1, replica_groups=mesh['wall_0'=4,'wall_1'=8,'wall_2'=2,'span'=12] {'wall_0'}, use_global_device_ids=true, to_apply=%region_32.33 | all-reduce | flops 6 | bytes 48 | tf_op jit(solution)/shard_map/psum | solution.py:63
  331.8 18.3 %all-reduce.14 = (f32[3]{0:T(128)}, f32[3]{0:T(128)}) all-reduce(f32[3]{0:T(128)} %get-tuple-element.574, f32[3]{0:T(128)} %get-tuple-element.575), channel_id=1, replica_groups=mesh['wall_0'=4,'wall_1'=8,'wall_2'=2,'span'=12] {'wall_1'}, use_global_device_ids=true, to_apply=%region_33.34 | all-reduce | flops 6 | bytes 48 | tf_op jit(solution)/shard_map/psum | solution.py:63
  350.1 3.2 all-reduce.20
  353.3 24.7 %all-reduce.11 = (f32[3]{0:T(128)}, f32[3]{0:T(128)}) all-reduce(f32[3]{0:T(128)} %get-tuple-element.580, f32[3]{0:T(128)} %get-tuple-element.581), channel_id=1, replica_groups=mesh['wall_0'=4,'wall_1'=8,'wall_2'=2,'span'=12] {'span'}, use_global_device_ids=true, to_apply=%region_35.36 | all-reduce | flops 6 | bytes 48 | tf_op jit(solution)/shard_map/psum | solution.py:63
  379.3 6.6 %multiply_subtract_fusion = (f32[3,16,16,16,8]{1,4,3,2,0:T(8,128)}, f32[3,16,16,128]{1,3,2,0:T(8,128)}) fusion(f32[3,16,16,16,8]{1,4,3,2,0:T(8,128)} %get-tuple-element.622, f32[3]{0:T(128)S(1)} %get-tuple-element.588, f32[3]{0:T(128)S(1)} %get-tuple-element.586, f32[3,16,16,16,1]{1,4,3,2,0:T(1,128)} %copy-done.20, f32[3,16,16,16,6]{1,4,3,2,0:T(8,128)} %copy-done.6, ...), kind=kLoop, calls=%fused_computation.81 | loop fusion | flops 786432 | bytes 1966104 | tf_op jit(solution)/shard_map/sub | solution.py:272
  386.0 3.2 copy.533
  393.9 4.0 copy.596
  398.0 7.0 %fusion.34 = f32[3,16,16,128]{3,2,1,0:T(8,128)S(1)} fusion(f32[3,16,16,128]{2,3,1,0:T(8,128)} %copy.596, f32[128,128,1,1]{1,0,2,3:T(8,128)} %reshape.854), kind=kOutput, calls=%fused_computation.157 | convolution fusion | flops 150994944 | bytes 851968 | tf_op jit(solution)/shard_map/cxzb,ab->cxza/dot_general | solution.py:181
  407.4 3.6 collective-permute-start.17
  414.5 5.1 %collective-permute-start.19 = (f32[3,18,1,128]{3,1,2,0:T(8,128)S(1)}, f32[3,18,1,128]{3,1,2,0:T(8,128)S(1)}, u32[]{:S(2)}, u32[]{:S(2)}) collective-permute-start(f32[3,18,1,128]{3,1,2,0:T(8,128)S(1)} %get-tuple-element.655), channel_id=1, source_target_pairs={{1,0},{2,1},{3,2},{4,3},{5,4},{6,5},{7,6},{8,7},{9,8},{10,9},{11,1... | collective-permute-start | bytes 82952 | tf_op jit(solution)/shard_map/ppermute | solution.py:54
  422.9 3.3 copy.549
  426.2 3.2 fusion.54
  431.7 3.9 slice_add_fusion.1
  438.8 8.5 %all-reduce.16 = (f32[3]{0:T(128)S(1)}, f32[3]{0:T(128)S(1)}) all-reduce(f32[3]{0:T(128)} %get-tuple-element.525, f32[3]{0:T(128)} %get-tuple-element.524), channel_id=1, replica_groups=mesh['wall_0'=4,'wall_1'=8,'wall_2'=2,'span'=12] {'wall_0'}, use_global_device_ids=true, to_apply=%region_42.43 | all-reduce | flops 6 | bytes 48 | tf_op jit(solution)/shard_map/psum | solution.py:63
  447.3 17.5 %all-reduce.13 = (f32[3]{0:T(128)S(1)}, f32[3]{0:T(128)S(1)}) all-reduce(f32[3]{0:T(128)S(1)} %get-tuple-element.572, f32[3]{0:T(128)S(1)} %get-tuple-element.573), channel_id=1, replica_groups=mesh['wall_0'=4,'wall_1'=8,'wall_2'=2,'span'=12] {'wall_1'}, use_global_device_ids=true, to_apply=%region_43.44 | all-reduce | flops 6 | bytes 48 | tf_op jit(solution)/shard_map/psum | solution.py:63
  467.3 24.1 %all-reduce.10 = (f32[3]{0:T(128)S(1)}, f32[3]{0:T(128)S(1)}) all-reduce(f32[3]{0:T(128)S(1)} %get-tuple-element.578, f32[3]{0:T(128)S(1)} %get-tuple-element.579), channel_id=1, replica_groups=mesh['wall_0'=4,'wall_1'=8,'wall_2'=2,'span'=12] {'span'}, use_global_device_ids=true, to_apply=%region_45.46 | all-reduce | flops 6 | bytes 48 | tf_op jit(solution)/shard_map/psum | solution.py:63
  (785 shorter events, 155.4 us)
Async XLA Ops:
  7.2 45.8 %collective-permute-start.2 = (f32[4,128]{0,1:T(8,128)S(1)}, f32[4,128]{0,1:T(8,128)S(1)}, u32[]{:S(2)}, u32[]{:S(2)}) collective-permute-start(f32[4,128]{0,1:T(8,128)S(1)} %slice.614), channel_id=1, source_target_pairs={{0,756},{12,0},{24,12},{36,24},{48,36},{60,48},{72,60},{84,72},{96... | collective-permute-start | bytes 6152 | tf_op jit(solution)/shard_map/ppermute | solution.py:70
  11.4 41.9 %collective-permute-start = (f32[4,128]{0,1:T(8,128)S(1)}, f32[4,128]{0,1:T(8,128)S(1)}, u32[]{:S(2)}, u32[]{:S(2)}) collective-permute-start(f32[4,128]{0,1:T(8,128)S(1)} %slice.611), channel_id=1, source_target_pairs={{0,12},{12,24},{24,36},{36,48},{48,60},{60,72},{72,84},{84,96},{96... | collective-permute-start | bytes 6152 | tf_op jit(solution)/shard_map/ppermute | solution.py:70
  34.1 18.7 %copy-start.51 = (f32[8,8]{1,0:T(8,128)S(1)}, f32[8,8]{1,0:T(8,128)}, u32[]{:S(2)}) copy-start(f32[8,8]{1,0:T(8,128)} %constant.202.clone) | copy-start | bytes 772
  69.3 26.2 %copy-start.52 = (f32[512]{0:T(512)S(1)}, f32[512]{0:T(512)}, u32[]{:S(2)}) copy-start(f32[512]{0:T(512)} %param.55) | copy-start | bytes 6148
  85.1 8.6 %collective-permute-start.3 = (f32[3,128]{0,1:T(8,128)S(1)}, f32[3,128]{0,1:T(8,128)S(1)}, u32[]{:S(2)}, u32[]{:S(2)}) collective-permute-start(f32[3,128]{0,1:T(8,128)S(1)} %bitcast.404), channel_id=1, source_target_pairs={{0,12},{12,24},{24,36},{36,48},{48,60},{60,72},{72,84},{84,96},{96... | collective-permute-start | bytes 4616 | tf_op jit(solution)/shard_map/ppermute | solution.py:70
  88.2 4.4 collective-permute-start.1
  106.6 5.9 %collective-permute-start.4 = (f32[3,1,16,128]{3,1,2,0:T(1,128)S(1)}, f32[3,1,16,128]{3,1,2,0:T(1,128)S(1)}, u32[]{:S(2)}, u32[]{:S(2)}) collective-permute-start(f32[3,1,16,128]{3,1,2,0:T(1,128)S(1)} %get-tuple-element.702), channel_id=1, source_target_pairs={{0,12},{12,24},{24,36},{36,48},{48,60},{60,72},{72,84},{84,96},{96... | collective-permute-start | bytes 73736 | tf_op jit(solution)/shard_map/ppermute | solution.py:52
  110.3 3.8 collective-permute-start.5
  114.1 17.8 %collective-permute-start.6 = (f32[3,18,1,128]{3,1,2,0:T(8,128)S(1)}, f32[3,18,1,128]{3,1,2,0:T(8,128)S(1)}, u32[]{:S(2)}, u32[]{:S(2)}) collective-permute-start(f32[3,18,1,128]{3,1,2,0:T(8,128)S(1)} %get-tuple-element.678), channel_id=1, source_target_pairs={{0,1},{1,2},{2,3},{3,4},{4,5},{5,6},{6,7},{7,8},{8,9},{9,10},{10,1... | collective-permute-start | bytes 82952 | tf_op jit(solution)/shard_map/ppermute | solution.py:52
  118.3 13.8 %collective-permute-start.7 = (f32[3,18,1,128]{3,1,2,0:T(8,128)S(1)}, f32[3,18,1,128]{3,1,2,0:T(8,128)S(1)}, u32[]{:S(2)}, u32[]{:S(2)}) collective-permute-start(f32[3,18,1,128]{3,1,2,0:T(8,128)S(1)} %get-tuple-element.679), channel_id=1, source_target_pairs={{1,0},{2,1},{3,2},{4,3},{5,4},{6,5},{7,6},{8,7},{9,8},{10,9},{11,1... | collective-permute-start | bytes 82952 | tf_op jit(solution)/shard_map/ppermute | solution.py:54
  154.7 7.1 %copy-start.4 = (f32[3,16,16,128]{2,3,1,0:T(8,128)S(1)}, f32[3,16,16,128]{2,3,1,0:T(8,128)}, u32[]{:S(2)}) copy-start(f32[3,16,16,128]{2,3,1,0:T(8,128)} %copy.591) | copy-start | bytes 1179652
  154.7 10.7 %copy-start.9 = (f32[3,16,16,16,1]{1,4,3,2,0:T(1,128)S(1)}, f32[3,16,16,16,1]{1,4,3,2,0:T(1,128)}, u32[]{:S(2)}) copy-start(f32[3,16,16,16,1]{1,4,3,2,0:T(1,128)} %copy-done.8) | copy-start | bytes 147460
  154.7 10.7 %copy-start.18 = (f32[3,16,16,128]{3,1,2,0:T(8,128)S(1)}, f32[3,16,16,128]{3,1,2,0:T(8,128)}, u32[]{:S(2)}) copy-start(f32[3,16,16,128]{3,1,2,0:T(8,128)} %copy.492) | copy-start | bytes 1179652
  154.7 10.7 %copy-start.22 = (f32[16,16,128]{2,0,1:T(8,128)S(1)}, f32[16,16,128]{2,0,1:T(8,128)}, u32[]{:S(2)}) copy-start(f32[16,16,128]{2,0,1:T(8,128)} %copy-done.21) | copy-start | bytes 393220
  154.7 10.7 %copy-start.32 = (f32[16,16,1,1]{1,0,3,2:T(8,128)S(1)}, f32[16,16,1,1]{1,0,3,2:T(8,128)}, u32[]{:S(2)}) copy-start(f32[16,16,1,1]{1,0,3,2:T(8,128)} %constant.260) | copy-start | bytes 3076
  154.7 10.7 %copy-start.34 = (f32[128]{0:T(128)S(1)}, f32[128]{0:T(128)}, u32[]{:S(2)}) copy-start(f32[128]{0:T(128)} %copy-done.33) | copy-start | bytes 1540
  154.7 10.7 %copy-start.40 = (f32[16]{0:T(128)S(1)}, f32[16]{0:T(128)}, u32[]{:S(2)}) copy-start(f32[16]{0:T(128)} %constant.204.clone) | copy-start | bytes 196
  169.6 5.6 %collective-permute-start.8 = (f32[3,1,16,128]{3,1,2,0:T(1,128)S(1)}, f32[3,1,16,128]{3,1,2,0:T(1,128)S(1)}, u32[]{:S(2)}, u32[]{:S(2)}) collective-permute-start(f32[3,1,16,128]{3,1,2,0:T(1,128)S(1)} %get-tuple-element.696), channel_id=1, source_target_pairs={{0,12},{12,24},{24,36},{36,48},{48,60},{60,72},{72,84},{84,96},{96... | collective-permute-start | bytes 73736 | tf_op jit(solution)/shard_map/ppermute | solution.py:52
  172.8 3.8 collective-permute-start.9
  176.7 7.4 %collective-permute-start.10 = (f32[3,18,1,128]{3,1,2,0:T(8,128)S(1)}, f32[3,18,1,128]{3,1,2,0:T(8,128)S(1)}, u32[]{:S(2)}, u32[]{:S(2)}) collective-permute-start(f32[3,18,1,128]{3,1,2,0:T(8,128)S(1)} %get-tuple-element.670), channel_id=1, source_target_pairs={{0,1},{1,2},{2,3},{3,4},{4,5},{5,6},{6,7},{7,8},{8,9},{9,10},{10,1... | collective-permute-start | bytes 82952 | tf_op jit(solution)/shard_map/ppermute | solution.py:52
  178.6 7.1 %collective-permute-start.11 = (f32[3,18,1,128]{3,1,2,0:T(8,128)S(1)}, f32[3,18,1,128]{3,1,2,0:T(8,128)S(1)}, u32[]{:S(2)}, u32[]{:S(2)}) collective-permute-start(f32[3,18,1,128]{3,1,2,0:T(8,128)S(1)} %get-tuple-element.671), channel_id=1, source_target_pairs={{1,0},{2,1},{3,2},{4,3},{5,4},{6,5},{7,6},{8,7},{9,8},{10,9},{11,1... | collective-permute-start | bytes 82952 | tf_op jit(solution)/shard_map/ppermute | solution.py:54
  193.7 7.7 %copy-start.10 = (f32[3,16,16,16,1]{1,4,3,2,0:T(1,128)S(1)}, f32[3,16,16,16,1]{1,4,3,2,0:T(1,128)}, u32[]{:S(2)}) copy-start(f32[3,16,16,16,1]{1,4,3,2,0:T(1,128)} %copy-done.8) | copy-start | bytes 147460
  193.8 7.7 %copy-start.13 = (f32[16,16,16,8]{0,3,2,1:T(8,128)S(1)}, f32[16,16,16,8]{0,3,2,1:T(8,128)}, u32[]{:S(2)}) copy-start(f32[16,16,16,8]{0,3,2,1:T(8,128)} %constant.235) | copy-start | bytes 393220
  196.3 9.4 %copy-start = (f32[3,16,16,16,6]{1,4,3,2,0:T(8,128)}, f32[3,16,16,16,6]{1,4,3,2,0:T(8,128)S(1)}, u32[]{:S(2)}) copy-start(f32[3,16,16,16,6]{1,4,3,2,0:T(8,128)S(1)} %slice.663) | copy-start | bytes 884740
  278.6 7.0 %copy-start.2 = (f32[3,16,16,16,8]{1,4,3,2,0:T(8,128)S(1)}, f32[3,16,16,16,8]{1,4,3,2,0:T(8,128)}, u32[]{:S(2)}) copy-start(f32[3,16,16,16,8]{1,4,3,2,0:T(8,128)} %get-tuple-element.622) | copy-start | bytes 1179652
  289.7 7.0 %copy-start.28 = (f32[3,16,16,128]{3,2,1,0:T(8,128)S(1)}, f32[3,16,16,128]{3,2,1,0:T(8,128)}, u32[]{:S(2)}) copy-start(f32[3,16,16,128]{3,2,1,0:T(8,128)} %fusion.12) | copy-start | bytes 1179652
  297.1 5.6 %collective-permute-start.12 = (f32[3,1,16,128]{3,1,2,0:T(1,128)S(1)}, f32[3,1,16,128]{3,1,2,0:T(1,128)S(1)}, u32[]{:S(2)}, u32[]{:S(2)}) collective-permute-start(f32[3,1,16,128]{3,1,2,0:T(1,128)S(1)} %get-tuple-element.690), channel_id=1, source_target_pairs={{0,12},{12,24},{24,36},{36,48},{48,60},{60,72},{72,84},{84,96},{96... | collective-permute-start | bytes 73736 | tf_op jit(solution)/shard_map/ppermute | solution.py:52
  299.0 5.1 %collective-permute-start.13 = (f32[3,1,16,128]{3,1,2,0:T(1,128)S(1)}, f32[3,1,16,128]{3,1,2,0:T(1,128)S(1)}, u32[]{:S(2)}, u32[]{:S(2)}) collective-permute-start(f32[3,1,16,128]{3,1,2,0:T(1,128)S(1)} %get-tuple-element.691), channel_id=1, source_target_pairs={{12,0},{24,12},{36,24},{48,36},{60,48},{72,60},{84,72},{96,84},{10... | collective-permute-start | bytes 73736 | tf_op jit(solution)/shard_map/ppermute | solution.py:54
  304.1 7.1 %collective-permute-start.14 = (f32[3,18,1,128]{3,1,2,0:T(8,128)S(1)}, f32[3,18,1,128]{3,1,2,0:T(8,128)S(1)}, u32[]{:S(2)}, u32[]{:S(2)}) collective-permute-start(f32[3,18,1,128]{3,1,2,0:T(8,128)S(1)} %get-tuple-element.662), channel_id=1, source_target_pairs={{0,1},{1,2},{2,3},{3,4},{4,5},{5,6},{6,7},{7,8},{8,9},{9,10},{10,1... | collective-permute-start | bytes 82952 | tf_op jit(solution)/shard_map/ppermute | solution.py:52
  306.1 6.8 %collective-permute-start.15 = (f32[3,18,1,128]{3,1,2,0:T(8,128)S(1)}, f32[3,18,1,128]{3,1,2,0:T(8,128)S(1)}, u32[]{:S(2)}, u32[]{:S(2)}) collective-permute-start(f32[3,18,1,128]{3,1,2,0:T(8,128)S(1)} %get-tuple-element.663), channel_id=1, source_target_pairs={{1,0},{2,1},{3,2},{4,3},{5,4},{6,5},{7,6},{8,7},{9,8},{10,9},{11,1... | collective-permute-start | bytes 82952 | tf_op jit(solution)/shard_map/ppermute | solution.py:54
  320.6 58.8 %copy-start.1 = (f32[3,16,16,16,6]{1,4,3,2,0:T(8,128)S(1)}, f32[3,16,16,16,6]{1,4,3,2,0:T(8,128)}, u32[]{:S(2)}) copy-start(f32[3,16,16,16,6]{1,4,3,2,0:T(8,128)} %copy-done) | copy-start | bytes 884740
  386.0 8.0 %copy-start.5 = (f32[3,16,16,16,8]{1,4,3,2,0:T(8,128)S(1)}, f32[3,16,16,16,8]{1,4,3,2,0:T(8,128)}, u32[]{:S(2)}) copy-start(f32[3,16,16,16,8]{1,4,3,2,0:T(8,128)} %get-tuple-element.620) | copy-start | bytes 1179652
  398.0 7.0 %copy-start.12 = (f32[3,16,16,128]{3,1,2,0:T(8,128)S(1)}, f32[3,16,16,128]{3,1,2,0:T(8,128)}, u32[]{:S(2)}) copy-start(f32[3,16,16,128]{3,1,2,0:T(8,128)} %copy-done.11) | copy-start | bytes 1179652
  398.0 7.1 %copy-start.24 = (f32[16,16,128]{2,0,1:T(8,128)S(1)}, f32[16,16,128]{2,0,1:T(8,128)}, u32[]{:S(2)}) copy-start(f32[16,16,128]{2,0,1:T(8,128)} %copy-done.21) | copy-start | bytes 393220
  398.0 7.1 %copy-start.26 = (f32[3,16,128,16]{2,3,1,0:T(8,128)S(1)}, f32[3,16,128,16]{2,3,1,0:T(8,128)}, u32[]{:S(2)}) copy-start(f32[3,16,128,16]{2,3,1,0:T(8,128)} %convolution_multiply_fusion) | copy-start | bytes 1179652
  398.0 7.1 %copy-start.27 = (f32[3,16,16,128]{3,2,1,0:T(8,128)S(1)}, f32[3,16,16,128]{3,2,1,0:T(8,128)}, u32[]{:S(2)}) copy-start(f32[3,16,16,128]{3,2,1,0:T(8,128)} %fusion.27) | copy-start | bytes 1179652
  398.0 7.1 %copy-start.36 = (f32[128]{0:T(128)S(1)}, f32[128]{0:T(128)}, u32[]{:S(2)}) copy-start(f32[128]{0:T(128)} %copy-done.33) | copy-start | bytes 1540
  398.0 21.7 %copy-start.38 = (f32[512]{0:T(512)S(1)}, f32[512]{0:T(512)}, u32[]{:S(2)}) copy-start(f32[512]{0:T(512)} %copy-done.37) | copy-start | bytes 6148
  398.0 21.7 %copy-start.46 = (f32[1,512]{1,0:T(1,128)S(1)}, f32[1,512]{1,0:T(1,128)}, u32[]{:S(2)}) copy-start(f32[1,512]{1,0:T(1,128)} %get-tuple-element.708) | copy-start | bytes 6148
  398.0 21.7 %copy-start.47 = (f32[1,512]{1,0:T(1,128)S(1)}, f32[1,512]{1,0:T(1,128)}, u32[]{:S(2)}) copy-start(f32[1,512]{1,0:T(1,128)} %get-tuple-element.712) | copy-start | bytes 6148
  405.5 5.6 %collective-permute-start.16 = (f32[3,1,16,128]{3,1,2,0:T(1,128)S(1)}, f32[3,1,16,128]{3,1,2,0:T(1,128)S(1)}, u32[]{:S(2)}, u32[]{:S(2)}) collective-permute-start(f32[3,1,16,128]{3,1,2,0:T(1,128)S(1)} %get-tuple-element.684), channel_id=1, source_target_pairs={{0,12},{12,24},{24,36},{36,48},{48,60},{60,72},{72,84},{84,96},{96... | collective-permute-start | bytes 73736 | tf_op jit(solution)/shard_map/ppermute | solution.py:52
  407.4 5.1 %collective-permute-start.17 = (f32[3,1,16,128]{3,1,2,0:T(1,128)S(1)}, f32[3,1,16,128]{3,1,2,0:T(1,128)S(1)}, u32[]{:S(2)}, u32[]{:S(2)}) collective-permute-start(f32[3,1,16,128]{3,1,2,0:T(1,128)S(1)} %get-tuple-element.685), channel_id=1, source_target_pairs={{12,0},{24,12},{36,24},{48,36},{60,48},{72,60},{84,72},{96,84},{10... | collective-permute-start | bytes 73736 | tf_op jit(solution)/shard_map/ppermute | solution.py:54
  412.6 7.7 %collective-permute-start.18 = (f32[3,18,1,128]{3,1,2,0:T(8,128)S(1)}, f32[3,18,1,128]{3,1,2,0:T(8,128)S(1)}, u32[]{:S(2)}, u32[]{:S(2)}) collective-permute-start(f32[3,18,1,128]{3,1,2,0:T(8,128)S(1)} %get-tuple-element.654), channel_id=1, source_target_pairs={{0,1},{1,2},{2,3},{3,4},{4,5},{5,6},{6,7},{7,8},{8,9},{9,10},{10,1... | collective-permute-start | bytes 82952 | tf_op jit(solution)/shard_map/ppermute | solution.py:52
  414.5 6.8 %collective-permute-start.19 = (f32[3,18,1,128]{3,1,2,0:T(8,128)S(1)}, f32[3,18,1,128]{3,1,2,0:T(8,128)S(1)}, u32[]{:S(2)}, u32[]{:S(2)}) collective-permute-start(f32[3,18,1,128]{3,1,2,0:T(8,128)S(1)} %get-tuple-element.655), channel_id=1, source_target_pairs={{1,0},{2,1},{3,2},{4,3},{5,4},{6,5},{7,6},{8,7},{9,8},{10,9},{11,1... | collective-permute-start | bytes 82952 | tf_op jit(solution)/shard_map/ppermute | solution.py:54
  435.7 55.7 %copy-start.53 = (f32[3]{0:T(128)S(1)}, f32[3]{0:T(128)}, u32[]{:S(2)}) copy-start(f32[3]{0:T(128)} %get-tuple-element.562) | copy-start | bytes 40
  435.7 56.3 %copy-start.43 = (f32[3]{0:T(128)S(1)}, f32[3]{0:T(128)}, u32[]{:S(2)}) copy-start(f32[3]{0:T(128)} %copy-done.42) | copy-start | bytes 40
  435.7 56.3 %copy-start.45 = (f32[3]{0:T(128)S(1)}, f32[3]{0:T(128)}, u32[]{:S(2)}) copy-start(f32[3]{0:T(128)} %copy-done.44) | copy-start | bytes 40
  435.7 56.3 %copy-start.50 = (f32[3]{0:T(128)S(1)}, f32[3]{0:T(128)}, u32[]{:S(2)}) copy-start(f32[3]{0:T(128)} %copy-done.49) | copy-start | bytes 40
  (26 other events, 116.1 us)
where the time goes:
time: 503 us; the launch traced here: 495 us
  blocking collectives  173 us (34%)
  local copies, waits for them, and re-layouts  127 us (25%)
  other arithmetic  73.2 us (15%)
  starting transfers between devices  70.7 us (14%)
  matrix products  33.8 us (7%)
  waiting for transfers between devices  12 us (2%)
    psum x12, blocking collectives, one_axis_at_a_time(): x = lax.psum(x, axis)  173 us
    ppermute x8, starting transfers between devices, with_halo(): lax.ppermute(head, axis, [((i + 1) % count, i) for i in range(count)])  39.8 us
    dot_general x3, matrix products, operate(): along_y = jnp.einsum('cxzb,ab->cxza', field, stiff_y, precision=precise)  21 us
    ppermute x8, starting transfers between devices, with_halo(): lax.ppermute(tail, axis, [(i, (i + 1) % count) for i in range(count)])  20.8 us
    gather x24, local copies, waits for them, and re-layouts, evaluate(): values = element_rows[row_ids].reshape(row_ids.shape[0], 3, 8, 8, 8)  15.4 us
    reshape x4, local copies, waits for them, and re-layouts, join_faces(): return joined.reshape(core.shape)  15 us
    sub x4, other arithmetic, body(): residual = residual - spread(step_size) * along_dir  15 us
    add x12, other arithmetic, join_faces(): first + prev_last  14.2 us
  transfers between devices with their start and end apart: 20, of which 9 were waited for; matrix products, arithmetic and copies ran while one was open for 9% of the time, Pallas kernels for 0%

commit v1 on v0

v1 whole, which is shorter than its diff:
```python
import functools

import jax
import jax.numpy as jnp
import numpy as np
from jax import lax
from jax.experimental import pallas as pl
from jax.experimental.pallas import tpu as pltpu
from jax.sharding import Mesh
from jax.sharding import PartitionSpec as P

AXES = ("wall_0", "wall_1", "wall_2", "span")
WALL_SPAN = AXES
WALL = ("wall_0", "wall_1", "wall_2")
MESH_ID = pl.DeviceIdType.MESH

GLL_NODES = (
    -1.0,
    -0.8717401485096066,
    -0.5917001814331423,
    -0.2092992179024789,
    0.2092992179024789,
    0.5917001814331423,
    0.8717401485096066,
    1.0,
)
GLL_WEIGHTS = (
    0.03571428571428571,
    0.2107042271435061,
    0.3411226924835044,
    0.4124587946587038,
    0.4124587946587038,
    0.3411226924835044,
    0.2107042271435061,
    0.03571428571428571,
)
viscosity = 0.02
inverse_step = 20.0
karman = 0.41
sample_height = 0.1
speed_floor = 0.01
element_dx = 0.05
element_dz = 0.13
precise = lax.Precision.HIGHEST

SCALE = 64.0

SHIFTS = ((1, 0), (-1, 0), (0, 1), (0, -1), (1, 1), (1, -1), (-1, 1), (-1, -1))

MZ, QMZ, COUNT, LAG, PLANE, HALFW, LAST, FIRST, KZ = range(9)


def stiffness_table():
    points = np.array(GLL_NODES)
    weights = np.array(GLL_WEIGHTS)
    previous = np.ones(8)
    current = points.copy()
    for degree in range(1, 7):
        previous, current = (
            current,
            ((2 * degree + 1) * points * current - degree * previous) / (degree + 1),
        )
    derivative = np.zeros((8, 8))
    for target in range(8):
        for source in range(8):
            if target != source:
                derivative[target, source] = (
                    current[target] / current[source] / (points[target] - points[source])
                )
    derivative[0, 0] = -14.0
    derivative[7, 7] = 14.0
    return derivative.T @ (weights[:, None] * derivative)


def tables():
    weights = np.array(GLL_WEIGHTS)
    points = np.array(GLL_NODES)
    stiffness = stiffness_table()
    ones = np.ones((8, 128))
    lane = np.arange(128)
    ends = np.array([2.0, 1, 1, 1, 1, 1, 1, 2.0])
    mass_x = 0.5 * element_dx * weights
    mass_z = 0.5 * element_dz * weights
    count_y = np.where((lane % 8 == 0) | (lane % 8 == 7), 0.5, 1.0)
    count_y[0] = count_y[127] = 1.0
    gaps = points[:, None] - points[None, :] + np.eye(8)
    kz = SCALE * (
        viscosity * (2.0 / element_dz) * stiffness + inverse_step * np.diag(mass_z)
    )
    rows = [
        mass_z[:, None] * ones,
        (mass_z * ends)[:, None] * ones,
        (1.0 / ends)[:, None] * count_y[None, :],
        (1.0 / np.prod(gaps, axis=1))[:, None] * ones,
        ones * (mass_x[lane // 16] * mass_z[lane % 8])[None, :],
        ones * (0.5 * weights[lane % 8])[None, :],
        ones * ((lane % 8 == 7) & (lane < 127))[None, :],
        ones * ((lane % 8 == 0) & (lane > 0))[None, :],
    ]
    rows += [kz[:, b][:, None] * ones for b in range(8)]
    block = np.kron(np.eye(16), SCALE * viscosity * 2.0 * stiffness)
    lift = np.zeros((8, 512))
    for comp in range(2):
        for half in range(2):
            column = (comp * 2 + half) * 128
            lift[comp * 4 + half, column] = 1.0
            lift[comp * 4 + 2 + half, column + 127] = 1.0
    as32 = lambda value: np.asarray(value, np.float32)
    return as32(np.stack(rows)), as32(block), as32(lift)


def kernel(sizes, velocity, heights, owner, element, coords, roughness, table, block, lift,
           out, neumann, res, one, two, stiff, slab, slab_in, plane, plane_in, face, face_in,
           edge, edge_in, mom, part, part_in, send, recv, slab_send, slab_recv, sum_send,
           sum_recv):
    nx, ny, nc, ns = sizes
    nw = nx * ny * nc
    wx, wy, wc, sp = (lax.axis_index(name) for name in AXES)
    wall = (wx * ny + wy) * nc + wc
    weights = np.array(GLL_WEIGHTS)
    stiffness = stiffness_table()
    mass_x = [float(v) for v in 0.5 * element_dx * weights]
    ends = [2.0, 1.0, 1.0, 1.0, 1.0, 1.0, 1.0, 2.0]

    def shifted(dw, ds):
        there = (wall + dw + nw) % nw
        return (there // (ny * nc), there // nc % ny, there % nc, (sp + ds + ns) % ns)

    neighbours = [shifted(dw, ds) for dw, ds in SHIFTS]
    pair = wx * nc + wc
    groups = [
        (nx * nc, pair, lambda q: (q // nc, wy, q % nc, sp)),
        (ny, wy, lambda q: (wx, q, wc, sp)),
        (ns, sp, lambda q: (wx, wy, wc, q)),
    ]
    peers = list(neighbours)
    for count, mine, place in groups:
        peers += [place((mine + k) % count) for k in range(1, count)]
    barrier = pltpu.get_barrier_semaphore()
    for peer in peers:
        pl.semaphore_signal(barrier, inc=1, device_id=peer, device_id_type=MESH_ID)

    lane = lax.broadcasted_iota(jnp.int32, (1, 128), 1)
    sub8 = lax.broadcasted_iota(jnp.int32, (8, 128), 0)
    lane8 = lax.broadcasted_iota(jnp.int32, (8, 128), 1)

    height = jnp.zeros((8, 128), jnp.float32)
    for layer in range(16):
        height = jnp.where(lane8 // 8 == layer, heights[layer], height)
    mass_y = height * table[HALFW]
    stiff[...] = block[...] * (1.0 / height)[:1]
    joined_y = (
        mass_y
        + table[LAST] * pltpu.roll(mass_y, 127, 1)
        + table[FIRST] * pltpu.roll(mass_y, 1, 1)
    )
    both = lambda value: jnp.concatenate([value, value], axis=0)
    mass_zy = both(table[MZ] * mass_y)
    mass_y2 = both(mass_y)
    mass_z2 = both(table[MZ])
    last2, first2 = both(table[LAST]), both(table[FIRST])
    count2 = both(table[COUNT])

    for comp in range(2):
        quarters = []
        for k in range(4):
            quarters.append(velocity[2 * comp, 4 * k : 4 * k + 4].reshape(64, 128))
        packed = jnp.zeros((64, 128), jnp.float32)
        where_to = lax.broadcasted_iota(jnp.int32, (64, 128), 1)
        for k in range(4):
            low = pltpu.roll(quarters[k], 32 * k, 1) if k else quarters[k]
            shift = (32 * k + 32) % 128
            high = pltpu.roll(quarters[k], shift, 1) if shift else quarters[k]
            packed = jnp.where(where_to // 16 == 2 * k, low, packed)
            packed = jnp.where(where_to // 16 == 2 * k + 1, high, packed)
        slab[comp] = packed.reshape(4, 16, 128)

    scale_zy = both(table[QMZ] * joined_y) * inverse_step
    for comp in range(3):
        for i in range(16):
            res[comp, 16 * i : 16 * i + 16] = velocity[comp, i] * (
                scale_zy * (mass_x[i % 8] * ends[i % 8])
            )

    def regroup(blocks):
        upper = (lane // 8) % 2 == 1
        result = []
        for ex in range(2):
            low, high = blocks[ex], blocks[2 + ex]
            result.append(jnp.where(upper, pltpu.roll(high, 8, 1), low))
            result.append(jnp.where(upper, high, pltpu.roll(low, 120, 1)))
        return result

    def ungroup(values):
        upper = (lane // 8) % 2 == 1
        low, high = [], []
        for ex in range(2):
            a, b = values[2 * ex], values[2 * ex + 1]
            low.append(jnp.where(upper, pltpu.roll(b, 8, 1), a))
            high.append(jnp.where(upper, b, pltpu.roll(a, 120, 1)))
        return low + high

    wide = lambda row: jnp.broadcast_to(row, (8, 128))
    quarter = lambda ref, row, q: ref[row : row + 1, 128 * q : 128 * q + 128]
    distance = [(quarter(owner, 0, q) - wall + nw) % nw for q in range(4)]
    to_next = regroup([wide(jnp.where(d == 1, 1.0, 0.0)) for d in distance])
    to_prev = regroup([wide(jnp.where(d == nw - 1, 1.0, 0.0)) for d in distance])
    layer = regroup([wide((quarter(element, 0, q) % 2).astype(jnp.float32)) for q in range(4)])
    axes = [regroup([wide(quarter(coords, k, q)) for q in range(4)]) for k in range(3)]

    def lagrange(coord):
        value = table[LAG]
        for b in range(8):
            value = value * jnp.where(sub8 == b, 1.0, coord - GLL_NODES[b])
        return value

    pl.semaphore_wait(barrier, len(peers))

    copies = []
    slab_copies = []
    for d in range(2):
        copy = pltpu.make_async_remote_copy(
            src_ref=slab,
            dst_ref=slab_in.at[d],
            send_sem=slab_send.at[d],
            recv_sem=slab_recv.at[d],
            device_id=neighbours[d],
            device_id_type=MESH_ID,
        )
        copy.start()
        slab_copies.append(copy)
        copies.append(copy)

    basis = [[lagrange(axes[k][g]) for k in range(3)] for g in range(4)]
    second_wall = (lane // 8) % 2 == 1
    columns = []
    for g in range(4):
        ly = basis[g][2]
        blocks = []
        for side in range(2):
            for ey in range(2):
                chosen = jnp.logical_and(
                    wide(second_wall) == (side == 1), layer[g] == float(ey)
                )
                blocks.append(jnp.where(chosen, ly, 0.0))
        columns.append(jnp.concatenate(blocks, axis=0))

    nothing = jnp.zeros((32, 128), jnp.float32)
    masks = [[1.0 - to_next[g] - to_prev[g], to_prev[g], to_next[g]] for g in range(4)]

    def sample(source, g):
        ex, ez = g // 2, g % 2
        right = [
            jnp.concatenate(
                [columns[g] if k == 2 * ex + kk else nothing for k in range(4)], axis=0
            )
            for kk in range(2)
        ]
        rows = source[:, :, 8 * ez : 8 * ez + 8, :].reshape(64, 128)
        total = [jnp.zeros((8, 128), jnp.float32) for _ in range(2)]
        for kk in range(2):
            values = jnp.dot(
                rows, right[kk], precision=precise, preferred_element_type=jnp.float32
            ).reshape(2, 4, 8, 128)
            for comp in range(2):
                for x in range(4):
                    a = 4 * kk + x
                    total[comp] = total[comp] + values[comp, x] * basis[g][0][a : a + 1]
        return total

    sums = []
    for g in range(4):
        own = sample(slab, g)
        sums.append([own[comp] * masks[g][0] for comp in range(2)])
    for d in range(2):
        slab_copies[d].wait_recv()
        for g in range(4):
            far = sample(slab_in.at[d], g)
            for comp in range(2):
                sums[g][comp] = sums[g][comp] + far[comp] * masks[g][1 + d]
    stream = ungroup(
        [wide(jnp.sum(sums[g][0] * basis[g][1], axis=0, keepdims=True)) for g in range(4)]
    )
    spanwise = ungroup(
        [wide(jnp.sum(sums[g][1] * basis[g][1], axis=0, keepdims=True)) for g in range(4)]
    )

    for q in range(4):
        u, v = stream[q], spanwise[q]
        speed = jnp.sqrt(u * u + v * v + speed_floor)
        ratio = karman / jnp.log(sample_height / wide(quarter(roughness, 0, q)))
        factor = -(ratio * ratio * speed / viscosity)
        for comp, value in enumerate((u, v)):
            slope = factor * value
            neumann[comp : comp + 1, 128 * q : 128 * q + 128] = slope[:1]
            plane[comp * 4 + q : comp * 4 + q + 1, :] = (viscosity * slope * table[PLANE])[:1]

    plane_copies = []
    for d in range(8):
        copy = pltpu.make_async_remote_copy(
            src_ref=plane,
            dst_ref=plane_in.at[d],
            send_sem=send.at[0, d],
            recv_sem=recv.at[0, d],
            device_id=neighbours[d],
            device_id_type=MESH_ID,
        )
        copy.start()
        plane_copies.append(copy)
        copies.append(copy)

    node_z = lane8 % 16
    node_x = lane8 // 16
    half = sub8 % 2

    def join_span(mine, before, after):
        return (
            mine
            + jnp.where(node_z == 7, pltpu.roll(mine, 127, 1), 0.0)
            + jnp.where(node_z == 8, pltpu.roll(mine, 1, 1), 0.0)
            + jnp.where(node_z == 0, pltpu.roll(before, 113, 1), 0.0)
            + jnp.where(node_z == 15, pltpu.roll(after, 15, 1), 0.0)
        )

    def join_wall(mine, before, after):
        later = jnp.where(half == 0, pltpu.roll(mine, 7, 0), pltpu.roll(after, 1, 0))
        earlier = jnp.where(half == 0, pltpu.roll(before, 7, 0), pltpu.roll(mine, 1, 0))
        return (
            mine
            + jnp.where(node_x == 7, pltpu.roll(later, 112, 1), 0.0)
            + jnp.where(node_x == 0, pltpu.roll(earlier, 16, 1), 0.0)
        )

    for d in range(8):
        plane_copies[d].wait_recv()
    own_line = join_span(plane[...], plane_in[2], plane_in[3])
    before_line = join_span(plane_in[0], plane_in[4], plane_in[5])
    after_line = join_span(plane_in[1], plane_in[6], plane_in[7])
    stress = join_wall(own_line, before_line, after_line)
    lifted = lax.dot_general(
        stress,
        lift[...],
        (((0,), (0,)), ((), ())),
        precision=precise,
        preferred_element_type=jnp.float32,
    )
    for comp in range(2):
        for ex in range(2):
            column = (comp * 2 + ex) * 128
            here = res[2 * comp, 128 * ex : 128 * ex + 128]
            res[2 * comp, 128 * ex : 128 * ex + 128] = here + lifted[:, column : column + 128]

    cx = SCALE * viscosity * (2.0 / element_dx) * stiffness
    even = 0.5 * (cx[:4, :4] + cx[:4, 7:3:-1])
    odd = 0.5 * (cx[:4, :4] - cx[:4, 7:3:-1])

    def fold(value):
        return value[:8] + value[8:]

    def operate(source, target, index):
        for comp in range(3):
            total = jnp.zeros((16, 128), jnp.float32)
            for ex in range(2):
                base = 128 * ex
                along_y = jnp.dot(
                    source[comp, base : base + 128],
                    stiff[...],
                    precision=precise,
                    preferred_element_type=jnp.float32,
                )
                nodes = [source[comp, base + 16 * b : base + 16 * b + 16] for b in range(8)]
                plus = [nodes[b] + nodes[7 - b] for b in range(4)]
                minus = [nodes[b] - nodes[7 - b] for b in range(4)]
                along_x = [None] * 8
                for a in range(4):
                    sum_e = plus[0] * float(even[a, 0])
                    sum_o = minus[0] * float(odd[a, 0])
                    for b in range(1, 4):
                        sum_e = sum_e + plus[b] * float(even[a, b])
                        sum_o = sum_o + minus[b] * float(odd[a, b])
                    along_x[a] = sum_e + sum_o
                    along_x[7 - a] = sum_e - sum_o
                for a in range(8):
                    start = base + 16 * a
                    halves = []
                    for h in range(2):
                        along_z = None
                        for b in range(8):
                            row = start + 8 * h + b
                            term = source[comp, row : row + 1] * table[KZ + b]
                            along_z = term if along_z is None else along_z + term
                        halves.append(along_z)
                    along_z = jnp.concatenate(halves, axis=0)
                    local = along_x[a] * mass_zy + (
                        along_z * mass_y2 + along_y[16 * a : 16 * a + 16] * mass_z2
                    ) * mass_x[a]
                    total = total + local * nodes[a]
                    if target is not None:
                        target[comp, start : start + 16] = (
                            local
                            + last2 * pltpu.roll(local, 127, 1)
                            + first2 * pltpu.roll(local, 1, 1)
                        )
            mom[3 * index + comp] = fold(total)

    def exchange(target, turn):
        for comp in range(3):
            both_x = target[comp, 112:128] + target[comp, 128:144]
            target[comp, 112:128] = both_x
            target[comp, 128:144] = both_x
            inner, outer = pl.ds(7, 16, stride=16), pl.ds(8, 16, stride=16)
            both_z = target[comp, inner, :] + target[comp, outer, :]
            target[comp, inner, :] = both_z
            target[comp, outer, :] = both_z
        started = []

        def put(d, source, into):
            copy = pltpu.make_async_remote_copy(
                src_ref=source,
                dst_ref=into,
                send_sem=send.at[turn, d],
                recv_sem=recv.at[turn, d],
                device_id=neighbours[d],
                device_id_type=MESH_ID,
            )
            copy.start()
            started.append(copy)
            copies.append(copy)

        faces = (pl.ds(240, 16), pl.ds(0, 16), pl.ds(15, 16, stride=16), pl.ds(0, 16, stride=16))
        corners = (255, 240, 15, 0)
        for d in range(4):
            for comp in range(3):
                face[turn - 1, d, comp] = target[comp, faces[d], :]
            put(d, face.at[turn - 1, d], face_in.at[turn - 1, d])
        for d in range(4):
            for comp in range(3):
                row = corners[d]
                edge[turn - 1, d, comp : comp + 1, :] = target[comp, row : row + 1, :]
            put(4 + d, edge.at[turn - 1, d], edge_in.at[turn - 1, d])
        for copy in started:
            copy.wait_recv()
        into = (faces[1], faces[0], faces[3], faces[2])
        corner_into = (0, 15, 240, 255)
        for d in range(4):
            for comp in range(3):
                target[comp, into[d], :] = target[comp, into[d], :] + face_in[turn - 1, d, comp]
        for d in range(4):
            for comp in range(3):
                row = corner_into[d]
                target[comp, row : row + 1, :] = (
                    target[comp, row : row + 1, :] + edge_in[turn - 1, d, comp : comp + 1, :]
                )

    def weighted(pairs):
        for comp in range(3):
            totals = [jnp.zeros((16, 128), jnp.float32) for _ in pairs]
            edges = [jnp.zeros((16, 128), jnp.float32) for _ in pairs]
            for i in range(16):
                for n, (first, second, _) in enumerate(pairs):
                    term = (
                        first[comp, 16 * i : 16 * i + 16] * second[comp, 16 * i : 16 * i + 16]
                    )
                    if i % 8 in (0, 7):
                        edges[n] = edges[n] + term
                    else:
                        totals[n] = totals[n] + term
            for n, (_, _, index) in enumerate(pairs):
                mom[3 * index + comp] = fold((totals[n] + 0.5 * edges[n]) * count2)

    operate(res, one, 1)
    exchange(one, 1)
    operate(one, two, 3)
    exchange(two, 2)
    weighted([(res, res, 0), (one, one, 2), (two, two, 4)])
    operate(two, None, 5)

    row = jnp.zeros((8, 128), jnp.float32)
    for k in range(18):
        value = jnp.sum(mom[k], axis=1, keepdims=True)
        row = row + jnp.where(lane8 == k, value, 0.0)
    row = jnp.sum(row, axis=0, keepdims=True)

    start = 0
    for phase, (count, mine, place) in enumerate(groups):
        part[phase] = row
        started = []
        for k in range(1, count):
            copy = pltpu.make_async_remote_copy(
                src_ref=part.at[phase],
                dst_ref=part_in.at[start + mine],
                send_sem=sum_send.at[start + k],
                recv_sem=sum_recv.at[start + k],
                device_id=place((mine + k) % count),
                device_id_type=MESH_ID,
            )
            copy.start()
            started.append(copy)
            copies.append(copy)
        part_in[start + mine] = row
        for copy in started:
            copy.wait_recv()
        row = part_in[start]
        for k in range(1, count):
            row = row + part_in[start + k]
        start += count

    row = jnp.broadcast_to(row, (8, 128))
    moments = [row if j == 0 else pltpu.roll(row, 128 - 3 * j, 1) for j in range(6)]

    def inner(first, second, raise_by):
        total = None
        for i, a in enumerate(first):
            for j, b in enumerate(second):
                term = a * b * moments[i + j + raise_by]
                total = term if total is None else total + term
        return total

    unit = jnp.ones((8, 128), jnp.float32)
    direction, residual = [unit], [unit]
    answer = [jnp.zeros((8, 128), jnp.float32)] * 3
    norm = moments[0]
    for step in range(3):
        alpha = norm / inner(direction, direction, 1)
        for i, value in enumerate(direction):
            answer[i] = answer[i] + alpha * value
        if step == 2:
            break
        lowered = [-alpha * value for value in direction]
        residual = [residual[0]] + [
            lowered[i] + residual[i + 1] if i + 1 < len(residual) else lowered[i]
            for i in range(len(lowered))
        ]
        newer = inner(residual, residual, 0)
        growth = newer / norm
        direction = [
            value + growth * direction[i] if i < len(direction) else value
            for i, value in enumerate(residual)
        ]
        norm = newer
    for comp in range(3):
        c0, c1, c2 = (
            jnp.broadcast_to(value[:1, comp : comp + 1] * SCALE, (16, 128)) for value in answer
        )
        for i in range(16):
            rows = pl.ds(16 * i, 16)
            out[comp, i] = (
                c0 * res[comp, rows, :] + c1 * one[comp, rows, :] + c2 * two[comp, rows, :]
            )
    for copy in copies:
        copy.wait_send()


def body(sizes, velocity_old, heights, owner_device, owner_element, ref_coords, roughness):
    nx, ny, nc, ns = sizes
    slots = nx * nc + ny + ns
    vmem = pl.BlockSpec(memory_space=pltpu.VMEM)
    smem = pl.BlockSpec(memory_space=pltpu.SMEM)
    f32 = jnp.float32
    constants = [jnp.asarray(value) for value in tables()]
    return pl.pallas_call(
        functools.partial(kernel, sizes),
        out_shape=(
            jax.ShapeDtypeStruct((3, 16, 16, 128), f32),
            jax.ShapeDtypeStruct((2, 512), f32),
        ),
        in_specs=[vmem, smem] + [vmem] * 7,
        out_specs=(vmem, vmem),
        scratch_shapes=[
            pltpu.VMEM((3, 256, 128), f32),
            pltpu.VMEM((3, 256, 128), f32),
            pltpu.VMEM((3, 256, 128), f32),
            pltpu.VMEM((128, 128), f32),
            pltpu.VMEM((2, 4, 16, 128), f32),
            pltpu.VMEM((2, 2, 4, 16, 128), f32),
            pltpu.VMEM((8, 128), f32),
            pltpu.VMEM((8, 8, 128), f32),
            pltpu.VMEM((2, 4, 3, 16, 128), f32),
            pltpu.VMEM((2, 4, 3, 16, 128), f32),
            pltpu.VMEM((2, 4, 3, 128), f32),
            pltpu.VMEM((2, 4, 3, 128), f32),
            pltpu.VMEM((18, 8, 128), f32),
            pltpu.VMEM((3, 1, 128), f32),
            pltpu.VMEM((slots, 1, 128), f32),
            pltpu.SemaphoreType.DMA((3, 8)),
            pltpu.SemaphoreType.DMA((3, 8)),
            pltpu.SemaphoreType.DMA((2,)),
            pltpu.SemaphoreType.DMA((2,)),
            pltpu.SemaphoreType.DMA((slots,)),
            pltpu.SemaphoreType.DMA((slots,)),
        ],
        compiler_params=pltpu.CompilerParams(collective_id=0, has_side_effects=True),
        name="channel_step",
    )(
        velocity_old,
        heights,
        owner_device.reshape(1, -1),
        owner_element.reshape(1, -1),
        ref_coords,
        roughness.reshape(1, -1),
        *constants,
    )


def torus_program(torus):
    sizes = tuple(torus.shape[name] for name in AXES)
    return jax.shard_map(
        functools.partial(body, sizes),
        mesh=torus,
        in_specs=(
            P(None, WALL, "span", None),
            P(),
            P(WALL_SPAN, None),
            P(WALL_SPAN, None),
            P(None, WALL_SPAN),
            P(WALL_SPAN),
        ),
        out_specs=(P(None, WALL, "span", None), P(None, WALL_SPAN)),
        check_vma=False,
    )


def solution(mesh):
    return torus_program(Mesh(mesh.devices.reshape(4, 8, 2, mesh.shape["span"]), AXES))
```

time: 503 us -> 58.8 us (0.12)
  the two profiles are of different devices: /device:TPU:10 before, /device:TPU:1 now
where the time goes in v1:
time: 58.8 us; the launch traced here: 57.9 us
  Pallas kernels  54.8 us (93%)
  local copies, waits for them, and re-layouts  2.36 us (4%)
  between operations  0.65 us (1%)
    pallas_call x1, Pallas kernels, body(): pl.pallas_call(functools.partial(kernel, sizes), out_shape=(jax.ShapeDtyp...  54.8 us
    unnamed x4, local copies, waits for them, and re-layouts  2.36 us

profile of v1, /device:TPU:1, one launch (start us, length us, event | category | flops | bytes accessed | tf_op | source)
XLA Modules:
  0.0 57.9 jit_solution(11431257643868768020)
XLA Ops:
  0.6 54.8 %channel_step.1 = (f32[3,16,16,128]{3,2,1,0:T(8,128)}, f32[2,512]{1,0:T(2,128)}) custom-call(f32[3,16,16,128]{3,2,1,0:T(8,128)} %velocity.1, f32[16]{0:T(128)} %heights.1, s32[1,512]{1,0:T(1,128)} %bitcast.3, s32[1,512]{1,0:T(1,128)} %bitcast.4, f32[3,512]{1,0:T(4,128)} %coords.1, f32[1,512]{1,0:T(1,128)} %bitcast.5, f32[16,8,128]{2,1,0:T(8,128)} %constant.6.clone.table, ...), custom_call_target="tpu_custom_call" | custom-call | tf_op jit(solution)/shard_map/channel_step/pallas_call | solution.py:561
  55.5 0.0 copy-start
  55.5 1.8 %copy.13 = f32[3,16,16,128]{3,2,1,0:T(8,128)} copy(f32[3,16,16,128]{3,2,1,0:T(8,128)} %get-tuple-element.4) | data formatting | bytes 786432
  57.3 0.0 copy-done
  57.3 0.6 %copy.14 = f32[2,512]{1,0:T(2,128)} copy(f32[2,512]{1,0:T(2,128)S(1)} %copy-done) | data formatting | bytes 8192
Async XLA Ops:
  55.5 1.8 %copy-start = (f32[2,512]{1,0:T(2,128)S(1)}, f32[2,512]{1,0:T(2,128)}, u32[]{:S(2)}) copy-start(f32[2,512]{1,0:T(2,128)} %get-tuple-element.5) | copy-start | bytes 12292

commit v2 on v1

--- a/solution.py
+++ b/solution.py
@@ -109,10 +109,17 @@
     return as32(np.stack(rows)), as32(block), as32(lift)
 
 
-def kernel(sizes, velocity, heights, owner, element, coords, roughness, table, block, lift,
-           out, neumann, res, one, two, stiff, slab, slab_in, plane, plane_in, face, face_in,
-           edge, edge_in, mom, part, part_in, send, recv, slab_send, slab_recv, sum_send,
-           sum_recv):
+def kernel(sizes, *refs):
+    operands, refs = refs[:9], refs[9:]
+    (res, one, two, scalars, neumann), refs = refs[:5], refs[5:]
+    local, refs = refs[:9], refs[9:]
+    velocity, heights, owner, element, coords, roughness, table, block, lift = local
+    (stiff, slab, slab_in, plane, plane_in, face, face_in, edge, edge_in, mom, part, part_in,
+     load, send, recv, slab_send, slab_recv, sum_send, sum_recv) = refs
+    loads = [
+        pltpu.make_async_copy(source, target, load.at[n])
+        for n, (source, target) in enumerate(zip(operands, local))
+    ]
     nx, ny, nc, ns = sizes
     nw = nx * ny * nc
     wx, wy, wc, sp = (lax.axis_index(name) for name in AXES)
@@ -136,9 +143,13 @@
     peers = list(neighbours)
     for count, mine, place in groups:
         peers += [place((mine + k) % count) for k in range(1, count)]
+    for copy in loads:
+        copy.start()
     barrier = pltpu.get_barrier_semaphore()
     for peer in peers:
         pl.semaphore_signal(barrier, inc=1, device_id=peer, device_id_type=MESH_ID)
+    for copy in loads:
+        copy.wait()
 
     lane = lax.broadcasted_iota(jnp.int32, (1, 128), 1)
     sub8 = lax.broadcasted_iota(jnp.int32, (8, 128), 0)
@@ -538,38 +549,59 @@
             for i, value in enumerate(residual)
         ]
         norm = newer
+    for i, value in enumerate(answer):
+        scalars[i : i + 1, :] = value[:1] * SCALE
+    for copy in copies:
+        copy.wait_send()
+
+
+def combine(res, one, two, scalars, slopes, out, neumann, sums, sent):
+    copies = [pltpu.make_async_copy(slopes, neumann, sent.at[3])]
+    copies[0].start()
     for comp in range(3):
         c0, c1, c2 = (
-            jnp.broadcast_to(value[:1, comp : comp + 1] * SCALE, (16, 128)) for value in answer
+            jnp.broadcast_to(scalars[k : k + 1, comp : comp + 1], (16, 128)) for k in range(3)
         )
         for i in range(16):
             rows = pl.ds(16 * i, 16)
-            out[comp, i] = (
+            sums[comp, i] = (
                 c0 * res[comp, rows, :] + c1 * one[comp, rows, :] + c2 * two[comp, rows, :]
             )
+        copy = pltpu.make_async_copy(sums.at[comp], out.at[comp], sent.at[comp])
+        copy.start()
+        copies.append(copy)
     for copy in copies:
-        copy.wait_send()
+        copy.wait()
 
 
 def body(sizes, velocity_old, heights, owner_device, owner_element, ref_coords, roughness):
     nx, ny, nc, ns = sizes
     slots = nx * nc + ny + ns
+    f32, i32 = jnp.float32, jnp.int32
     vmem = pl.BlockSpec(memory_space=pltpu.VMEM)
-    smem = pl.BlockSpec(memory_space=pltpu.SMEM)
-    f32 = jnp.float32
+    anywhere = pl.BlockSpec(memory_space=pl.ANY)
     constants = [jnp.asarray(value) for value in tables()]
-    return pl.pallas_call(
+    res, one, two, scalars, slopes = pl.pallas_call(
         functools.partial(kernel, sizes),
         out_shape=(
-            jax.ShapeDtypeStruct((3, 16, 16, 128), f32),
-            jax.ShapeDtypeStruct((2, 512), f32),
-        ),
-        in_specs=[vmem, smem] + [vmem] * 7,
-        out_specs=(vmem, vmem),
-        scratch_shapes=[
             pltpu.VMEM((3, 256, 128), f32),
             pltpu.VMEM((3, 256, 128), f32),
             pltpu.VMEM((3, 256, 128), f32),
+            pltpu.VMEM((8, 128), f32),
+            pltpu.VMEM((2, 512), f32),
+        ),
+        in_specs=[anywhere] * 9,
+        out_specs=(vmem,) * 5,
+        scratch_shapes=[
+            pltpu.VMEM((3, 16, 16, 128), f32),
+            pltpu.SMEM((16,), f32),
+            pltpu.VMEM((1, 512), i32),
+            pltpu.VMEM((1, 512), i32),
+            pltpu.VMEM((3, 512), f32),
+            pltpu.VMEM((1, 512), f32),
+            pltpu.VMEM(constants[0].shape, f32),
+            pltpu.VMEM(constants[1].shape, f32),
+            pltpu.VMEM(constants[2].shape, f32),
             pltpu.VMEM((128, 128), f32),
             pltpu.VMEM((2, 4, 16, 128), f32),
             pltpu.VMEM((2, 2, 4, 16, 128), f32),
@@ -582,6 +614,7 @@
             pltpu.VMEM((18, 8, 128), f32),
             pltpu.VMEM((3, 1, 128), f32),
             pltpu.VMEM((slots, 1, 128), f32),
+            pltpu.SemaphoreType.DMA((9,)),
             pltpu.SemaphoreType.DMA((3, 8)),
             pltpu.SemaphoreType.DMA((3, 8)),
             pltpu.SemaphoreType.DMA((2,)),
@@ -600,6 +633,25 @@
         roughness.reshape(1, -1),
         *constants,
     )
+    return pl.pallas_call(
+        combine,
+        out_shape=(
+            jax.ShapeDtypeStruct((3, 16, 16, 128), f32),
+            jax.ShapeDtypeStruct((2, 512), f32),
+        ),
+        in_specs=[vmem] * 5,
+        out_specs=(anywhere, anywhere),
+        scratch_shapes=[
+            pltpu.VMEM((3, 16, 16, 128), f32),
+            pltpu.SemaphoreType.DMA((4,)),
+        ],
+        name="combine",
+    )(
+        *(
+            pltpu.with_memory_space_constraint(value, pltpu.VMEM)
+            for value in (res, one, two, scalars, slopes)
+        )
+    )
 
 
 def torus_program(torus):

time: 58.8 us -> 55.5 us (0.944)
  local copies, waits for them, and re-layouts: 2.36 us -> 0 us
  Pallas kernels: 54.8 us -> 53.9 us
    unnamed x4 -> x0, local copies, waits for them, and re-layouts: 2.36 us -> none
    pallas_call x1 -> x2, Pallas kernels: 54.8 us -> 53.9 us  [the longest x1 53 us: body(): pl.pallas_call(functools.partial(kernel, sizes), out_shape=(pltpu.VMEM((3...]
where the time goes in v2:
time: 55.5 us; the launch traced here: 54.5 us
  Pallas kernels  53.9 us (97%)
  between operations  0.64 us (1%)
    pallas_call x1, Pallas kernels, body(): pl.pallas_call(functools.partial(kernel, sizes), out_shape=(pltpu.VMEM((3...  53 us

profile of v2, /device:TPU:1, one launch (start us, length us, event | category | flops | bytes accessed | tf_op | source)
XLA Modules:
  0.0 54.5 jit_solution(190295260136443656)
XLA Ops:
  0.6 53.0 %channel_step.1 = (f32[3,256,128]{2,1,0:T(8,128)S(1)}, f32[3,256,128]{2,1,0:T(8,128)S(1)}, f32[3,256,128]{2,1,0:T(8,128)S(1)}, f32[8,128]{1,0:T(8,128)S(1)}, f32[2,512]{1,0:T(2,128)S(1)}) custom-call(f32[3,16,16,128]{3,2,1,0:T(8,128)} %refs_0_.1, f32[16]{0:T(128)} %refs_1_.1, s32[1,512]{1,0:T(1,128)} %bitcast.3, s32[1,512]{1,0:T(1,128)} %bitcast.4, ...), custom_call_target="tpu_custom_call" | custom-call | tf_op jit(solution)/shard_map/channel_step/pallas_call | solution.py:584
  53.7 0.9 %combine.1 = (f32[3,16,16,128]{3,2,1,0:T(8,128)}, f32[2,512]{1,0:T(2,128)}) custom-call(f32[3,256,128]{2,1,0:T(8,128)S(1)} %get-tuple-element.7.res, f32[3,256,128]{2,1,0:T(8,128)S(1)} %get-tuple-element.8.one, f32[3,256,128]{2,1,0:T(8,128)S(1)} %get-tuple-element.9.two, f32[8,128]{1,0:T(8,128)S(1)} %get-tuple-element.10.scalars, ...), custom_call_target="tpu_custom_call" | custom-call | tf_op jit(solution)/shard_map/combine/pallas_call | solution.py:636

commit v3 on v2

--- a/solution.py
+++ b/solution.py
@@ -48,6 +48,7 @@
 SHIFTS = ((1, 0), (-1, 0), (0, 1), (0, -1), (1, 1), (1, -1), (-1, 1), (-1, -1))
 
 MZ, QMZ, COUNT, LAG, PLANE, HALFW, LAST, FIRST, KZ = range(9)
+BLOCK, LIFT = 16, 32
 
 
 def stiffness_table():
@@ -105,23 +106,25 @@
             column = (comp * 2 + half) * 128
             lift[comp * 4 + half, column] = 1.0
             lift[comp * 4 + 2 + half, column + 127] = 1.0
-    as32 = lambda value: np.asarray(value, np.float32)
-    return as32(np.stack(rows)), as32(block), as32(lift)
+    pieces = [np.stack(rows), block.reshape(16, 8, 128), lift.reshape(8, 4, 128).transpose(1, 0, 2)]
+    return np.concatenate(pieces).astype(np.float32)
 
 
 def kernel(sizes, *refs):
-    operands, refs = refs[:9], refs[9:]
+    operands, refs = refs[:7], refs[7:]
     (res, one, two, scalars, neumann), refs = refs[:5], refs[5:]
-    local, refs = refs[:9], refs[9:]
-    velocity, heights, owner, element, coords, roughness, table, block, lift = local
-    (stiff, slab, slab_in, plane, plane_in, face, face_in, edge, edge_in, mom, part, part_in,
-     load, send, recv, slab_send, slab_recv, sum_send, sum_recv) = refs
+    local, refs = refs[:7], refs[7:]
+    velocity, heights, owner, element, coords, roughness, table = local
+    (stiff, stiff_joined, slab, slab_in, plane, plane_in, face, face_in, mom, part, part_in,
+     load, send, slab_recv, recv, ready) = refs
+    nx, ny, nc, ns = sizes
+    nw = nx * ny * nc
     loads = [
         pltpu.make_async_copy(source, target, load.at[n])
         for n, (source, target) in enumerate(zip(operands, local))
     ]
-    nx, ny, nc, ns = sizes
-    nw = nx * ny * nc
+    for copy in loads:
+        copy.start()
     wx, wy, wc, sp = (lax.axis_index(name) for name in AXES)
     wall = (wx * ny + wy) * nc + wc
     weights = np.array(GLL_WEIGHTS)
@@ -129,25 +132,72 @@
     mass_x = [float(v) for v in 0.5 * element_dx * weights]
     ends = [2.0, 1.0, 1.0, 1.0, 1.0, 1.0, 1.0, 2.0]
 
-    def shifted(dw, ds):
-        there = (wall + dw + nw) % nw
-        return (there // (ny * nc), there // nc % ny, there % nc, (sp + ds + ns) % ns)
-
-    neighbours = [shifted(dw, ds) for dw, ds in SHIFTS]
-    pair = wx * nc + wc
+    def ring(value, shift, count):
+        if shift > 0:
+            return jnp.where(value >= count - shift, value + shift - count, value + shift)
+        return jnp.where(value < -shift, value + shift + count, value + shift)
+
+    def beside(dw):
+        if dw == 0:
+            return wx, wy, wc
+        turn = wc == (nc - 1 if dw > 0 else 0)
+        turn_y = jnp.logical_and(turn, wy == (ny - 1 if dw > 0 else 0))
+        return (
+            jnp.where(turn_y, ring(wx, dw, nx), wx),
+            jnp.where(turn, ring(wy, dw, ny), wy),
+            ring(wc, dw, nc),
+        )
+
+    along = {dw: beside(dw) for dw in (-1, 0, 1)}
+    across = {0: sp, 1: ring(sp, 1, ns), -1: ring(sp, -1, ns)}
+    neighbours = [(*along[dw], across[ds]) for dw, ds in SHIFTS]
+    over_x = lambda k: (ring(wx, k, nx), wy, wc, sp)
+    over_y = lambda k: (wx, ring(wy, k, ny), wc, sp)
+    over_z = lambda k: (wx, wy, wc, ring(sp, k, ns))
+    over_pair = lambda k: (
+        ring(wx, k // nc, nx) if k // nc else wx,
+        wy,
+        ring(wc, k % nc, nc) if k % nc else wc,
+        sp,
+    )
     groups = [
-        (nx * nc, pair, lambda q: (q // nc, wy, q % nc, sp)),
-        (ny, wy, lambda q: (wx, q, wc, sp)),
-        (ns, sp, lambda q: (wx, wy, wc, q)),
+        (nx * nc, wx * nc + wc, over_pair),
+        (ny, wy, over_y),
+        (ns, sp, over_z),
     ]
-    peers = list(neighbours)
-    for count, mine, place in groups:
-        peers += [place((mine + k) % count) for k in range(1, count)]
-    for copy in loads:
-        copy.start()
+
     barrier = pltpu.get_barrier_semaphore()
-    for peer in peers:
+    near = list(neighbours) + [over_pair(k) for k in range(nc)][1:]
+    near += [over_pair(k * nc + c) for k in (1, nx - 1) for c in range(nc)]
+    near += [over_y(1), over_y(-1)]
+    for peer in near:
         pl.semaphore_signal(barrier, inc=1, device_id=peer, device_id_type=MESH_ID)
+    relays = [
+        [over_x(1), over_x(-1), over_y(1), over_y(-1), over_z(1), over_z(-1)],
+        [over_y(2), over_y(-2), over_z(2), over_z(-2)],
+        [over_z(2), over_z(-2)],
+    ]
+
+    def tell(n):
+        for peer in relays[n]:
+            pl.semaphore_signal(ready.at[n], inc=1, device_id=peer, device_id_type=MESH_ID)
+
+    def hear(n):
+        pl.semaphore_wait(ready.at[n], len(relays[n]))
+
+    def push(source, target, send_sem, recv_sem, peer):
+        pltpu.make_async_remote_copy(
+            src_ref=source,
+            dst_ref=target,
+            send_sem=send_sem,
+            recv_sem=recv_sem,
+            device_id=peer,
+            device_id_type=MESH_ID,
+        ).start()
+
+    def wait_bytes(like, sem):
+        pltpu.make_async_copy(like, like, sem).wait()
+
     for copy in loads:
         copy.wait()
 
@@ -159,7 +209,13 @@
     for layer in range(16):
         height = jnp.where(lane8 // 8 == layer, heights[layer], height)
     mass_y = height * table[HALFW]
-    stiff[...] = block[...] * (1.0 / height)[:1]
+    block = table[BLOCK : BLOCK + 16].reshape(128, 128) * (1.0 / height)[:1]
+    stiff[...] = block
+    stiff_joined[...] = (
+        block
+        + table[LAST][:1] * pltpu.roll(block, 127, 1)
+        + table[FIRST][:1] * pltpu.roll(block, 1, 1)
+    )
     joined_y = (
         mass_y
         + table[LAST] * pltpu.roll(mass_y, 127, 1)
@@ -169,7 +225,9 @@
     mass_zy = both(table[MZ] * mass_y)
     mass_y2 = both(mass_y)
     mass_z2 = both(table[MZ])
-    last2, first2 = both(table[LAST]), both(table[FIRST])
+    joined_y2 = both(joined_y)
+    joined_z2 = both(table[QMZ])
+    joined_zy = both(table[QMZ] * joined_y)
     count2 = both(table[COUNT])
 
     for comp in range(2):
@@ -225,22 +283,11 @@
             value = value * jnp.where(sub8 == b, 1.0, coord - GLL_NODES[b])
         return value
 
-    pl.semaphore_wait(barrier, len(peers))
-
-    copies = []
-    slab_copies = []
+    pl.semaphore_wait(barrier, len(near))
+
+    tell(0)
     for d in range(2):
-        copy = pltpu.make_async_remote_copy(
-            src_ref=slab,
-            dst_ref=slab_in.at[d],
-            send_sem=slab_send.at[d],
-            recv_sem=slab_recv.at[d],
-            device_id=neighbours[d],
-            device_id_type=MESH_ID,
-        )
-        copy.start()
-        slab_copies.append(copy)
-        copies.append(copy)
+        push(slab, slab_in.at[d], send.at[0], slab_recv.at[d], neighbours[d])
 
     basis = [[lagrange(axes[k][g]) for k in range(3)] for g in range(4)]
     second_wall = (lane // 8) % 2 == 1
@@ -284,7 +331,7 @@
         own = sample(slab, g)
         sums.append([own[comp] * masks[g][0] for comp in range(2)])
     for d in range(2):
-        slab_copies[d].wait_recv()
+        wait_bytes(slab_in.at[d], slab_recv.at[d])
         for g in range(4):
             far = sample(slab_in.at[d], g)
             for comp in range(2):
@@ -306,19 +353,10 @@
             neumann[comp : comp + 1, 128 * q : 128 * q + 128] = slope[:1]
             plane[comp * 4 + q : comp * 4 + q + 1, :] = (viscosity * slope * table[PLANE])[:1]
 
-    plane_copies = []
     for d in range(8):
-        copy = pltpu.make_async_remote_copy(
-            src_ref=plane,
-            dst_ref=plane_in.at[d],
-            send_sem=send.at[0, d],
-            recv_sem=recv.at[0, d],
-            device_id=neighbours[d],
-            device_id_type=MESH_ID,
-        )
-        copy.start()
-        plane_copies.append(copy)
-        copies.append(copy)
+        push(plane, plane_in.at[d], send.at[1], recv.at[0], neighbours[d])
+    hear(0)
+    tell(1)
 
     node_z = lane8 % 16
     node_x = lane8 // 16
@@ -342,15 +380,14 @@
             + jnp.where(node_x == 0, pltpu.roll(earlier, 16, 1), 0.0)
         )
 
-    for d in range(8):
-        plane_copies[d].wait_recv()
+    wait_bytes(plane_in, recv.at[0])
     own_line = join_span(plane[...], plane_in[2], plane_in[3])
     before_line = join_span(plane_in[0], plane_in[4], plane_in[5])
     after_line = join_span(plane_in[1], plane_in[6], plane_in[7])
     stress = join_wall(own_line, before_line, after_line)
     lifted = lax.dot_general(
         stress,
-        lift[...],
+        jnp.concatenate([table[LIFT + k] for k in range(4)], axis=1),
         (((0,), (0,)), ((), ())),
         precision=precise,
         preferred_element_type=jnp.float32,
@@ -368,100 +405,104 @@
     def fold(value):
         return value[:8] + value[8:]
 
-    def operate(source, target, index):
+    def spectral_x(nodes):
+        plus = [nodes[b] + nodes[7 - b] for b in range(4)]
+        minus = [nodes[b] - nodes[7 - b] for b in range(4)]
+        result = [None] * 8
+        for a in range(4):
+            sum_e = plus[0] * float(even[a, 0])
+            sum_o = minus[0] * float(odd[a, 0])
+            for b in range(1, 4):
+                sum_e = sum_e + plus[b] * float(even[a, b])
+                sum_o = sum_o + minus[b] * float(odd[a, b])
+            result[a] = sum_e + sum_o
+            result[7 - a] = sum_e - sum_o
+        return result
+
+    def spectral_z(source, comp, start):
+        halves = []
+        for h in range(2):
+            total = None
+            for b in range(8):
+                row = start + 8 * h + b
+                term = source[comp, row : row + 1] * table[KZ + b]
+                total = term if total is None else total + term
+            halves.append(total)
+        return halves
+
+    def along_y(source, comp, base, matrix):
+        return jnp.dot(
+            source[comp, base : base + 128],
+            matrix[...],
+            precision=precise,
+            preferred_element_type=jnp.float32,
+        )
+
+    def operate(source, target, turn):
+        for comp in range(3):
+            seam = None
+            for ex in range(2):
+                base = 128 * ex
+                normal = along_y(source, comp, base, stiff_joined)
+                nodes = [source[comp, base + 16 * b : base + 16 * b + 16] for b in range(8)]
+                stream = [value * joined_zy for value in spectral_x(nodes)]
+                if ex == 0:
+                    face[turn, 1, comp] = stream[0]
+                    seam = stream[7]
+                else:
+                    face[turn, 0, comp] = stream[7]
+                    target[comp, 112:128] = target[comp, 112:128] + stream[0]
+                    stream[0] = stream[0] + seam
+                for a in range(8):
+                    start = base + 16 * a
+                    low, high = spectral_z(source, comp, start)
+                    i = 8 * ex + a
+                    edge = mass_x[a] * ends[a]
+                    face[turn, 3, comp, i : i + 1] = (low * joined_y)[:1] * edge
+                    face[turn, 2, comp, i : i + 1] = (high * joined_y)[7:] * edge
+                    joined = jnp.concatenate(
+                        [
+                            low + jnp.where(sub8 == 7, pltpu.roll(high, 7, 0), 0.0),
+                            high + jnp.where(sub8 == 0, pltpu.roll(low, 1, 0), 0.0),
+                        ],
+                        axis=0,
+                    )
+                    target[comp, start : start + 16] = stream[a] + edge * (
+                        joined * joined_y2 + normal[16 * a : 16 * a + 16] * joined_z2
+                    )
+        for d in range(4):
+            push(
+                face.at[turn, d], face_in.at[turn, d], send.at[2 + turn], recv.at[1 + turn],
+                neighbours[d],
+            )
+
+    def receive(target, turn):
+        wait_bytes(face_in.at[turn], recv.at[1 + turn])
+        into = (
+            pl.ds(0, 16),
+            pl.ds(240, 16),
+            pl.ds(0, 16, stride=16),
+            pl.ds(15, 16, stride=16),
+        )
+        for d in range(4):
+            for comp in range(3):
+                target[comp, into[d], :] = target[comp, into[d], :] + face_in[turn, d, comp]
+
+    def energy(source, index):
         for comp in range(3):
             total = jnp.zeros((16, 128), jnp.float32)
             for ex in range(2):
                 base = 128 * ex
-                along_y = jnp.dot(
-                    source[comp, base : base + 128],
-                    stiff[...],
-                    precision=precise,
-                    preferred_element_type=jnp.float32,
-                )
+                normal = along_y(source, comp, base, stiff)
                 nodes = [source[comp, base + 16 * b : base + 16 * b + 16] for b in range(8)]
-                plus = [nodes[b] + nodes[7 - b] for b in range(4)]
-                minus = [nodes[b] - nodes[7 - b] for b in range(4)]
-                along_x = [None] * 8
-                for a in range(4):
-                    sum_e = plus[0] * float(even[a, 0])
-                    sum_o = minus[0] * float(odd[a, 0])
-                    for b in range(1, 4):
-                        sum_e = sum_e + plus[b] * float(even[a, b])
-                        sum_o = sum_o + minus[b] * float(odd[a, b])
-                    along_x[a] = sum_e + sum_o
-                    along_x[7 - a] = sum_e - sum_o
+                stream = spectral_x(nodes)
                 for a in range(8):
-                    start = base + 16 * a
-                    halves = []
-                    for h in range(2):
-                        along_z = None
-                        for b in range(8):
-                            row = start + 8 * h + b
-                            term = source[comp, row : row + 1] * table[KZ + b]
-                            along_z = term if along_z is None else along_z + term
-                        halves.append(along_z)
-                    along_z = jnp.concatenate(halves, axis=0)
-                    local = along_x[a] * mass_zy + (
-                        along_z * mass_y2 + along_y[16 * a : 16 * a + 16] * mass_z2
-                    ) * mass_x[a]
+                    spanned = jnp.concatenate(spectral_z(source, comp, base + 16 * a), axis=0)
+                    local = stream[a] * mass_zy + mass_x[a] * (
+                        spanned * mass_y2 + normal[16 * a : 16 * a + 16] * mass_z2
+                    )
                     total = total + local * nodes[a]
-                    if target is not None:
-                        target[comp, start : start + 16] = (
-                            local
-                            + last2 * pltpu.roll(local, 127, 1)
-                            + first2 * pltpu.roll(local, 1, 1)
-                        )
             mom[3 * index + comp] = fold(total)
-
-    def exchange(target, turn):
-        for comp in range(3):
-            both_x = target[comp, 112:128] + target[comp, 128:144]
-            target[comp, 112:128] = both_x
-            target[comp, 128:144] = both_x
-            inner, outer = pl.ds(7, 16, stride=16), pl.ds(8, 16, stride=16)
-            both_z = target[comp, inner, :] + target[comp, outer, :]
-            target[comp, inner, :] = both_z
-            target[comp, outer, :] = both_z
-        started = []
-
-        def put(d, source, into):
-            copy = pltpu.make_async_remote_copy(
-                src_ref=source,
-                dst_ref=into,
-                send_sem=send.at[turn, d],
-                recv_sem=recv.at[turn, d],
-                device_id=neighbours[d],
-                device_id_type=MESH_ID,
-            )
-            copy.start()
-            started.append(copy)
-            copies.append(copy)
-
-        faces = (pl.ds(240, 16), pl.ds(0, 16), pl.ds(15, 16, stride=16), pl.ds(0, 16, stride=16))
-        corners = (255, 240, 15, 0)
-        for d in range(4):
-            for comp in range(3):
-                face[turn - 1, d, comp] = target[comp, faces[d], :]
-            put(d, face.at[turn - 1, d], face_in.at[turn - 1, d])
-        for d in range(4):
-            for comp in range(3):
-                row = corners[d]
-                edge[turn - 1, d, comp : comp + 1, :] = target[comp, row : row + 1, :]
-            put(4 + d, edge.at[turn - 1, d], edge_in.at[turn - 1, d])
-        for copy in started:
-            copy.wait_recv()
-        into = (faces[1], faces[0], faces[3], faces[2])
-        corner_into = (0, 15, 240, 255)
-        for d in range(4):
-            for comp in range(3):
-                target[comp, into[d], :] = target[comp, into[d], :] + face_in[turn - 1, d, comp]
-        for d in range(4):
-            for comp in range(3):
-                row = corner_into[d]
-                target[comp, row : row + 1, :] = (
-                    target[comp, row : row + 1, :] + edge_in[turn - 1, d, comp : comp + 1, :]
-                )
 
     def weighted(pairs):
         for comp in range(3):
@@ -479,12 +520,16 @@
             for n, (_, _, index) in enumerate(pairs):
                 mom[3 * index + comp] = fold((totals[n] + 0.5 * edges[n]) * count2)
 
-    operate(res, one, 1)
-    exchange(one, 1)
-    operate(one, two, 3)
-    exchange(two, 2)
-    weighted([(res, res, 0), (one, one, 2), (two, two, 4)])
-    operate(two, None, 5)
+    operate(res, one, 0)
+    hear(1)
+    tell(2)
+    receive(one, 0)
+    operate(one, two, 1)
+    weighted([(res, res, 0), (res, one, 1), (one, one, 2)])
+    hear(2)
+    receive(two, 1)
+    weighted([(one, two, 3), (two, two, 4)])
+    energy(two, 5)
 
     row = jnp.zeros((8, 128), jnp.float32)
     for k in range(18):
@@ -495,22 +540,13 @@
     start = 0
     for phase, (count, mine, place) in enumerate(groups):
         part[phase] = row
-        started = []
         for k in range(1, count):
-            copy = pltpu.make_async_remote_copy(
-                src_ref=part.at[phase],
-                dst_ref=part_in.at[start + mine],
-                send_sem=sum_send.at[start + k],
-                recv_sem=sum_recv.at[start + k],
-                device_id=place((mine + k) % count),
-                device_id_type=MESH_ID,
+            push(
+                part.at[phase], part_in.at[start + mine], send.at[4 + phase], recv.at[3 + phase],
+                place(k),
             )
-            copy.start()
-            started.append(copy)
-            copies.append(copy)
         part_in[start + mine] = row
-        for copy in started:
-            copy.wait_recv()
+        wait_bytes(part_in.at[pl.ds(start, count - 1)], recv.at[3 + phase])
         row = part_in[start]
         for k in range(1, count):
             row = row + part_in[start + k]
@@ -551,8 +587,14 @@
         norm = newer
     for i, value in enumerate(answer):
         scalars[i : i + 1, :] = value[:1] * SCALE
-    for copy in copies:
-        copy.wait_send()
+    wait_bytes(slab_in, send.at[0])
+    wait_bytes(plane_in, send.at[1])
+    for turn in range(2):
+        wait_bytes(face_in.at[turn], send.at[2 + turn])
+    start = 0
+    for phase, (count, _, _) in enumerate(groups):
+        wait_bytes(part_in.at[pl.ds(start, count - 1)], send.at[4 + phase])
+        start += count
 
 
 def combine(res, one, two, scalars, slopes, out, neumann, sums, sent):
@@ -580,7 +622,7 @@
     f32, i32 = jnp.float32, jnp.int32
     vmem = pl.BlockSpec(memory_space=pltpu.VMEM)
     anywhere = pl.BlockSpec(memory_space=pl.ANY)
-    constants = [jnp.asarray(value) for value in tables()]
+    constants = jnp.asarray(tables())
     res, one, two, scalars, slopes = pl.pallas_call(
         functools.partial(kernel, sizes),
         out_shape=(
@@ -590,7 +632,7 @@
             pltpu.VMEM((8, 128), f32),
             pltpu.VMEM((2, 512), f32),
         ),
-        in_specs=[anywhere] * 9,
+        in_specs=[anywhere] * 7,
         out_specs=(vmem,) * 5,
         scratch_shapes=[
             pltpu.VMEM((3, 16, 16, 128), f32),
@@ -599,9 +641,8 @@
             pltpu.VMEM((1, 512), i32),
             pltpu.VMEM((3, 512), f32),
             pltpu.VMEM((1, 512), f32),
-            pltpu.VMEM(constants[0].shape, f32),
-            pltpu.VMEM(constants[1].shape, f32),
-            pltpu.VMEM(constants[2].shape, f32),
+            pltpu.VMEM(constants.shape, f32),
+            pltpu.VMEM((128, 128), f32),
             pltpu.VMEM((128, 128), f32),
             pltpu.VMEM((2, 4, 16, 128), f32),
             pltpu.VMEM((2, 2, 4, 16, 128), f32),
@@ -609,18 +650,14 @@
             pltpu.VMEM((8, 8, 128), f32),
             pltpu.VMEM((2, 4, 3, 16, 128), f32),
             pltpu.VMEM((2, 4, 3, 16, 128), f32),
-            pltpu.VMEM((2, 4, 3, 128), f32),
-            pltpu.VMEM((2, 4, 3, 128), f32),
             pltpu.VMEM((18, 8, 128), f32),
             pltpu.VMEM((3, 1, 128), f32),
             pltpu.VMEM((slots, 1, 128), f32),
-            pltpu.SemaphoreType.DMA((9,)),
-            pltpu.SemaphoreType.DMA((3, 8)),
-            pltpu.SemaphoreType.DMA((3, 8)),
+            pltpu.SemaphoreType.DMA((7,)),
+            pltpu.SemaphoreType.DMA((7,)),
             pltpu.SemaphoreType.DMA((2,)),
-            pltpu.SemaphoreType.DMA((2,)),
-            pltpu.SemaphoreType.DMA((slots,)),
-            pltpu.SemaphoreType.DMA((slots,)),
+            pltpu.SemaphoreType.DMA((6,)),
+            pltpu.SemaphoreType.REGULAR((3,)),
         ],
         compiler_params=pltpu.CompilerParams(collective_id=0, has_side_effects=True),
         name="channel_step",
@@ -631,7 +668,7 @@
         owner_element.reshape(1, -1),
         ref_coords,
         roughness.reshape(1, -1),
-        *constants,
+        constants,
     )
     return pl.pallas_call(
         combine,

time: 55.5 us -> 50.2 us (0.905)
  Pallas kernels: 53.9 us -> 48.6 us
    pallas_call x1, Pallas kernels: 53 us -> 47.8 us  [body(): pl.pallas_call(functools.partial(kernel, sizes), out_shape=(pltpu.VMEM((3...]
where the time goes in v3:
time: 50.2 us; the launch traced here: 49.3 us
  Pallas kernels  48.6 us (97%)
  between operations  0.64 us (1%)
    pallas_call x1, Pallas kernels, body(): pl.pallas_call(functools.partial(kernel, sizes), out_shape=(pltpu.VMEM((3...  47.8 us

profile of v3, /device:TPU:1, one launch (start us, length us, event | category | flops | bytes accessed | tf_op | source)
XLA Modules:
  0.0 49.3 jit_solution(6602215857070339575)
XLA Ops:
  0.6 47.8 %channel_step.1 = (f32[3,256,128]{2,1,0:T(8,128)S(1)}, f32[3,256,128]{2,1,0:T(8,128)S(1)}, f32[3,256,128]{2,1,0:T(8,128)S(1)}, f32[8,128]{1,0:T(8,128)S(1)}, f32[2,512]{1,0:T(2,128)S(1)}) custom-call(f32[3,16,16,128]{3,2,1,0:T(8,128)} %refs_0_.1, f32[16]{0:T(128)} %refs_1_.1, s32[1,512]{1,0:T(1,128)} %bitcast.3, s32[1,512]{1,0:T(1,128)} %bitcast.4, ...), custom_call_target="tpu_custom_call" | custom-call | tf_op jit(solution)/shard_map/channel_step/pallas_call | solution.py:626
  48.4 0.9 %combine.1 = (f32[3,16,16,128]{3,2,1,0:T(8,128)}, f32[2,512]{1,0:T(2,128)}) custom-call(f32[3,256,128]{2,1,0:T(8,128)S(1)} %get-tuple-element.7.res, f32[3,256,128]{2,1,0:T(8,128)S(1)} %get-tuple-element.8.one, f32[3,256,128]{2,1,0:T(8,128)S(1)} %get-tuple-element.9.two, f32[8,128]{1,0:T(8,128)S(1)} %get-tuple-element.10.scalars, ...), custom_call_target="tpu_custom_call" | custom-call | tf_op jit(solution)/shard_map/combine/pallas_call | solution.py:673

commit v4 on v3

--- a/solution.py
+++ b/solution.py
@@ -47,8 +47,8 @@
 
 SHIFTS = ((1, 0), (-1, 0), (0, 1), (0, -1), (1, 1), (1, -1), (-1, 1), (-1, -1))
 
-MZ, QMZ, COUNT, LAG, PLANE, HALFW, LAST, FIRST, KZ = range(9)
-BLOCK, LIFT = 16, 32
+MZ, QMZ, COUNT, LAG, PLANE, HALFW, LAST, FIRST = range(8)
+BLOCK, LIFT, FLAT = 8, 24, 28
 
 
 def stiffness_table():
@@ -85,9 +85,6 @@
     count_y = np.where((lane % 8 == 0) | (lane % 8 == 7), 0.5, 1.0)
     count_y[0] = count_y[127] = 1.0
     gaps = points[:, None] - points[None, :] + np.eye(8)
-    kz = SCALE * (
-        viscosity * (2.0 / element_dz) * stiffness + inverse_step * np.diag(mass_z)
-    )
     rows = [
         mass_z[:, None] * ones,
         (mass_z * ends)[:, None] * ones,
@@ -98,7 +95,6 @@
         ones * ((lane % 8 == 7) & (lane < 127))[None, :],
         ones * ((lane % 8 == 0) & (lane > 0))[None, :],
     ]
-    rows += [kz[:, b][:, None] * ones for b in range(8)]
     block = np.kron(np.eye(16), SCALE * viscosity * 2.0 * stiffness)
     lift = np.zeros((8, 512))
     for comp in range(2):
@@ -106,16 +102,36 @@
             column = (comp * 2 + half) * 128
             lift[comp * 4 + half, column] = 1.0
             lift[comp * 4 + 2 + half, column + 127] = 1.0
+    joined_x = np.tile(mass_x * ends, 2)
+    joined_z = np.tile(mass_z * ends, 2)
+
+    def chain(length):
+        scaled = SCALE * viscosity * (2.0 / length) * stiffness
+        full = np.kron(np.eye(2), scaled)
+        ends_only = full[[15, 0]]
+        full[7] = full[8] = full[7] + full[8]
+        return full, ends_only
+
+    chain_x, ends_x = chain(element_dx)
+    chain_z, ends_z = chain(element_dz)
+    flat = np.kron(chain_x, np.diag(joined_z)) + np.kron(np.diag(joined_x), chain_z)
+    flat += SCALE * inverse_step * np.diag(np.kron(joined_x, joined_z))
+    faces = [np.kron(ends_x[d : d + 1], np.diag(joined_z)) for d in range(2)]
+    faces += [np.kron(np.diag(joined_x), ends_z[d : d + 1]) for d in range(2)]
+    flat = np.concatenate([flat] + faces).astype(np.float32)
+    flat_high = flat.astype(jnp.bfloat16)
+    flat_low = (flat - flat_high.astype(np.float32)).astype(jnp.bfloat16)
     pieces = [np.stack(rows), block.reshape(16, 8, 128), lift.reshape(8, 4, 128).transpose(1, 0, 2)]
-    return np.concatenate(pieces).astype(np.float32)
+    pieces += [joined_x[:, None, None] * (mass_z * ends)[None, :, None] * np.ones((16, 8, 128))]
+    return np.concatenate(pieces).astype(np.float32), np.stack([flat_high, flat_low])
 
 
 def kernel(sizes, *refs):
-    operands, refs = refs[:7], refs[7:]
+    operands, refs = refs[:8], refs[8:]
     (res, one, two, scalars, neumann), refs = refs[:5], refs[5:]
-    local, refs = refs[:7], refs[7:]
-    velocity, heights, owner, element, coords, roughness, table = local
-    (stiff, stiff_joined, slab, slab_in, plane, plane_in, face, face_in, mom, part, part_in,
+    local, refs = refs[:8], refs[8:]
+    velocity, heights, owner, element, coords, roughness, table, flat = local
+    (normal, right_high, right_low, slab, slab_in, plane, plane_in, face, face_in, mom, part, part_in,
      load, send, slab_recv, recv, ready) = refs
     nx, ny, nc, ns = sizes
     nw = nx * ny * nc
@@ -151,31 +167,39 @@
     along = {dw: beside(dw) for dw in (-1, 0, 1)}
     across = {0: sp, 1: ring(sp, 1, ns), -1: ring(sp, -1, ns)}
     neighbours = [(*along[dw], across[ds]) for dw, ds in SHIFTS]
-    over_x = lambda k: (ring(wx, k, nx), wy, wc, sp)
-    over_y = lambda k: (wx, ring(wy, k, ny), wc, sp)
-    over_z = lambda k: (wx, wy, wc, ring(sp, k, ns))
-    over_pair = lambda k: (
-        ring(wx, k // nc, nx) if k // nc else wx,
-        wy,
-        ring(wc, k % nc, nc) if k % nc else wc,
-        sp,
-    )
+    place_x = {0: wx, 1: ring(wx, 1, nx), -1: ring(wx, -1, nx), 2: ring(wx, 2, nx)}
+    place_y = {k: ring(wy, k, ny) if k else wy for k in range(-(ny // 2) + 1, ny // 2 + 1)}
+    place_y[-2] = ring(wy, -2, ny)
+    place_z = {k: ring(sp, k, ns) if k else sp for k in range(-(ns // 2) + 1, ns // 2 + 1)}
+    place_z[-2] = ring(sp, -2, ns)
+    other = ring(wc, 1, nc)
+    flat_peer = lambda dx, dy: (place_x[dx], place_y[dy], wc, sp)
+    deep_peer = lambda c, ds: (wx, wy, c, place_z[ds])
+
+    def far_first(keys):
+        return sorted(keys, key=lambda key: -abs(key[0]) - abs(key[1]))
+
+    deep = far_first([(c, k) for c in (0, 1) for k in range(-(ns // 2) + 1, ns // 2 + 1)])
+    deep = [key for key in deep if key != (0, 0)]
+    wide_x = [k for k in (-1, 0, 1, 2) if -(nx // 2) < k <= nx // 2]
+    plain = far_first([(a, b) for a in wide_x for b in range(-(ny // 2) + 1, ny // 2 + 1)])
+    plain = [key for key in plain if key != (0, 0)]
     groups = [
-        (nx * nc, wx * nc + wc, over_pair),
-        (ny, wy, over_y),
-        (ns, sp, over_z),
+        (nc * ns, wc * ns + sp, [deep_peer((wc, other)[c], k) for c, k in deep]),
+        (nx * ny, wx * ny + wy, [flat_peer(a, b) for a, b in plain]),
     ]
 
     barrier = pltpu.get_barrier_semaphore()
-    near = list(neighbours) + [over_pair(k) for k in range(nc)][1:]
-    near += [over_pair(k * nc + c) for k in (1, nx - 1) for c in range(nc)]
-    near += [over_y(1), over_y(-1)]
+    near = neighbours[:4] + [deep_peer(other, 0)]
+    near += [flat_peer(1, 0), flat_peer(-1, 0), flat_peer(0, 1), flat_peer(0, -1)]
     for peer in near:
         pl.semaphore_signal(barrier, inc=1, device_id=peer, device_id_type=MESH_ID)
     relays = [
-        [over_x(1), over_x(-1), over_y(1), over_y(-1), over_z(1), over_z(-1)],
-        [over_y(2), over_y(-2), over_z(2), over_z(-2)],
-        [over_z(2), over_z(-2)],
+        near,
+        [flat_peer(1, 0), flat_peer(-1, 0), flat_peer(0, 2), flat_peer(0, -2)]
+        + [deep_peer(wc, 2), deep_peer(wc, -2)],
+        [flat_peer(1, 0), flat_peer(-1, 0), flat_peer(0, 2), flat_peer(0, -2)]
+        + [flat_peer(2, 2), flat_peer(2, -2), deep_peer(wc, 4), deep_peer(wc, -4)],
     ]
 
     def tell(n):
@@ -210,24 +234,30 @@
         height = jnp.where(lane8 // 8 == layer, heights[layer], height)
     mass_y = height * table[HALFW]
     block = table[BLOCK : BLOCK + 16].reshape(128, 128) * (1.0 / height)[:1]
-    stiff[...] = block
-    stiff_joined[...] = (
+    block = (
         block
         + table[LAST][:1] * pltpu.roll(block, 127, 1)
         + table[FIRST][:1] * pltpu.roll(block, 1, 1)
     )
+
+    def split(value):
+        high = value.astype(jnp.bfloat16)
+        return high, (value - high.astype(jnp.float32)).astype(jnp.bfloat16)
+
+    block_high, block_low = split(block)
+    normal[:128, :128] = block_high
+    normal[128:, :128] = block_high
+    normal[:128, 128:] = block_low
+    normal[128:, 128:] = jnp.zeros((128, 128), jnp.bfloat16)
+    right_high[...] = jnp.zeros(right_high.shape, jnp.bfloat16)
+    right_low[...] = jnp.zeros(right_low.shape, jnp.bfloat16)
     joined_y = (
         mass_y
         + table[LAST] * pltpu.roll(mass_y, 127, 1)
         + table[FIRST] * pltpu.roll(mass_y, 1, 1)
     )
     both = lambda value: jnp.concatenate([value, value], axis=0)
-    mass_zy = both(table[MZ] * mass_y)
-    mass_y2 = both(mass_y)
-    mass_z2 = both(table[MZ])
     joined_y2 = both(joined_y)
-    joined_z2 = both(table[QMZ])
-    joined_zy = both(table[QMZ] * joined_y)
     count2 = both(table[COUNT])
 
     for comp in range(2):
@@ -291,7 +321,6 @@
 
     basis = [[lagrange(axes[k][g]) for k in range(3)] for g in range(4)]
     second_wall = (lane // 8) % 2 == 1
-    columns = []
     for g in range(4):
         ly = basis[g][2]
         blocks = []
@@ -301,25 +330,26 @@
                     wide(second_wall) == (side == 1), layer[g] == float(ey)
                 )
                 blocks.append(jnp.where(chosen, ly, 0.0))
-        columns.append(jnp.concatenate(blocks, axis=0))
-
-    nothing = jnp.zeros((32, 128), jnp.float32)
+        high, low = split(jnp.concatenate(blocks, axis=0))
+        for kk in range(2):
+            k = 2 * (g // 2) + kk
+            column = slice(128 * kk, 128 * kk + 128)
+            right_high[g, 32 * k : 32 * k + 32, column] = high
+            right_high[g, 128 + 32 * k : 160 + 32 * k, column] = high
+            right_low[g, 32 * k : 32 * k + 32, column] = low
+
     masks = [[1.0 - to_next[g] - to_prev[g], to_prev[g], to_next[g]] for g in range(4)]
 
     def sample(source, g):
-        ex, ez = g // 2, g % 2
-        right = [
-            jnp.concatenate(
-                [columns[g] if k == 2 * ex + kk else nothing for k in range(4)], axis=0
-            )
-            for kk in range(2)
-        ]
-        rows = source[:, :, 8 * ez : 8 * ez + 8, :].reshape(64, 128)
+        ez = g % 2
+        high, low = split(source[:, :, 8 * ez : 8 * ez + 8, :].reshape(64, 128))
+        product = jnp.dot(
+            jnp.concatenate([high, low], axis=1), right_high[g],
+            preferred_element_type=jnp.float32,
+        ) + jnp.dot(high, right_low[g], preferred_element_type=jnp.float32)
         total = [jnp.zeros((8, 128), jnp.float32) for _ in range(2)]
         for kk in range(2):
-            values = jnp.dot(
-                rows, right[kk], precision=precise, preferred_element_type=jnp.float32
-            ).reshape(2, 4, 8, 128)
+            values = product[:, 128 * kk : 128 * kk + 128].reshape(2, 4, 8, 128)
             for comp in range(2):
                 for x in range(4):
                     a = 4 * kk + x
@@ -353,9 +383,9 @@
             neumann[comp : comp + 1, 128 * q : 128 * q + 128] = slope[:1]
             plane[comp * 4 + q : comp * 4 + q + 1, :] = (viscosity * slope * table[PLANE])[:1]
 
+    hear(0)
     for d in range(8):
         push(plane, plane_in.at[d], send.at[1], recv.at[0], neighbours[d])
-    hear(0)
     tell(1)
 
     node_z = lane8 % 16
@@ -385,11 +415,12 @@
     before_line = join_span(plane_in[0], plane_in[4], plane_in[5])
     after_line = join_span(plane_in[1], plane_in[6], plane_in[7])
     stress = join_wall(own_line, before_line, after_line)
+    lift = jnp.concatenate([table[LIFT + k] for k in range(4)], axis=1)
+    stress_high = stress.astype(jnp.bfloat16).astype(jnp.float32)
     lifted = lax.dot_general(
-        stress,
-        jnp.concatenate([table[LIFT + k] for k in range(4)], axis=1),
+        jnp.concatenate([stress_high, stress - stress_high], axis=0),
+        jnp.concatenate([lift, lift], axis=0),
         (((0,), (0,)), ((), ())),
-        precision=precise,
         preferred_element_type=jnp.float32,
     )
     for comp in range(2):
@@ -398,83 +429,37 @@
             here = res[2 * comp, 128 * ex : 128 * ex + 128]
             res[2 * comp, 128 * ex : 128 * ex + 128] = here + lifted[:, column : column + 128]
 
-    cx = SCALE * viscosity * (2.0 / element_dx) * stiffness
-    even = 0.5 * (cx[:4, :4] + cx[:4, 7:3:-1])
-    odd = 0.5 * (cx[:4, :4] - cx[:4, 7:3:-1])
+    row16 = lax.broadcasted_iota(jnp.int32, (16, 128), 0) % 8
+    share_x = jnp.where(jnp.logical_or(row16 == 0, row16 == 7), 0.5, 1.0)
+    half_y = wide(table[COUNT][:1])
 
     def fold(value):
         return value[:8] + value[8:]
 
-    def spectral_x(nodes):
-        plus = [nodes[b] + nodes[7 - b] for b in range(4)]
-        minus = [nodes[b] - nodes[7 - b] for b in range(4)]
-        result = [None] * 8
-        for a in range(4):
-            sum_e = plus[0] * float(even[a, 0])
-            sum_o = minus[0] * float(odd[a, 0])
-            for b in range(1, 4):
-                sum_e = sum_e + plus[b] * float(even[a, b])
-                sum_o = sum_o + minus[b] * float(odd[a, b])
-            result[a] = sum_e + sum_o
-            result[7 - a] = sum_e - sum_o
-        return result
-
-    def spectral_z(source, comp, start):
-        halves = []
-        for h in range(2):
-            total = None
-            for b in range(8):
-                row = start + 8 * h + b
-                term = source[comp, row : row + 1] * table[KZ + b]
-                total = term if total is None else total + term
-            halves.append(total)
-        return halves
-
-    def along_y(source, comp, base, matrix):
-        return jnp.dot(
-            source[comp, base : base + 128],
-            matrix[...],
-            precision=precise,
-            preferred_element_type=jnp.float32,
-        )
+    def apply(source, comp):
+        high, low = split(source[comp])
+        parts = jnp.concatenate([high, low], axis=1)
+        along = jnp.dot(flat[0], parts, preferred_element_type=jnp.float32)
+        along = along[:, :128] + along[:, 128:]
+        along = along + jnp.dot(flat[1], high, preferred_element_type=jnp.float32)
+        across_y = jnp.dot(parts, normal[...], preferred_element_type=jnp.float32)
+        return along, across_y[:, :128] + across_y[:, 128:]
 
     def operate(source, target, turn):
         for comp in range(3):
-            seam = None
-            for ex in range(2):
-                base = 128 * ex
-                normal = along_y(source, comp, base, stiff_joined)
-                nodes = [source[comp, base + 16 * b : base + 16 * b + 16] for b in range(8)]
-                stream = [value * joined_zy for value in spectral_x(nodes)]
-                if ex == 0:
-                    face[turn, 1, comp] = stream[0]
-                    seam = stream[7]
-                else:
-                    face[turn, 0, comp] = stream[7]
-                    target[comp, 112:128] = target[comp, 112:128] + stream[0]
-                    stream[0] = stream[0] + seam
-                for a in range(8):
-                    start = base + 16 * a
-                    low, high = spectral_z(source, comp, start)
-                    i = 8 * ex + a
-                    edge = mass_x[a] * ends[a]
-                    face[turn, 3, comp, i : i + 1] = (low * joined_y)[:1] * edge
-                    face[turn, 2, comp, i : i + 1] = (high * joined_y)[7:] * edge
-                    joined = jnp.concatenate(
-                        [
-                            low + jnp.where(sub8 == 7, pltpu.roll(high, 7, 0), 0.0),
-                            high + jnp.where(sub8 == 0, pltpu.roll(low, 1, 0), 0.0),
-                        ],
-                        axis=0,
-                    )
-                    target[comp, start : start + 16] = stream[a] + edge * (
-                        joined * joined_y2 + normal[16 * a : 16 * a + 16] * joined_z2
-                    )
-        for d in range(4):
-            push(
-                face.at[turn, d], face_in.at[turn, d], send.at[2 + turn], recv.at[1 + turn],
-                neighbours[d],
-            )
+            along, across_y = apply(source, comp)
+            for d in range(4):
+                rows = slice(256 + 16 * d, 272 + 16 * d)
+                face[turn, d, comp] = along[rows] * joined_y2
+                push(
+                    face.at[turn, d, comp], face_in.at[turn, d, comp], send.at[2 + turn],
+                    recv.at[1 + turn], neighbours[d],
+                )
+            for i in range(16):
+                rows = slice(16 * i, 16 * i + 16)
+                target[comp, rows] = along[rows] * joined_y2 + across_y[rows] * both(
+                    table[FLAT + i]
+                )
 
     def receive(target, turn):
         wait_bytes(face_in.at[turn], recv.at[1 + turn])
@@ -490,19 +475,27 @@
 
     def energy(source, index):
         for comp in range(3):
-            total = jnp.zeros((16, 128), jnp.float32)
-            for ex in range(2):
-                base = 128 * ex
-                normal = along_y(source, comp, base, stiff)
-                nodes = [source[comp, base + 16 * b : base + 16 * b + 16] for b in range(8)]
-                stream = spectral_x(nodes)
-                for a in range(8):
-                    spanned = jnp.concatenate(spectral_z(source, comp, base + 16 * a), axis=0)
-                    local = stream[a] * mass_zy + mass_x[a] * (
-                        spanned * mass_y2 + normal[16 * a : 16 * a + 16] * mass_z2
-                    )
-                    total = total + local * nodes[a]
-            mom[3 * index + comp] = fold(total)
+            along, across_y = apply(source, comp)
+            inside = jnp.zeros((16, 128), jnp.float32)
+            edges = jnp.zeros((16, 128), jnp.float32)
+            for i in range(16):
+                rows = slice(16 * i, 16 * i + 16)
+                term = source[comp, rows] * (
+                    along[rows] * joined_y2 + across_y[rows] * both(table[FLAT + i])
+                )
+                if i % 8 in (0, 7):
+                    edges = edges + term
+                else:
+                    inside = inside + term
+            for d, i in ((0, 15), (1, 0)):
+                sent = along[256 + 16 * d : 272 + 16 * d] * joined_y2
+                edges = edges + sent * source[comp, 16 * i : 16 * i + 16]
+            total = fold((inside + 0.5 * edges) * count2)
+            for d, first in ((2, 15), (3, 0)):
+                sent = along[256 + 16 * d : 272 + 16 * d] * joined_y2
+                term = sent * source[comp, pl.ds(first, 16, stride=16), :]
+                total = total + fold(term * share_x) * half_y
+            mom[3 * index + comp] = total
 
     def weighted(pairs):
         for comp in range(3):
@@ -538,12 +531,12 @@
     row = jnp.sum(row, axis=0, keepdims=True)
 
     start = 0
-    for phase, (count, mine, place) in enumerate(groups):
+    for phase, (count, mine, peers) in enumerate(groups):
         part[phase] = row
-        for k in range(1, count):
+        for peer in peers:
             push(
                 part.at[phase], part_in.at[start + mine], send.at[4 + phase], recv.at[3 + phase],
-                place(k),
+                peer,
             )
         part_in[start + mine] = row
         wait_bytes(part_in.at[pl.ds(start, count - 1)], recv.at[3 + phase])
@@ -618,11 +611,11 @@
 
 def body(sizes, velocity_old, heights, owner_device, owner_element, ref_coords, roughness):
     nx, ny, nc, ns = sizes
-    slots = nx * nc + ny + ns
+    slots = nc * ns + nx * ny
     f32, i32 = jnp.float32, jnp.int32
     vmem = pl.BlockSpec(memory_space=pltpu.VMEM)
     anywhere = pl.BlockSpec(memory_space=pl.ANY)
-    constants = jnp.asarray(tables())
+    constants, flat = (jnp.asarray(value) for value in tables())
     res, one, two, scalars, slopes = pl.pallas_call(
         functools.partial(kernel, sizes),
         out_shape=(
@@ -632,7 +625,7 @@
             pltpu.VMEM((8, 128), f32),
             pltpu.VMEM((2, 512), f32),
         ),
-        in_specs=[anywhere] * 7,
+        in_specs=[anywhere] * 8,
         out_specs=(vmem,) * 5,
         scratch_shapes=[
             pltpu.VMEM((3, 16, 16, 128), f32),
@@ -642,8 +635,10 @@
             pltpu.VMEM((3, 512), f32),
             pltpu.VMEM((1, 512), f32),
             pltpu.VMEM(constants.shape, f32),
-            pltpu.VMEM((128, 128), f32),
-            pltpu.VMEM((128, 128), f32),
+            pltpu.VMEM(flat.shape, jnp.bfloat16),
+            pltpu.VMEM((256, 256), jnp.bfloat16),
+            pltpu.VMEM((4, 256, 256), jnp.bfloat16),
+            pltpu.VMEM((4, 128, 256), jnp.bfloat16),
             pltpu.VMEM((2, 4, 16, 128), f32),
             pltpu.VMEM((2, 2, 4, 16, 128), f32),
             pltpu.VMEM((8, 128), f32),
@@ -651,12 +646,12 @@
             pltpu.VMEM((2, 4, 3, 16, 128), f32),
             pltpu.VMEM((2, 4, 3, 16, 128), f32),
             pltpu.VMEM((18, 8, 128), f32),
-            pltpu.VMEM((3, 1, 128), f32),
+            pltpu.VMEM((2, 1, 128), f32),
             pltpu.VMEM((slots, 1, 128), f32),
-            pltpu.SemaphoreType.DMA((7,)),
-            pltpu.SemaphoreType.DMA((7,)),
+            pltpu.SemaphoreType.DMA((8,)),
+            pltpu.SemaphoreType.DMA((6,)),
             pltpu.SemaphoreType.DMA((2,)),
-            pltpu.SemaphoreType.DMA((6,)),
+            pltpu.SemaphoreType.DMA((5,)),
             pltpu.SemaphoreType.REGULAR((3,)),
         ],
         compiler_params=pltpu.CompilerParams(collective_id=0, has_side_effects=True),
@@ -669,6 +664,7 @@
         ref_coords,
         roughness.reshape(1, -1),
         constants,
+        flat,
     )
     return pl.pallas_call(
         combine,

time: 50.2 us -> 47.1 us (0.938); the launches traced: 49.3 us -> 46.9 us
  Pallas kernels: 48.6 us -> 46.3 us
    pallas_call x1, Pallas kernels: 47.8 us -> 45.4 us  [body(): pl.pallas_call(functools.partial(kernel, sizes), out_shape=(pltpu.VMEM((3...]
where the time goes in v4:
time: 47.1 us; the launch traced here: 46.9 us
  Pallas kernels  46.3 us (98%)
  between operations  0.64 us (1%)
    pallas_call x1, Pallas kernels, body(): pl.pallas_call(functools.partial(kernel, sizes), out_shape=(pltpu.VMEM((3...  45.4 us

profile of v4, /device:TPU:1, one launch (start us, length us, event | category | flops | bytes accessed | tf_op | source)
XLA Modules:
  0.0 46.9 jit_solution(15147928858286847099)
XLA Ops:
  0.6 45.4 %channel_step.1 = (f32[3,256,128]{2,1,0:T(8,128)S(1)}, f32[3,256,128]{2,1,0:T(8,128)S(1)}, f32[3,256,128]{2,1,0:T(8,128)S(1)}, f32[8,128]{1,0:T(8,128)S(1)}, f32[2,512]{1,0:T(2,128)S(1)}) custom-call(f32[3,16,16,128]{3,2,1,0:T(8,128)} %refs_0_.1, f32[16]{0:T(128)} %refs_1_.1, s32[1,512]{1,0:T(1,128)} %bitcast.3, s32[1,512]{1,0:T(1,128)} %bitcast.4, ...), custom_call_target="tpu_custom_call" | custom-call | tf_op jit(solution)/shard_map/channel_step/pallas_call | solution.py:619
  46.0 0.9 %combine.1 = (f32[3,16,16,128]{3,2,1,0:T(8,128)}, f32[2,512]{1,0:T(2,128)}) custom-call(f32[3,256,128]{2,1,0:T(8,128)S(1)} %get-tuple-element.7.res, f32[3,256,128]{2,1,0:T(8,128)S(1)} %get-tuple-element.8.one, f32[3,256,128]{2,1,0:T(8,128)S(1)} %get-tuple-element.9.two, f32[8,128]{1,0:T(8,128)S(1)} %get-tuple-element.10.scalars, ...), custom_call_target="tpu_custom_call" | custom-call | tf_op jit(solution)/shard_map/combine/pallas_call | solution.py:669

commit v5 on v4

--- a/solution.py
+++ b/solution.py
@@ -47,8 +47,8 @@
 
 SHIFTS = ((1, 0), (-1, 0), (0, 1), (0, -1), (1, 1), (1, -1), (-1, 1), (-1, -1))
 
-MZ, QMZ, COUNT, LAG, PLANE, HALFW, LAST, FIRST = range(8)
-BLOCK, LIFT, FLAT = 8, 24, 28
+MZ, QMZ, COUNT, LAG, PLANE, HALFW, LAST, FIRST, LANEX, LANEZ = range(10)
+BLOCK, LIFT, FLAT = 10, 26, 30
 
 
 def stiffness_table():
@@ -121,17 +121,27 @@
     flat = np.concatenate([flat] + faces).astype(np.float32)
     flat_high = flat.astype(jnp.bfloat16)
     flat_low = (flat - flat_high.astype(np.float32)).astype(jnp.bfloat16)
+    line_x = SCALE * viscosity * (2.0 / element_dx) * stiffness
+    line_z = SCALE * viscosity * (2.0 / element_dz) * stiffness
+    line = np.concatenate([np.kron(line_x.T, np.eye(16)), np.kron(np.eye(16), line_z.T)], axis=1)
+    line_high = line.astype(np.float32).astype(jnp.bfloat16)
+    line_low = (line.astype(np.float32) - line_high.astype(np.float32)).astype(jnp.bfloat16)
+    lines = np.concatenate([line_high, line_high, line_low])
+    rows += [
+        ones * (mass_x * ends)[lane // 16][None, :],
+        ones * (mass_z * ends)[lane % 8][None, :],
+    ]
     pieces = [np.stack(rows), block.reshape(16, 8, 128), lift.reshape(8, 4, 128).transpose(1, 0, 2)]
     pieces += [joined_x[:, None, None] * (mass_z * ends)[None, :, None] * np.ones((16, 8, 128))]
-    return np.concatenate(pieces).astype(np.float32), np.stack([flat_high, flat_low])
+    return np.concatenate(pieces).astype(np.float32), np.stack([flat_high, flat_low]), lines
 
 
 def kernel(sizes, *refs):
-    operands, refs = refs[:8], refs[8:]
+    operands, refs = refs[:9], refs[9:]
     (res, one, two, scalars, neumann), refs = refs[:5], refs[5:]
-    local, refs = refs[:8], refs[8:]
-    velocity, heights, owner, element, coords, roughness, table, flat = local
-    (normal, right_high, right_low, slab, slab_in, plane, plane_in, face, face_in, mom, part, part_in,
+    local, refs = refs[:9], refs[9:]
+    velocity, heights, owner, element, coords, roughness, table, flat, lines = local
+    (normal, lifting, right_high, right_low, slab, slab_in, plane, plane_in, face, face_in, mom, part, part_in,
      load, send, slab_recv, recv, ready) = refs
     nx, ny, nc, ns = sizes
     nw = nx * ny * nc
@@ -222,43 +232,11 @@
     def wait_bytes(like, sem):
         pltpu.make_async_copy(like, like, sem).wait()
 
-    for copy in loads:
-        copy.wait()
+    loads[0].wait()
 
     lane = lax.broadcasted_iota(jnp.int32, (1, 128), 1)
     sub8 = lax.broadcasted_iota(jnp.int32, (8, 128), 0)
     lane8 = lax.broadcasted_iota(jnp.int32, (8, 128), 1)
-
-    height = jnp.zeros((8, 128), jnp.float32)
-    for layer in range(16):
-        height = jnp.where(lane8 // 8 == layer, heights[layer], height)
-    mass_y = height * table[HALFW]
-    block = table[BLOCK : BLOCK + 16].reshape(128, 128) * (1.0 / height)[:1]
-    block = (
-        block
-        + table[LAST][:1] * pltpu.roll(block, 127, 1)
-        + table[FIRST][:1] * pltpu.roll(block, 1, 1)
-    )
-
-    def split(value):
-        high = value.astype(jnp.bfloat16)
-        return high, (value - high.astype(jnp.float32)).astype(jnp.bfloat16)
-
-    block_high, block_low = split(block)
-    normal[:128, :128] = block_high
-    normal[128:, :128] = block_high
-    normal[:128, 128:] = block_low
-    normal[128:, 128:] = jnp.zeros((128, 128), jnp.bfloat16)
-    right_high[...] = jnp.zeros(right_high.shape, jnp.bfloat16)
-    right_low[...] = jnp.zeros(right_low.shape, jnp.bfloat16)
-    joined_y = (
-        mass_y
-        + table[LAST] * pltpu.roll(mass_y, 127, 1)
-        + table[FIRST] * pltpu.roll(mass_y, 1, 1)
-    )
-    both = lambda value: jnp.concatenate([value, value], axis=0)
-    joined_y2 = both(joined_y)
-    count2 = both(table[COUNT])
 
     for comp in range(2):
         quarters = []
@@ -274,6 +252,55 @@
             packed = jnp.where(where_to // 16 == 2 * k + 1, high, packed)
         slab[comp] = packed.reshape(4, 16, 128)
 
+    pl.semaphore_wait(barrier, len(near))
+
+    tell(0)
+    for d in range(2):
+        push(slab, slab_in.at[d], send.at[0], slab_recv.at[d], neighbours[d])
+
+    for copy in loads[1:]:
+        copy.wait()
+    height = jnp.zeros((8, 128), jnp.float32)
+    for layer in range(16):
+        height = jnp.where(lane8 // 8 == layer, heights[layer], height)
+    mass_y = height * table[HALFW]
+    block = table[BLOCK : BLOCK + 16].reshape(128, 128) * (1.0 / height)[:1]
+    block = (
+        block
+        + table[LAST][:1] * pltpu.roll(block, 127, 1)
+        + table[FIRST][:1] * pltpu.roll(block, 1, 1)
+    )
+
+    def split(value):
+        high = value.astype(jnp.bfloat16)
+        return high, (value - high.astype(jnp.float32)).astype(jnp.bfloat16)
+
+    block_high, block_low = split(block)
+    normal[:128, :128] = block_high
+    normal[128:, :128] = block_high
+    normal[:128, 128:] = block_low
+    normal[128:, 128:] = jnp.zeros((128, 128), jnp.bfloat16)
+    right_high[...] = jnp.zeros(right_high.shape, jnp.bfloat16)
+    right_low[...] = jnp.zeros(right_low.shape, jnp.bfloat16)
+    side = sub8 // 2 % 2
+    wall_row = jnp.where(side == 0, block[:1], block[127:])
+    lift = jnp.concatenate([table[LIFT + k] for k in range(4)], axis=1)
+    home = (sub8 // 4 * 2 + sub8 % 2)[:, :1]
+    rises = jnp.concatenate([jnp.where(home == k, wall_row, 0.0) for k in range(4)], axis=1)
+    rises_high = rises.astype(jnp.bfloat16).astype(jnp.float32)
+    for n, part_of in enumerate((lift, lift, rises_high, rises_high, rises - rises_high)):
+        lifting[8 * n : 8 * n + 8] = part_of
+    lifting[40:] = jnp.zeros((8, 512), jnp.float32)
+    joined_y = (
+        mass_y
+        + table[LAST] * pltpu.roll(mass_y, 127, 1)
+        + table[FIRST] * pltpu.roll(mass_y, 1, 1)
+    )
+    both = lambda value: jnp.concatenate([value, value], axis=0)
+    joined_y2 = both(joined_y)
+    count2 = both(table[COUNT])
+
+    wall_mass = jnp.where(side == 0, joined_y[:, :1], joined_y[:, 127:])
     scale_zy = both(table[QMZ] * joined_y) * inverse_step
     for comp in range(3):
         for i in range(16):
@@ -281,6 +308,39 @@
                 scale_zy * (mass_x[i % 8] * ends[i % 8])
             )
 
+    row16 = lax.broadcasted_iota(jnp.int32, (16, 128), 0) % 8
+    share_x = jnp.where(jnp.logical_or(row16 == 0, row16 == 7), 0.5, 1.0)
+    half_y = jnp.broadcast_to(table[COUNT][:1], (8, 128))
+
+    def fold(value):
+        return value[:8] + value[8:]
+
+    def apply(source, comp):
+        high, low = split(source[comp])
+        parts = jnp.concatenate([high, low], axis=1)
+        along = jnp.dot(flat[0], parts, preferred_element_type=jnp.float32)
+        along = along[:, :128] + along[:, 128:]
+        along = along + jnp.dot(flat[1], high, preferred_element_type=jnp.float32)
+        across_y = jnp.dot(parts, normal[...], preferred_element_type=jnp.float32)
+        return along, across_y[:, :128] + across_y[:, 128:]
+
+    def operate(source, target, turn):
+        for comp in range(3):
+            along, across_y = apply(source, comp)
+            for d in range(4):
+                rows = slice(256 + 16 * d, 272 + 16 * d)
+                face[turn, d, comp] = along[rows] * joined_y2
+                push(
+                    face.at[turn, d, comp], face_in.at[turn, d, comp], send.at[2 + turn],
+                    recv.at[1 + turn], neighbours[d],
+                )
+            for i in range(16):
+                rows = slice(16 * i, 16 * i + 16)
+                target[comp, rows] = along[rows] * joined_y2 + across_y[rows] * both(
+                    table[FLAT + i]
+                )
+
+    operate(res, one, 0)
     def regroup(blocks):
         upper = (lane // 8) % 2 == 1
         result = []
@@ -312,12 +372,6 @@
         for b in range(8):
             value = value * jnp.where(sub8 == b, 1.0, coord - GLL_NODES[b])
         return value
-
-    pl.semaphore_wait(barrier, len(near))
-
-    tell(0)
-    for d in range(2):
-        push(slab, slab_in.at[d], send.at[0], slab_recv.at[d], neighbours[d])
 
     basis = [[lagrange(axes[k][g]) for k in range(3)] for g in range(4)]
     second_wall = (lane // 8) % 2 == 1
@@ -410,57 +464,6 @@
             + jnp.where(node_x == 0, pltpu.roll(earlier, 16, 1), 0.0)
         )
 
-    wait_bytes(plane_in, recv.at[0])
-    own_line = join_span(plane[...], plane_in[2], plane_in[3])
-    before_line = join_span(plane_in[0], plane_in[4], plane_in[5])
-    after_line = join_span(plane_in[1], plane_in[6], plane_in[7])
-    stress = join_wall(own_line, before_line, after_line)
-    lift = jnp.concatenate([table[LIFT + k] for k in range(4)], axis=1)
-    stress_high = stress.astype(jnp.bfloat16).astype(jnp.float32)
-    lifted = lax.dot_general(
-        jnp.concatenate([stress_high, stress - stress_high], axis=0),
-        jnp.concatenate([lift, lift], axis=0),
-        (((0,), (0,)), ((), ())),
-        preferred_element_type=jnp.float32,
-    )
-    for comp in range(2):
-        for ex in range(2):
-            column = (comp * 2 + ex) * 128
-            here = res[2 * comp, 128 * ex : 128 * ex + 128]
-            res[2 * comp, 128 * ex : 128 * ex + 128] = here + lifted[:, column : column + 128]
-
-    row16 = lax.broadcasted_iota(jnp.int32, (16, 128), 0) % 8
-    share_x = jnp.where(jnp.logical_or(row16 == 0, row16 == 7), 0.5, 1.0)
-    half_y = wide(table[COUNT][:1])
-
-    def fold(value):
-        return value[:8] + value[8:]
-
-    def apply(source, comp):
-        high, low = split(source[comp])
-        parts = jnp.concatenate([high, low], axis=1)
-        along = jnp.dot(flat[0], parts, preferred_element_type=jnp.float32)
-        along = along[:, :128] + along[:, 128:]
-        along = along + jnp.dot(flat[1], high, preferred_element_type=jnp.float32)
-        across_y = jnp.dot(parts, normal[...], preferred_element_type=jnp.float32)
-        return along, across_y[:, :128] + across_y[:, 128:]
-
-    def operate(source, target, turn):
-        for comp in range(3):
-            along, across_y = apply(source, comp)
-            for d in range(4):
-                rows = slice(256 + 16 * d, 272 + 16 * d)
-                face[turn, d, comp] = along[rows] * joined_y2
-                push(
-                    face.at[turn, d, comp], face_in.at[turn, d, comp], send.at[2 + turn],
-                    recv.at[1 + turn], neighbours[d],
-                )
-            for i in range(16):
-                rows = slice(16 * i, 16 * i + 16)
-                target[comp, rows] = along[rows] * joined_y2 + across_y[rows] * both(
-                    table[FLAT + i]
-                )
-
     def receive(target, turn):
         wait_bytes(face_in.at[turn], recv.at[1 + turn])
         into = (
@@ -472,6 +475,60 @@
         for d in range(4):
             for comp in range(3):
                 target[comp, into[d], :] = target[comp, into[d], :] + face_in[turn, d, comp]
+
+    receive(one, 0)
+    wait_bytes(plane_in, recv.at[0])
+    raw = {(-dw, -ds): plane_in[d] for d, (dw, ds) in enumerate(SHIFTS)}
+    raw[0, 0] = plane[...]
+    none = jnp.zeros((8, 128), jnp.float32)
+    line_of = {
+        (dw, ds): join_span(raw[dw, ds], raw.get((dw, ds - 1), none), raw.get((dw, ds + 1), none))
+        for dw in (-1, 0, 1)
+        for ds in (-1, 0, 1)
+    }
+    cross = ((0, 0), (-1, 0), (1, 0), (0, -1), (0, 1))
+    sums_of = [
+        join_wall(
+            line_of[dw, ds], line_of.get((dw - 1, ds), none), line_of.get((dw + 1, ds), none)
+        )
+        for dw, ds in cross
+    ]
+    stress = sums_of[0]
+    high, low = split(jnp.concatenate(sums_of + [none], axis=0))
+    pulls = jnp.dot(
+        jnp.concatenate([high, low, high], axis=1), lines[...], preferred_element_type=jnp.float32
+    )
+    in_x = [pulls[8 * n : 8 * n + 8, :128] for n in range(5)]
+    in_z = [pulls[8 * n : 8 * n + 8, 128:] for n in range(5)]
+    plane_mass = table[LANEX] * table[LANEZ] * stress
+    plane_pull = (
+        table[LANEZ] * join_wall(in_x[0], in_x[1], in_x[2])
+        + table[LANEX] * join_span(in_z[0], in_z[3], in_z[4])
+        + SCALE * inverse_step * plane_mass
+    ) * wall_mass
+    def coarse(value):
+        return value.astype(jnp.bfloat16).astype(jnp.float32)
+
+    def raised(parts, rows):
+        return lax.dot_general(
+            jnp.concatenate(parts, axis=0),
+            lifting[:rows],
+            (((0,), (0,)), ((), ())),
+            preferred_element_type=jnp.float32,
+        )
+
+    stress_high, pull_high, mass_high = coarse(stress), coarse(plane_pull), coarse(plane_mass)
+    lifted = raised([stress_high, stress - stress_high], 16)
+    lifted_one = raised(
+        [pull_high, plane_pull - pull_high, mass_high, plane_mass - mass_high, mass_high, none], 48
+    )
+    for comp in range(2):
+        for ex in range(2):
+            column = (comp * 2 + ex) * 128
+            here = res[2 * comp, 128 * ex : 128 * ex + 128]
+            res[2 * comp, 128 * ex : 128 * ex + 128] = here + lifted[:, column : column + 128]
+            here = one[2 * comp, 128 * ex : 128 * ex + 128]
+            one[2 * comp, 128 * ex : 128 * ex + 128] = here + lifted_one[:, column : column + 128]
 
     def energy(source, index):
         for comp in range(3):
@@ -513,14 +570,12 @@
             for n, (_, _, index) in enumerate(pairs):
                 mom[3 * index + comp] = fold((totals[n] + 0.5 * edges[n]) * count2)
 
-    operate(res, one, 0)
     hear(1)
     tell(2)
-    receive(one, 0)
     operate(one, two, 1)
     weighted([(res, res, 0), (res, one, 1), (one, one, 2)])
+    receive(two, 1)
     hear(2)
-    receive(two, 1)
     weighted([(one, two, 3), (two, two, 4)])
     energy(two, 5)
 
@@ -615,7 +670,7 @@
     f32, i32 = jnp.float32, jnp.int32
     vmem = pl.BlockSpec(memory_space=pltpu.VMEM)
     anywhere = pl.BlockSpec(memory_space=pl.ANY)
-    constants, flat = (jnp.asarray(value) for value in tables())
+    constants, flat, lines = (jnp.asarray(value) for value in tables())
     res, one, two, scalars, slopes = pl.pallas_call(
         functools.partial(kernel, sizes),
         out_shape=(
@@ -625,7 +680,7 @@
             pltpu.VMEM((8, 128), f32),
             pltpu.VMEM((2, 512), f32),
         ),
-        in_specs=[anywhere] * 8,
+        in_specs=[anywhere] * 9,
         out_specs=(vmem,) * 5,
         scratch_shapes=[
             pltpu.VMEM((3, 16, 16, 128), f32),
@@ -636,7 +691,9 @@
             pltpu.VMEM((1, 512), f32),
             pltpu.VMEM(constants.shape, f32),
             pltpu.VMEM(flat.shape, jnp.bfloat16),
+            pltpu.VMEM(lines.shape, jnp.bfloat16),
             pltpu.VMEM((256, 256), jnp.bfloat16),
+            pltpu.VMEM((48, 512), f32),
             pltpu.VMEM((4, 256, 256), jnp.bfloat16),
             pltpu.VMEM((4, 128, 256), jnp.bfloat16),
             pltpu.VMEM((2, 4, 16, 128), f32),
@@ -648,7 +705,7 @@
             pltpu.VMEM((18, 8, 128), f32),
             pltpu.VMEM((2, 1, 128), f32),
             pltpu.VMEM((slots, 1, 128), f32),
-            pltpu.SemaphoreType.DMA((8,)),
+            pltpu.SemaphoreType.DMA((9,)),
             pltpu.SemaphoreType.DMA((6,)),
             pltpu.SemaphoreType.DMA((2,)),
             pltpu.SemaphoreType.DMA((5,)),
@@ -665,6 +722,7 @@
         roughness.reshape(1, -1),
         constants,
         flat,
+        lines,
     )
     return pl.pallas_call(
         combine,

time: 47.1 us -> 43 us (0.913)
  Pallas kernels: 46.3 us -> 42.2 us
    pallas_call x1, Pallas kernels: 45.4 us -> 41.3 us  [body(): pl.pallas_call(functools.partial(kernel, sizes), out_shape=(pltpu.VMEM((3...]
where the time goes in v5:
time: 43 us; the launch traced here: 42.8 us
  Pallas kernels  42.2 us (98%)
  between operations  0.64 us (1%)
    pallas_call x1, Pallas kernels, body(): pl.pallas_call(functools.partial(kernel, sizes), out_shape=(pltpu.VMEM((3...  41.3 us
    pallas_call x1, Pallas kernels, body(): pl.pallas_call(combine, out_shape=(jax.ShapeDtypeStruct((3, 16, 16, 128),...  0.86 us

profile of v5, /device:TPU:1, one launch (start us, length us, event | category | flops | bytes accessed | tf_op | source)
XLA Modules:
  0.0 42.8 jit_solution(17566748474750473071)
XLA Ops:
  0.6 41.3 %channel_step.1 = (f32[3,256,128]{2,1,0:T(8,128)S(1)}, f32[3,256,128]{2,1,0:T(8,128)S(1)}, f32[3,256,128]{2,1,0:T(8,128)S(1)}, f32[8,128]{1,0:T(8,128)S(1)}, f32[2,512]{1,0:T(2,128)S(1)}) custom-call(f32[3,16,16,128]{3,2,1,0:T(8,128)} %refs_0_.1, f32[16]{0:T(128)} %refs_1_.1, s32[1,512]{1,0:T(1,128)} %bitcast.3, s32[1,512]{1,0:T(1,128)} %bitcast.4, ...), custom_call_target="tpu_custom_call" | custom-call | tf_op jit(solution)/shard_map/channel_step/pallas_call | solution.py:674
  41.9 0.9 %combine.1 = (f32[3,16,16,128]{3,2,1,0:T(8,128)}, f32[2,512]{1,0:T(2,128)}) custom-call(f32[3,256,128]{2,1,0:T(8,128)S(1)} %get-tuple-element.7.res, f32[3,256,128]{2,1,0:T(8,128)S(1)} %get-tuple-element.8.one, f32[3,256,128]{2,1,0:T(8,128)S(1)} %get-tuple-element.9.two, f32[8,128]{1,0:T(8,128)S(1)} %get-tuple-element.10.scalars, ...), custom_call_target="tpu_custom_call" | custom-call | tf_op jit(solution)/shard_map/combine/pallas_call | solution.py:727

commit v6 on v5

--- a/solution.py
+++ b/solution.py
@@ -46,6 +46,11 @@
 SCALE = 64.0
 
 SHIFTS = ((1, 0), (-1, 0), (0, 1), (0, -1), (1, 1), (1, -1), (-1, 1), (-1, -1))
+
+FAR_SHIFTS = (
+    (2, 0), (2, 1), (2, -1), (-2, 0), (-2, 1), (-2, -1),
+    (0, 2), (1, 2), (-1, 2), (0, -2), (1, -2), (-1, -2),
+)
 
 MZ, QMZ, COUNT, LAG, PLANE, HALFW, LAST, FIRST, LANEX, LANEZ = range(10)
 BLOCK, LIFT, FLAT = 10, 26, 30
@@ -141,7 +146,8 @@
     (res, one, two, scalars, neumann), refs = refs[:5], refs[5:]
     local, refs = refs[:9], refs[9:]
     velocity, heights, owner, element, coords, roughness, table, flat, lines = local
-    (normal, lifting, right_high, right_low, slab, slab_in, plane, plane_in, face, face_in, mom, part, part_in,
+    (normal, lifting, lifting_two, right_high, right_low, slab, slab_in, plane, plane_in,
+     verge, verge_in, face, face_in, mom, part, part_in,
      load, send, slab_recv, recv, ready) = refs
     nx, ny, nc, ns = sizes
     nw = nx * ny * nc
@@ -166,6 +172,10 @@
     def beside(dw):
         if dw == 0:
             return wx, wy, wc
+        sign = 1 if dw > 0 else -1
+        if abs(dw) == 2:
+            turn_y = wy == (ny - 1 if dw > 0 else 0)
+            return jnp.where(turn_y, ring(wx, sign, nx), wx), ring(wy, sign, ny), wc
         turn = wc == (nc - 1 if dw > 0 else 0)
         turn_y = jnp.logical_and(turn, wy == (ny - 1 if dw > 0 else 0))
         return (
@@ -174,9 +184,10 @@
             ring(wc, dw, nc),
         )
 
-    along = {dw: beside(dw) for dw in (-1, 0, 1)}
-    across = {0: sp, 1: ring(sp, 1, ns), -1: ring(sp, -1, ns)}
+    along = {dw: beside(dw) for dw in (-2, -1, 0, 1, 2)}
+    across = {k: ring(sp, k, ns) if k else sp for k in (-2, -1, 0, 1, 2)}
     neighbours = [(*along[dw], across[ds]) for dw, ds in SHIFTS]
+    distant = [(*along[dw], across[ds]) for dw, ds in FAR_SHIFTS]
     place_x = {0: wx, 1: ring(wx, 1, nx), -1: ring(wx, -1, nx), 2: ring(wx, 2, nx)}
     place_y = {k: ring(wy, k, ny) if k else wy for k in range(-(ny // 2) + 1, ny // 2 + 1)}
     place_y[-2] = ring(wy, -2, ny)
@@ -201,6 +212,7 @@
 
     barrier = pltpu.get_barrier_semaphore()
     near = neighbours[:4] + [deep_peer(other, 0)]
+    near += [(*along[2], sp), (*along[-2], sp), (*along[0], across[2]), (*along[0], across[-2])]
     near += [flat_peer(1, 0), flat_peer(-1, 0), flat_peer(0, 1), flat_peer(0, -1)]
     for peer in near:
         pl.semaphore_signal(barrier, inc=1, device_id=peer, device_id_type=MESH_ID)
@@ -286,11 +298,6 @@
     wall_row = jnp.where(side == 0, block[:1], block[127:])
     lift = jnp.concatenate([table[LIFT + k] for k in range(4)], axis=1)
     home = (sub8 // 4 * 2 + sub8 % 2)[:, :1]
-    rises = jnp.concatenate([jnp.where(home == k, wall_row, 0.0) for k in range(4)], axis=1)
-    rises_high = rises.astype(jnp.bfloat16).astype(jnp.float32)
-    for n, part_of in enumerate((lift, lift, rises_high, rises_high, rises - rises_high)):
-        lifting[8 * n : 8 * n + 8] = part_of
-    lifting[40:] = jnp.zeros((8, 512), jnp.float32)
     joined_y = (
         mass_y
         + table[LAST] * pltpu.roll(mass_y, 127, 1)
@@ -300,6 +307,28 @@
     joined_y2 = both(joined_y)
     count2 = both(table[COUNT])
 
+    def at_home(value):
+        return jnp.concatenate([jnp.where(home == k, value, 0.0) for k in range(4)], axis=1)
+
+    def coarse(value):
+        return value.astype(jnp.bfloat16).astype(jnp.float32)
+
+    twice = jnp.dot(wall_row, block, precision=precise, preferred_element_type=jnp.float32)
+    pieces, pieces_two = [lift, lift], [lift, lift]
+    for n, value in enumerate((wall_row, joined_y * wall_row, wall_row, twice)):
+        rises = at_home(value)
+        high = coarse(rises)
+        triple = [high, high, rises - high]
+        if n == 0:
+            pieces += triple
+        else:
+            pieces_two += triple
+    for n, value in enumerate(pieces):
+        lifting[8 * n : 8 * n + 8] = value
+    lifting[40:] = jnp.zeros((8, 512), jnp.float32)
+    for n, value in enumerate(pieces_two):
+        lifting_two[8 * n : 8 * n + 8] = value
+    lifting_two[88:] = jnp.zeros((8, 512), jnp.float32)
     wall_mass = jnp.where(side == 0, joined_y[:, :1], joined_y[:, 127:])
     scale_zy = both(table[QMZ] * joined_y) * inverse_step
     for comp in range(3):
@@ -437,7 +466,26 @@
             neumann[comp : comp + 1, 128 * q : 128 * q + 128] = slope[:1]
             plane[comp * 4 + q : comp * 4 + q + 1, :] = (viscosity * slope * table[PLANE])[:1]
 
+    mine = plane[...]
+    lines_x = jnp.zeros((8, 128), jnp.float32)
+    for q in range(4):
+        here = jnp.logical_and(sub8 == 2 * q + 1, lane8 // 16 == 3 - q)
+        lines_x = jnp.where(here, pltpu.roll(mine, (16 * (3 - q) - 112) % 128, 1), lines_x)
+        here = jnp.logical_and(sub8 == 2 * q, lane8 // 16 == 7 - q)
+        lines_x = jnp.where(here, pltpu.roll(mine, (64 + 16 * (3 - q)) % 128, 1), lines_x)
+    lines_z = jnp.zeros((8, 128), jnp.float32)
+    for r in range(8):
+        here = jnp.logical_and(sub8 == r, lane8 % 16 == 7 - r)
+        lines_z = jnp.where(here, pltpu.roll(mine, (7 - r - 15) % 128, 1), lines_z)
+        here = jnp.logical_and(sub8 == r, lane8 % 16 == 15 - r)
+        lines_z = jnp.where(here, pltpu.roll(mine, (15 - r) % 128, 1), lines_z)
+    verge[0] = jnp.sum(lines_x, axis=0, keepdims=True)
+    verge[1] = jnp.sum(lines_z, axis=0, keepdims=True)
     hear(0)
+    for d, (dw, ds) in enumerate(FAR_SHIFTS):
+        push(
+            verge.at[0 if abs(dw) == 2 else 1], verge_in.at[d], send.at[6], recv.at[5], distant[d]
+        )
     for d in range(8):
         push(plane, plane_in.at[d], send.at[1], recv.at[0], neighbours[d])
     tell(1)
@@ -477,58 +525,103 @@
                 target[comp, into[d], :] = target[comp, into[d], :] + face_in[turn, d, comp]
 
     receive(one, 0)
+    operate(one, two, 1)
+    hear(1)
+    tell(2)
     wait_bytes(plane_in, recv.at[0])
+    wait_bytes(verge_in, recv.at[5])
     raw = {(-dw, -ds): plane_in[d] for d, (dw, ds) in enumerate(SHIFTS)}
     raw[0, 0] = plane[...]
+    for d, (dw, ds) in enumerate(FAR_SHIFTS):
+        row = wide(verge_in[d])
+        if abs(dw) == 2:
+            value = pltpu.roll(row, 56 if dw > 0 else 16, 1, stride=8, stride_axis=0)
+        else:
+            value = pltpu.roll(row, 8 if ds > 0 else 113, 1, stride=1, stride_axis=0)
+        raw[-dw, -ds] = value
     none = jnp.zeros((8, 128), jnp.float32)
-    line_of = {
-        (dw, ds): join_span(raw[dw, ds], raw.get((dw, ds - 1), none), raw.get((dw, ds + 1), none))
-        for dw in (-1, 0, 1)
-        for ds in (-1, 0, 1)
-    }
-    cross = ((0, 0), (-1, 0), (1, 0), (0, -1), (0, 1))
-    sums_of = [
-        join_wall(
-            line_of[dw, ds], line_of.get((dw - 1, ds), none), line_of.get((dw + 1, ds), none)
-        )
-        for dw, ds in cross
-    ]
-    stress = sums_of[0]
-    high, low = split(jnp.concatenate(sums_of + [none], axis=0))
-    pulls = jnp.dot(
-        jnp.concatenate([high, low, high], axis=1), lines[...], preferred_element_type=jnp.float32
-    )
-    in_x = [pulls[8 * n : 8 * n + 8, :128] for n in range(5)]
-    in_z = [pulls[8 * n : 8 * n + 8, 128:] for n in range(5)]
-    plane_mass = table[LANEX] * table[LANEZ] * stress
-    plane_pull = (
-        table[LANEZ] * join_wall(in_x[0], in_x[1], in_x[2])
-        + table[LANEX] * join_span(in_z[0], in_z[3], in_z[4])
-        + SCALE * inverse_step * plane_mass
-    ) * wall_mass
-    def coarse(value):
-        return value.astype(jnp.bfloat16).astype(jnp.float32)
-
-    def raised(parts, rows):
+    square = [(dw, ds) for dw in (-1, 0, 1) for ds in (-1, 0, 1)]
+    cross = [(0, 0), (-1, 0), (1, 0), (0, -1), (0, 1)]
+
+    def spans(values, at):
+        dw, ds = at
+        return join_span(
+            values[at], values.get((dw, ds - 1), none), values.get((dw, ds + 1), none)
+        )
+
+    def walls(values, at):
+        dw, ds = at
+        return join_wall(
+            values[at], values.get((dw - 1, ds), none), values.get((dw + 1, ds), none)
+        )
+
+    def pulled(values):
+        fill = [none] * (len(values) % 2)
+        high, low = split(jnp.concatenate(list(values) + fill, axis=0))
+        product = jnp.dot(
+            jnp.concatenate([high, low, high], axis=1),
+            lines[...],
+            preferred_element_type=jnp.float32,
+        )
+        return [
+            (product[8 * n : 8 * n + 8, :128], product[8 * n : 8 * n + 8, 128:])
+            for n in range(len(values))
+        ]
+
+    mass_flat = table[LANEX] * table[LANEZ]
+
+    def plane_operator(in_x, in_z, value, at):
+        return (
+            table[LANEZ] * walls(in_x, at)
+            + table[LANEX] * spans(in_z, at)
+            + (SCALE * inverse_step) * mass_flat * value
+        )
+
+    line_of = {at: spans(raw, at) for at in square + [(-2, 0), (2, 0)]}
+    stress = {at: walls(line_of, at) for at in square}
+    pulls = pulled([stress[at] for at in square])
+    in_x = {at: pulls[n][0] for n, at in enumerate(square)}
+    in_z = {at: pulls[n][1] for n, at in enumerate(square)}
+    first = {at: plane_operator(in_x, in_z, stress[at], at) for at in cross}
+    mass_of = {at: mass_flat * stress[at] for at in cross}
+    pulls = pulled([first[at] for at in cross] + [mass_of[at] for at in cross])
+    seconds = []
+    for offset, values in ((0, first), (5, mass_of)):
+        in_x = {at: pulls[offset + n][0] for n, at in enumerate(cross)}
+        in_z = {at: pulls[offset + n][1] for n, at in enumerate(cross)}
+        seconds.append(plane_operator(in_x, in_z, values[0, 0], (0, 0)))
+
+    def raised(doubles, triples, rights, rows):
+        parts = []
+        for value in doubles:
+            parts += [coarse(value), value - coarse(value)]
+        for value in triples:
+            parts += [coarse(value), value - coarse(value), coarse(value)]
+        parts += [none] * (rows // 8 - len(parts))
         return lax.dot_general(
             jnp.concatenate(parts, axis=0),
-            lifting[:rows],
+            rights[:rows],
             (((0,), (0,)), ((), ())),
             preferred_element_type=jnp.float32,
         )
 
-    stress_high, pull_high, mass_high = coarse(stress), coarse(plane_pull), coarse(plane_mass)
-    lifted = raised([stress_high, stress - stress_high], 16)
-    lifted_one = raised(
-        [pull_high, plane_pull - pull_high, mass_high, plane_mass - mass_high, mass_high, none], 48
+    here, pull, mass_here = stress[0, 0], first[0, 0] * wall_mass, mass_of[0, 0]
+    lifted = raised([here], [], lifting, 16)
+    lifted_one = raised([pull], [mass_here], lifting, 48)
+    lifted_two = raised(
+        [seconds[0] * wall_mass * wall_mass],
+        [seconds[1], mass_flat * pull, mass_flat * mass_here],
+        lifting_two,
+        96,
     )
+    receive(two, 1)
+    hear(2)
     for comp in range(2):
         for ex in range(2):
             column = (comp * 2 + ex) * 128
-            here = res[2 * comp, 128 * ex : 128 * ex + 128]
-            res[2 * comp, 128 * ex : 128 * ex + 128] = here + lifted[:, column : column + 128]
-            here = one[2 * comp, 128 * ex : 128 * ex + 128]
-            one[2 * comp, 128 * ex : 128 * ex + 128] = here + lifted_one[:, column : column + 128]
+            rows = slice(128 * ex, 128 * ex + 128)
+            for target, value in ((res, lifted), (one, lifted_one), (two, lifted_two)):
+                target[2 * comp, rows] = target[2 * comp, rows] + value[:, column : column + 128]
 
     def energy(source, index):
         for comp in range(3):
@@ -570,13 +663,7 @@
             for n, (_, _, index) in enumerate(pairs):
                 mom[3 * index + comp] = fold((totals[n] + 0.5 * edges[n]) * count2)
 
-    hear(1)
-    tell(2)
-    operate(one, two, 1)
-    weighted([(res, res, 0), (res, one, 1), (one, one, 2)])
-    receive(two, 1)
-    hear(2)
-    weighted([(one, two, 3), (two, two, 4)])
+    weighted([(res, res, 0), (res, one, 1), (one, one, 2), (one, two, 3), (two, two, 4)])
     energy(two, 5)
 
     row = jnp.zeros((8, 128), jnp.float32)
@@ -637,6 +724,7 @@
         scalars[i : i + 1, :] = value[:1] * SCALE
     wait_bytes(slab_in, send.at[0])
     wait_bytes(plane_in, send.at[1])
+    wait_bytes(verge_in, send.at[6])
     for turn in range(2):
         wait_bytes(face_in.at[turn], send.at[2 + turn])
     start = 0
@@ -694,21 +782,24 @@
             pltpu.VMEM(lines.shape, jnp.bfloat16),
             pltpu.VMEM((256, 256), jnp.bfloat16),
             pltpu.VMEM((48, 512), f32),
+            pltpu.VMEM((96, 512), f32),
             pltpu.VMEM((4, 256, 256), jnp.bfloat16),
             pltpu.VMEM((4, 128, 256), jnp.bfloat16),
             pltpu.VMEM((2, 4, 16, 128), f32),
             pltpu.VMEM((2, 2, 4, 16, 128), f32),
             pltpu.VMEM((8, 128), f32),
             pltpu.VMEM((8, 8, 128), f32),
+            pltpu.VMEM((2, 1, 128), f32),
+            pltpu.VMEM((12, 1, 128), f32),
             pltpu.VMEM((2, 4, 3, 16, 128), f32),
             pltpu.VMEM((2, 4, 3, 16, 128), f32),
             pltpu.VMEM((18, 8, 128), f32),
             pltpu.VMEM((2, 1, 128), f32),
             pltpu.VMEM((slots, 1, 128), f32),
             pltpu.SemaphoreType.DMA((9,)),
+            pltpu.SemaphoreType.DMA((7,)),
+            pltpu.SemaphoreType.DMA((2,)),
             pltpu.SemaphoreType.DMA((6,)),
-            pltpu.SemaphoreType.DMA((2,)),
-            pltpu.SemaphoreType.DMA((5,)),
             pltpu.SemaphoreType.REGULAR((3,)),
         ],
         compiler_params=pltpu.CompilerParams(collective_id=0, has_side_effects=True),

time: 43 us -> 40.8 us (0.949)
  Pallas kernels: 42.2 us -> 40 us
    pallas_call x1, Pallas kernels: 41.3 us -> 39.2 us  [body(): pl.pallas_call(functools.partial(kernel, sizes), out_shape=(pltpu.VMEM((3...]
where the time goes in v6:
time: 40.8 us; the launch traced here: 40.7 us
  Pallas kernels  40 us (98%)
  between operations  0.64 us (2%)
    pallas_call x1, Pallas kernels, body(): pl.pallas_call(functools.partial(kernel, sizes), out_shape=(pltpu.VMEM((3...  39.2 us
    pallas_call x1, Pallas kernels, body(): pl.pallas_call(combine, out_shape=(jax.ShapeDtypeStruct((3, 16, 16, 128),...  0.86 us

profile of v6, /device:TPU:1, one launch (start us, length us, event | category | flops | bytes accessed | tf_op | source)
XLA Modules:
  0.0 40.7 jit_solution(15333661770421942317)
XLA Ops:
  0.6 39.2 %channel_step.1 = (f32[3,256,128]{2,1,0:T(8,128)S(1)}, f32[3,256,128]{2,1,0:T(8,128)S(1)}, f32[3,256,128]{2,1,0:T(8,128)S(1)}, f32[8,128]{1,0:T(8,128)S(1)}, f32[2,512]{1,0:T(2,128)S(1)}) custom-call(f32[3,16,16,128]{3,2,1,0:T(8,128)} %refs_0_.1, f32[16]{0:T(128)} %refs_1_.1, s32[1,512]{1,0:T(1,128)} %bitcast.3, s32[1,512]{1,0:T(1,128)} %bitcast.4, ...), custom_call_target="tpu_custom_call" | custom-call | tf_op jit(solution)/shard_map/channel_step/pallas_call | solution.py:762
  39.8 0.9 %combine.1 = (f32[3,16,16,128]{3,2,1,0:T(8,128)}, f32[2,512]{1,0:T(2,128)}) custom-call(f32[3,256,128]{2,1,0:T(8,128)S(1)} %get-tuple-element.7.res, f32[3,256,128]{2,1,0:T(8,128)S(1)} %get-tuple-element.8.one, f32[3,256,128]{2,1,0:T(8,128)S(1)} %get-tuple-element.9.two, f32[8,128]{1,0:T(8,128)S(1)} %get-tuple-element.10.scalars, ...), custom_call_target="tpu_custom_call" | custom-call | tf_op jit(solution)/shard_map/combine/pallas_call | solution.py:818

commit v7 on v6

--- a/solution.py
+++ b/solution.py
@@ -200,15 +200,10 @@
     def far_first(keys):
         return sorted(keys, key=lambda key: -abs(key[0]) - abs(key[1]))
 
-    deep = far_first([(c, k) for c in (0, 1) for k in range(-(ns // 2) + 1, ns // 2 + 1)])
-    deep = [key for key in deep if key != (0, 0)]
+    deep_shifts = range(-(ns // 2) + 1, ns // 2 + 1)
     wide_x = [k for k in (-1, 0, 1, 2) if -(nx // 2) < k <= nx // 2]
     plain = far_first([(a, b) for a in wide_x for b in range(-(ny // 2) + 1, ny // 2 + 1)])
     plain = [key for key in plain if key != (0, 0)]
-    groups = [
-        (nc * ns, wc * ns + sp, [deep_peer((wc, other)[c], k) for c, k in deep]),
-        (nx * ny, wx * ny + wy, [flat_peer(a, b) for a, b in plain]),
-    ]
 
     barrier = pltpu.get_barrier_semaphore()
     near = neighbours[:4] + [deep_peer(other, 0)]
@@ -443,6 +438,8 @@
     for g in range(4):
         own = sample(slab, g)
         sums.append([own[comp] * masks[g][0] for comp in range(2)])
+    hear(0)
+    tell(1)
     for d in range(2):
         wait_bytes(slab_in.at[d], slab_recv.at[d])
         for g in range(4):
@@ -481,14 +478,12 @@
         lines_z = jnp.where(here, pltpu.roll(mine, (15 - r) % 128, 1), lines_z)
     verge[0] = jnp.sum(lines_x, axis=0, keepdims=True)
     verge[1] = jnp.sum(lines_z, axis=0, keepdims=True)
-    hear(0)
     for d, (dw, ds) in enumerate(FAR_SHIFTS):
         push(
             verge.at[0 if abs(dw) == 2 else 1], verge_in.at[d], send.at[6], recv.at[5], distant[d]
         )
     for d in range(8):
         push(plane, plane_in.at[d], send.at[1], recv.at[0], neighbours[d])
-    tell(1)
 
     node_z = lane8 % 16
     node_x = lane8 // 16
@@ -524,10 +519,10 @@
             for comp in range(3):
                 target[comp, into[d], :] = target[comp, into[d], :] + face_in[turn, d, comp]
 
+    hear(1)
+    tell(2)
     receive(one, 0)
     operate(one, two, 1)
-    hear(1)
-    tell(2)
     wait_bytes(plane_in, recv.at[0])
     wait_bytes(verge_in, recv.at[5])
     raw = {(-dw, -ds): plane_in[d] for d, (dw, ds) in enumerate(SHIFTS)}
@@ -615,13 +610,15 @@
         96,
     )
     receive(two, 1)
-    hear(2)
     for comp in range(2):
         for ex in range(2):
             column = (comp * 2 + ex) * 128
             rows = slice(128 * ex, 128 * ex + 128)
             for target, value in ((res, lifted), (one, lifted_one), (two, lifted_two)):
                 target[2 * comp, rows] = target[2 * comp, rows] + value[:, column : column + 128]
+
+    def note(k, value):
+        mom[k : k + 1, :] = jnp.sum(value, axis=0, keepdims=True)
 
     def energy(source, index):
         for comp in range(3):
@@ -645,7 +642,7 @@
                 sent = along[256 + 16 * d : 272 + 16 * d] * joined_y2
                 term = sent * source[comp, pl.ds(first, 16, stride=16), :]
                 total = total + fold(term * share_x) * half_y
-            mom[3 * index + comp] = total
+            note(3 * index + comp, total)
 
     def weighted(pairs):
         for comp in range(3):
@@ -661,31 +658,57 @@
                     else:
                         totals[n] = totals[n] + term
             for n, (_, _, index) in enumerate(pairs):
-                mom[3 * index + comp] = fold((totals[n] + 0.5 * edges[n]) * count2)
+                note(3 * index + comp, fold((totals[n] + 0.5 * edges[n]) * count2))
 
     weighted([(res, res, 0), (res, one, 1), (one, one, 2), (one, two, 3), (two, two, 4)])
     energy(two, 5)
 
+    mom[18:24, :] = jnp.zeros((6, 128), jnp.float32)
+    total = jnp.sum(mom[...], axis=1, keepdims=True)
     row = jnp.zeros((8, 128), jnp.float32)
-    for k in range(18):
-        value = jnp.sum(mom[k], axis=1, keepdims=True)
-        row = row + jnp.where(lane8 == k, value, 0.0)
-    row = jnp.sum(row, axis=0, keepdims=True)
-
-    start = 0
-    for phase, (count, mine, peers) in enumerate(groups):
-        part[phase] = row
-        for peer in peers:
+    for k in range(3):
+        row = row + jnp.where(lane8 == 8 * k + sub8, total[8 * k : 8 * k + 8], 0.0)
+    part[0] = jnp.sum(row, axis=0, keepdims=True)
+    hear(2)
+    line_slots, plane_slots = nc * ns, nx * ny
+    for ds in sorted(deep_shifts, key=lambda k: -abs(k)):
+        if ds:
             push(
-                part.at[phase], part_in.at[start + mine], send.at[4 + phase], recv.at[3 + phase],
-                peer,
+                part.at[0], part_in.at[wc * ns + sp], send.at[4], recv.at[3], deep_peer(1, ds)
             )
-        part_in[start + mine] = row
-        wait_bytes(part_in.at[pl.ds(start, count - 1)], recv.at[3 + phase])
-        row = part_in[start]
-        for k in range(1, count):
-            row = row + part_in[start + k]
-        start += count
+    relays_sums = wc == 1
+
+    @pl.when(jnp.logical_not(relays_sums))
+    def _():
+        push(part.at[0], part_in.at[wc * ns + sp], send.at[4], recv.at[3], deep_peer(1, 0))
+        wait_bytes(part_in.at[pl.ds(line_slots, plane_slots)], recv.at[4])
+        wait_bytes(part_in.at[pl.ds(0, ns)], send.at[4])
+
+    @pl.when(relays_sums)
+    def _():
+        part_in[wc * ns + sp] = part[0]
+        wait_bytes(part_in.at[pl.ds(0, line_slots - 1)], recv.at[3])
+        row = part_in[0]
+        for k in range(1, line_slots):
+            row = row + part_in[k]
+        part[1] = row
+        slot = line_slots + wx * ny + wy
+        for a, b in plain:
+            for c in (0, 1):
+                push(
+                    part.at[1], part_in.at[slot], send.at[5 if c else 7], recv.at[4],
+                    (place_x[a], place_y[b], c, sp),
+                )
+        push(part.at[1], part_in.at[slot], send.at[7], recv.at[4], (wx, wy, 0, sp))
+        part_in[slot] = row
+        wait_bytes(part_in.at[pl.ds(line_slots, plane_slots - 1)], recv.at[4])
+        wait_bytes(part_in.at[pl.ds(0, ns - 1)], send.at[4])
+        wait_bytes(part_in.at[pl.ds(line_slots, plane_slots - 1)], send.at[5])
+        wait_bytes(part_in.at[pl.ds(line_slots, plane_slots)], send.at[7])
+
+    row = part_in[line_slots]
+    for k in range(1, plane_slots):
+        row = row + part_in[line_slots + k]
 
     row = jnp.broadcast_to(row, (8, 128))
     moments = [row if j == 0 else pltpu.roll(row, 128 - 3 * j, 1) for j in range(6)]
@@ -727,10 +750,6 @@
     wait_bytes(verge_in, send.at[6])
     for turn in range(2):
         wait_bytes(face_in.at[turn], send.at[2 + turn])
-    start = 0
-    for phase, (count, _, _) in enumerate(groups):
-        wait_bytes(part_in.at[pl.ds(start, count - 1)], send.at[4 + phase])
-        start += count
 
 
 def combine(res, one, two, scalars, slopes, out, neumann, sums, sent):
@@ -793,11 +812,11 @@
             pltpu.VMEM((12, 1, 128), f32),
             pltpu.VMEM((2, 4, 3, 16, 128), f32),
             pltpu.VMEM((2, 4, 3, 16, 128), f32),
-            pltpu.VMEM((18, 8, 128), f32),
+            pltpu.VMEM((24, 128), f32),
             pltpu.VMEM((2, 1, 128), f32),
             pltpu.VMEM((slots, 1, 128), f32),
             pltpu.SemaphoreType.DMA((9,)),
-            pltpu.SemaphoreType.DMA((7,)),
+            pltpu.SemaphoreType.DMA((8,)),
             pltpu.SemaphoreType.DMA((2,)),
             pltpu.SemaphoreType.DMA((6,)),
             pltpu.SemaphoreType.REGULAR((3,)),

time: 40.8 us -> 40.8 us (level)
  no operation moved by 1% of the time
where the time goes in v7:
time: 40.8 us; the launch traced here: 40.7 us
  Pallas kernels  40 us (98%)
  between operations  0.64 us (2%)
    pallas_call x1, Pallas kernels, body(): pl.pallas_call(functools.partial(kernel, sizes), out_shape=(pltpu.VMEM((3...  39.2 us
    pallas_call x1, Pallas kernels, body(): pl.pallas_call(combine, out_shape=(jax.ShapeDtypeStruct((3, 16, 16, 128),...  0.86 us

profile of v7, /device:TPU:1, one launch (start us, length us, event | category | flops | bytes accessed | tf_op | source)
XLA Modules:
  0.0 40.7 jit_solution(3135609430164904231)
XLA Ops:
  0.6 39.2 %channel_step.1 = (f32[3,256,128]{2,1,0:T(8,128)S(1)}, f32[3,256,128]{2,1,0:T(8,128)S(1)}, f32[3,256,128]{2,1,0:T(8,128)S(1)}, f32[8,128]{1,0:T(8,128)S(1)}, f32[2,512]{1,0:T(2,128)S(1)}) custom-call(f32[3,16,16,128]{3,2,1,0:T(8,128)} %refs_0_.1, f32[16]{0:T(128)} %refs_1_.1, s32[1,512]{1,0:T(1,128)} %bitcast.3, s32[1,512]{1,0:T(1,128)} %bitcast.4, ...), custom_call_target="tpu_custom_call" | custom-call | tf_op jit(solution)/shard_map/channel_step/pallas_call | solution.py:781
  39.8 0.9 %combine.1 = (f32[3,16,16,128]{3,2,1,0:T(8,128)}, f32[2,512]{1,0:T(2,128)}) custom-call(f32[3,256,128]{2,1,0:T(8,128)S(1)} %get-tuple-element.7.res, f32[3,256,128]{2,1,0:T(8,128)S(1)} %get-tuple-element.8.one, f32[3,256,128]{2,1,0:T(8,128)S(1)} %get-tuple-element.9.two, f32[8,128]{1,0:T(8,128)S(1)} %get-tuple-element.10.scalars, ...), custom_call_target="tpu_custom_call" | custom-call | tf_op jit(solution)/shard_map/combine/pallas_call | solution.py:837

commit v8 on v7

--- a/solution.py
+++ b/solution.py
@@ -438,8 +438,6 @@
     for g in range(4):
         own = sample(slab, g)
         sums.append([own[comp] * masks[g][0] for comp in range(2)])
-    hear(0)
-    tell(1)
     for d in range(2):
         wait_bytes(slab_in.at[d], slab_recv.at[d])
         for g in range(4):
@@ -478,12 +476,14 @@
         lines_z = jnp.where(here, pltpu.roll(mine, (15 - r) % 128, 1), lines_z)
     verge[0] = jnp.sum(lines_x, axis=0, keepdims=True)
     verge[1] = jnp.sum(lines_z, axis=0, keepdims=True)
+    hear(0)
     for d, (dw, ds) in enumerate(FAR_SHIFTS):
         push(
             verge.at[0 if abs(dw) == 2 else 1], verge_in.at[d], send.at[6], recv.at[5], distant[d]
         )
     for d in range(8):
         push(plane, plane_in.at[d], send.at[1], recv.at[0], neighbours[d])
+    tell(1)
 
     node_z = lane8 % 16
     node_x = lane8 // 16
@@ -519,109 +519,11 @@
             for comp in range(3):
                 target[comp, into[d], :] = target[comp, into[d], :] + face_in[turn, d, comp]
 
-    hear(1)
-    tell(2)
-    receive(one, 0)
-    operate(one, two, 1)
-    wait_bytes(plane_in, recv.at[0])
-    wait_bytes(verge_in, recv.at[5])
-    raw = {(-dw, -ds): plane_in[d] for d, (dw, ds) in enumerate(SHIFTS)}
-    raw[0, 0] = plane[...]
-    for d, (dw, ds) in enumerate(FAR_SHIFTS):
-        row = wide(verge_in[d])
-        if abs(dw) == 2:
-            value = pltpu.roll(row, 56 if dw > 0 else 16, 1, stride=8, stride_axis=0)
-        else:
-            value = pltpu.roll(row, 8 if ds > 0 else 113, 1, stride=1, stride_axis=0)
-        raw[-dw, -ds] = value
-    none = jnp.zeros((8, 128), jnp.float32)
-    square = [(dw, ds) for dw in (-1, 0, 1) for ds in (-1, 0, 1)]
-    cross = [(0, 0), (-1, 0), (1, 0), (0, -1), (0, 1)]
-
-    def spans(values, at):
-        dw, ds = at
-        return join_span(
-            values[at], values.get((dw, ds - 1), none), values.get((dw, ds + 1), none)
-        )
-
-    def walls(values, at):
-        dw, ds = at
-        return join_wall(
-            values[at], values.get((dw - 1, ds), none), values.get((dw + 1, ds), none)
-        )
-
-    def pulled(values):
-        fill = [none] * (len(values) % 2)
-        high, low = split(jnp.concatenate(list(values) + fill, axis=0))
-        product = jnp.dot(
-            jnp.concatenate([high, low, high], axis=1),
-            lines[...],
-            preferred_element_type=jnp.float32,
-        )
-        return [
-            (product[8 * n : 8 * n + 8, :128], product[8 * n : 8 * n + 8, 128:])
-            for n in range(len(values))
-        ]
-
-    mass_flat = table[LANEX] * table[LANEZ]
-
-    def plane_operator(in_x, in_z, value, at):
-        return (
-            table[LANEZ] * walls(in_x, at)
-            + table[LANEX] * spans(in_z, at)
-            + (SCALE * inverse_step) * mass_flat * value
-        )
-
-    line_of = {at: spans(raw, at) for at in square + [(-2, 0), (2, 0)]}
-    stress = {at: walls(line_of, at) for at in square}
-    pulls = pulled([stress[at] for at in square])
-    in_x = {at: pulls[n][0] for n, at in enumerate(square)}
-    in_z = {at: pulls[n][1] for n, at in enumerate(square)}
-    first = {at: plane_operator(in_x, in_z, stress[at], at) for at in cross}
-    mass_of = {at: mass_flat * stress[at] for at in cross}
-    pulls = pulled([first[at] for at in cross] + [mass_of[at] for at in cross])
-    seconds = []
-    for offset, values in ((0, first), (5, mass_of)):
-        in_x = {at: pulls[offset + n][0] for n, at in enumerate(cross)}
-        in_z = {at: pulls[offset + n][1] for n, at in enumerate(cross)}
-        seconds.append(plane_operator(in_x, in_z, values[0, 0], (0, 0)))
-
-    def raised(doubles, triples, rights, rows):
-        parts = []
-        for value in doubles:
-            parts += [coarse(value), value - coarse(value)]
-        for value in triples:
-            parts += [coarse(value), value - coarse(value), coarse(value)]
-        parts += [none] * (rows // 8 - len(parts))
-        return lax.dot_general(
-            jnp.concatenate(parts, axis=0),
-            rights[:rows],
-            (((0,), (0,)), ((), ())),
-            preferred_element_type=jnp.float32,
-        )
-
-    here, pull, mass_here = stress[0, 0], first[0, 0] * wall_mass, mass_of[0, 0]
-    lifted = raised([here], [], lifting, 16)
-    lifted_one = raised([pull], [mass_here], lifting, 48)
-    lifted_two = raised(
-        [seconds[0] * wall_mass * wall_mass],
-        [seconds[1], mass_flat * pull, mass_flat * mass_here],
-        lifting_two,
-        96,
-    )
-    receive(two, 1)
-    for comp in range(2):
-        for ex in range(2):
-            column = (comp * 2 + ex) * 128
-            rows = slice(128 * ex, 128 * ex + 128)
-            for target, value in ((res, lifted), (one, lifted_one), (two, lifted_two)):
-                target[2 * comp, rows] = target[2 * comp, rows] + value[:, column : column + 128]
-
     def note(k, value):
         mom[k : k + 1, :] = jnp.sum(value, axis=0, keepdims=True)
 
-    def energy(source, index):
-        for comp in range(3):
+    def energy(source, index, comps):
+        for comp in comps:
             along, across_y = apply(source, comp)
             inside = jnp.zeros((16, 128), jnp.float32)
             edges = jnp.zeros((16, 128), jnp.float32)
@@ -644,8 +546,8 @@
                 total = total + fold(term * share_x) * half_y
             note(3 * index + comp, total)
 
-    def weighted(pairs):
-        for comp in range(3):
+    def weighted(pairs, comps):
+        for comp in comps:
             totals = [jnp.zeros((16, 128), jnp.float32) for _ in pairs]
             edges = [jnp.zeros((16, 128), jnp.float32) for _ in pairs]
             for i in range(16):
@@ -660,8 +562,109 @@
             for n, (_, _, index) in enumerate(pairs):
                 note(3 * index + comp, fold((totals[n] + 0.5 * edges[n]) * count2))
 
-    weighted([(res, res, 0), (res, one, 1), (one, one, 2), (one, two, 3), (two, two, 4)])
-    energy(two, 5)
+    receive(one, 0)
+    operate(one, two, 1)
+    hear(1)
+    tell(2)
+    receive(two, 1)
+    products = [(res, res, 0), (res, one, 1), (one, one, 2), (one, two, 3), (two, two, 4)]
+    weighted(products, (1,))
+    energy(two, 5, (1,))
+    wait_bytes(plane_in, recv.at[0])
+    wait_bytes(verge_in, recv.at[5])
+    raw = {(-dw, -ds): plane_in[d] for d, (dw, ds) in enumerate(SHIFTS)}
+    raw[0, 0] = plane[...]
+    for d, (dw, ds) in enumerate(FAR_SHIFTS):
+        row = wide(verge_in[d])
+        if abs(dw) == 2:
+            value = pltpu.roll(row, 56 if dw > 0 else 16, 1, stride=8, stride_axis=0)
+        else:
+            value = pltpu.roll(row, 8 if ds > 0 else 113, 1, stride=1, stride_axis=0)
+        raw[-dw, -ds] = value
+    none = jnp.zeros((8, 128), jnp.float32)
+    square = [(dw, ds) for dw in (-1, 0, 1) for ds in (-1, 0, 1)]
+    cross = [(0, 0), (-1, 0), (1, 0), (0, -1), (0, 1)]
+
+    def spans(values, at):
+        dw, ds = at
+        return join_span(
+            values[at], values.get((dw, ds - 1), none), values.get((dw, ds + 1), none)
+        )
+
+    def walls(values, at):
+        dw, ds = at
+        return join_wall(
+            values[at], values.get((dw - 1, ds), none), values.get((dw + 1, ds), none)
+        )
+
+    def pulled(values):
+        fill = [none] * (len(values) % 2)
+        high, low = split(jnp.concatenate(list(values) + fill, axis=0))
+        product = jnp.dot(
+            jnp.concatenate([high, low, high], axis=1),
+            lines[...],
+            preferred_element_type=jnp.float32,
+        )
+        return [
+            (product[8 * n : 8 * n + 8, :128], product[8 * n : 8 * n + 8, 128:])
+            for n in range(len(values))
+        ]
+
+    mass_flat = table[LANEX] * table[LANEZ]
+
+    def plane_operator(in_x, in_z, value, at):
+        return (
+            table[LANEZ] * walls(in_x, at)
+            + table[LANEX] * spans(in_z, at)
+            + (SCALE * inverse_step) * mass_flat * value
+        )
+
+    line_of = {at: spans(raw, at) for at in square + [(-2, 0), (2, 0)]}
+    stress = {at: walls(line_of, at) for at in square}
+    pulls = pulled([stress[at] for at in square])
+    in_x = {at: pulls[n][0] for n, at in enumerate(square)}
+    in_z = {at: pulls[n][1] for n, at in enumerate(square)}
+    first = {at: plane_operator(in_x, in_z, stress[at], at) for at in cross}
+    mass_of = {at: mass_flat * stress[at] for at in cross}
+    pulls = pulled([first[at] for at in cross] + [mass_of[at] for at in cross])
+    seconds = []
+    for offset, values in ((0, first), (5, mass_of)):
+        in_x = {at: pulls[offset + n][0] for n, at in enumerate(cross)}
+        in_z = {at: pulls[offset + n][1] for n, at in enumerate(cross)}
+        seconds.append(plane_operator(in_x, in_z, values[0, 0], (0, 0)))
+
+    def raised(doubles, triples, rights, rows):
+        parts = []
+        for value in doubles:
+            parts += [coarse(value), value - coarse(value)]
+        for value in triples:
+            parts += [coarse(value), value - coarse(value), coarse(value)]
+        parts += [none] * (rows // 8 - len(parts))
+        return lax.dot_general(
+            jnp.concatenate(parts, axis=0),
+            rights[:rows],
+            (((0,), (0,)), ((), ())),
+            preferred_element_type=jnp.float32,
+        )
+
+    here, pull, mass_here = stress[0, 0], first[0, 0] * wall_mass, mass_of[0, 0]
+    lifted = raised([here], [], lifting, 16)
+    lifted_one = raised([pull], [mass_here], lifting, 48)
+    lifted_two = raised(
+        [seconds[0] * wall_mass * wall_mass],
+        [seconds[1], mass_flat * pull, mass_flat * mass_here],
+        lifting_two,
+        96,
+    )
+    for comp in range(2):
+        for ex in range(2):
+            column = (comp * 2 + ex) * 128
+            rows = slice(128 * ex, 128 * ex + 128)
+            for target, value in ((res, lifted), (one, lifted_one), (two, lifted_two)):
+                target[2 * comp, rows] = target[2 * comp, rows] + value[:, column : column + 128]
+
+    weighted(products, (0, 2))
+    energy(two, 5, (0, 2))
 
     mom[18:24, :] = jnp.zeros((6, 128), jnp.float32)
     total = jnp.sum(mom[...], axis=1, keepdims=True)

time: 40.8 us -> 40.7 us (level)
  no operation moved by 1% of the time
where the time goes in v8:
time: 40.7 us; the launch traced here: 40.5 us
  Pallas kernels  39.9 us (98%)
  between operations  0.64 us (2%)
    pallas_call x1, Pallas kernels, body(): pl.pallas_call(functools.partial(kernel, sizes), out_shape=(pltpu.VMEM((3...  39 us
    pallas_call x1, Pallas kernels, body(): pl.pallas_call(combine, out_shape=(jax.ShapeDtypeStruct((3, 16, 16, 128),...  0.86 us

profile of v8, /device:TPU:1, one launch (start us, length us, event | category | flops | bytes accessed | tf_op | source)
XLA Modules:
  0.0 40.5 jit_solution(6915623380237486392)
XLA Ops:
  0.6 39.0 %channel_step.1 = (f32[3,256,128]{2,1,0:T(8,128)S(1)}, f32[3,256,128]{2,1,0:T(8,128)S(1)}, f32[3,256,128]{2,1,0:T(8,128)S(1)}, f32[8,128]{1,0:T(8,128)S(1)}, f32[2,512]{1,0:T(2,128)S(1)}) custom-call(f32[3,16,16,128]{3,2,1,0:T(8,128)} %refs_0_.1, f32[16]{0:T(128)} %refs_1_.1, s32[1,512]{1,0:T(1,128)} %bitcast.3, s32[1,512]{1,0:T(1,128)} %bitcast.4, ...), custom_call_target="tpu_custom_call" | custom-call | tf_op jit(solution)/shard_map/channel_step/pallas_call | solution.py:784
  39.7 0.9 %combine.1 = (f32[3,16,16,128]{3,2,1,0:T(8,128)}, f32[2,512]{1,0:T(2,128)}) custom-call(f32[3,256,128]{2,1,0:T(8,128)S(1)} %get-tuple-element.7.res, f32[3,256,128]{2,1,0:T(8,128)S(1)} %get-tuple-element.8.one, f32[3,256,128]{2,1,0:T(8,128)S(1)} %get-tuple-element.9.two, f32[8,128]{1,0:T(8,128)S(1)} %get-tuple-element.10.scalars, ...), custom_call_target="tpu_custom_call" | custom-call | tf_op jit(solution)/shard_map/combine/pallas_call | solution.py:840

commit v9 on v8

--- a/solution.py
+++ b/solution.py
@@ -131,14 +131,14 @@
     line = np.concatenate([np.kron(line_x.T, np.eye(16)), np.kron(np.eye(16), line_z.T)], axis=1)
     line_high = line.astype(np.float32).astype(jnp.bfloat16)
     line_low = (line.astype(np.float32) - line_high.astype(np.float32)).astype(jnp.bfloat16)
-    lines = np.concatenate([line_high, line_high, line_low])
+    lines = np.concatenate([line_high, line_low])
     rows += [
         ones * (mass_x * ends)[lane // 16][None, :],
         ones * (mass_z * ends)[lane % 8][None, :],
     ]
     pieces = [np.stack(rows), block.reshape(16, 8, 128), lift.reshape(8, 4, 128).transpose(1, 0, 2)]
     pieces += [joined_x[:, None, None] * (mass_z * ends)[None, :, None] * np.ones((16, 8, 128))]
-    return np.concatenate(pieces).astype(np.float32), np.stack([flat_high, flat_low]), lines
+    return np.concatenate(pieces).astype(np.float32), np.concatenate([flat_high, flat_low]), lines
 
 
 def kernel(sizes, *refs):
@@ -146,7 +146,7 @@
     (res, one, two, scalars, neumann), refs = refs[:5], refs[5:]
     local, refs = refs[:9], refs[9:]
     velocity, heights, owner, element, coords, roughness, table, flat, lines = local
-    (normal, lifting, lifting_two, right_high, right_low, slab, slab_in, plane, plane_in,
+    (normal, lifting, lifting_two, right, slab, slab_in, plane, plane_in,
      verge, verge_in, face, face_in, mom, part, part_in,
      load, send, slab_recv, recv, ready) = refs
     nx, ny, nc, ns = sizes
@@ -282,13 +282,28 @@
         high = value.astype(jnp.bfloat16)
         return high, (value - high.astype(jnp.float32)).astype(jnp.bfloat16)
 
+    def split_product(left, right):
+        rows = left.shape[0]
+        high, low = split(left)
+        product = jnp.dot(
+            jnp.concatenate(
+                [
+                    jnp.concatenate([high, high], axis=1),
+                    jnp.concatenate([low, jnp.zeros_like(low)], axis=1),
+                ],
+                axis=0,
+            ),
+            right,
+            preferred_element_type=jnp.float32,
+        )
+        return product[:rows] + product[rows:]
+
     block_high, block_low = split(block)
     normal[:128, :128] = block_high
     normal[128:, :128] = block_high
     normal[:128, 128:] = block_low
     normal[128:, 128:] = jnp.zeros((128, 128), jnp.bfloat16)
-    right_high[...] = jnp.zeros(right_high.shape, jnp.bfloat16)
-    right_low[...] = jnp.zeros(right_low.shape, jnp.bfloat16)
+    right[...] = jnp.zeros(right.shape, jnp.bfloat16)
     side = sub8 // 2 % 2
     wall_row = jnp.where(side == 0, block[:1], block[127:])
     lift = jnp.concatenate([table[LIFT + k] for k in range(4)], axis=1)
@@ -342,9 +357,8 @@
     def apply(source, comp):
         high, low = split(source[comp])
         parts = jnp.concatenate([high, low], axis=1)
-        along = jnp.dot(flat[0], parts, preferred_element_type=jnp.float32)
-        along = along[:, :128] + along[:, 128:]
-        along = along + jnp.dot(flat[1], high, preferred_element_type=jnp.float32)
+        product = jnp.dot(flat[...], parts, preferred_element_type=jnp.float32)
+        along = product[:320, :128] + product[:320, 128:] + product[320:, :128]
         across_y = jnp.dot(parts, normal[...], preferred_element_type=jnp.float32)
         return along, across_y[:, :128] + across_y[:, 128:]
 
@@ -412,19 +426,16 @@
         for kk in range(2):
             k = 2 * (g // 2) + kk
             column = slice(128 * kk, 128 * kk + 128)
-            right_high[g, 32 * k : 32 * k + 32, column] = high
-            right_high[g, 128 + 32 * k : 160 + 32 * k, column] = high
-            right_low[g, 32 * k : 32 * k + 32, column] = low
+            right[g, 32 * k : 32 * k + 32, column] = high
+            right[g, 128 + 32 * k : 160 + 32 * k, column] = low
 
     masks = [[1.0 - to_next[g] - to_prev[g], to_prev[g], to_next[g]] for g in range(4)]
 
     def sample(source, g):
         ez = g % 2
-        high, low = split(source[:, :, 8 * ez : 8 * ez + 8, :].reshape(64, 128))
-        product = jnp.dot(
-            jnp.concatenate([high, low], axis=1), right_high[g],
-            preferred_element_type=jnp.float32,
-        ) + jnp.dot(high, right_low[g], preferred_element_type=jnp.float32)
+        product = split_product(
+            source[:, :, 8 * ez : 8 * ez + 8, :].reshape(64, 128), right[g]
+        )
         total = [jnp.zeros((8, 128), jnp.float32) for _ in range(2)]
         for kk in range(2):
             values = product[:, 128 * kk : 128 * kk + 128].reshape(2, 4, 8, 128)
@@ -599,12 +610,7 @@
 
     def pulled(values):
         fill = [none] * (len(values) % 2)
-        high, low = split(jnp.concatenate(list(values) + fill, axis=0))
-        product = jnp.dot(
-            jnp.concatenate([high, low, high], axis=1),
-            lines[...],
-            preferred_element_type=jnp.float32,
-        )
+        product = split_product(jnp.concatenate(list(values) + fill, axis=0), lines[...])
         return [
             (product[8 * n : 8 * n + 8, :128], product[8 * n : 8 * n + 8, 128:])
             for n in range(len(values))
@@ -806,7 +812,6 @@
             pltpu.VMEM((48, 512), f32),
             pltpu.VMEM((96, 512), f32),
             pltpu.VMEM((4, 256, 256), jnp.bfloat16),
-            pltpu.VMEM((4, 128, 256), jnp.bfloat16),
             pltpu.VMEM((2, 4, 16, 128), f32),
             pltpu.VMEM((2, 2, 4, 16, 128), f32),
             pltpu.VMEM((8, 128), f32),

time: 40.7 us -> 41 us (level)
  no operation moved by 1% of the time
where the time goes in v9:
time: 41 us; the launch traced here: 40.9 us
  Pallas kernels  40.2 us (98%)
  between operations  0.64 us (2%)
    pallas_call x1, Pallas kernels, body(): pl.pallas_call(functools.partial(kernel, sizes), out_shape=(pltpu.VMEM((3...  39.4 us
    pallas_call x1, Pallas kernels, body(): pl.pallas_call(combine, out_shape=(jax.ShapeDtypeStruct((3, 16, 16, 128),...  0.86 us

profile of v9, /device:TPU:1, one launch (start us, length us, event | category | flops | bytes accessed | tf_op | source)
XLA Modules:
  0.0 40.9 jit_solution(11959862753019055279)
XLA Ops:
  0.6 39.4 %channel_step.1 = (f32[3,256,128]{2,1,0:T(8,128)S(1)}, f32[3,256,128]{2,1,0:T(8,128)S(1)}, f32[3,256,128]{2,1,0:T(8,128)S(1)}, f32[8,128]{1,0:T(8,128)S(1)}, f32[2,512]{1,0:T(2,128)S(1)}) custom-call(f32[3,16,16,128]{3,2,1,0:T(8,128)} %refs_0_.1, f32[16]{0:T(128)} %refs_1_.1, s32[1,512]{1,0:T(1,128)} %bitcast.3, s32[1,512]{1,0:T(1,128)} %bitcast.4, ...), custom_call_target="tpu_custom_call" | custom-call | tf_op jit(solution)/shard_map/channel_step/pallas_call | solution.py:790
  40.0 0.9 %combine.1 = (f32[3,16,16,128]{3,2,1,0:T(8,128)}, f32[2,512]{1,0:T(2,128)}) custom-call(f32[3,256,128]{2,1,0:T(8,128)S(1)} %get-tuple-element.7.res, f32[3,256,128]{2,1,0:T(8,128)S(1)} %get-tuple-element.8.one, f32[3,256,128]{2,1,0:T(8,128)S(1)} %get-tuple-element.9.two, f32[8,128]{1,0:T(8,128)S(1)} %get-tuple-element.10.scalars, ...), custom_call_target="tpu_custom_call" | custom-call | tf_op jit(solution)/shard_map/combine/pallas_call | solution.py:845

commit v10 on v9

--- a/solution.py
+++ b/solution.py
@@ -138,7 +138,7 @@
     ]
     pieces = [np.stack(rows), block.reshape(16, 8, 128), lift.reshape(8, 4, 128).transpose(1, 0, 2)]
     pieces += [joined_x[:, None, None] * (mass_z * ends)[None, :, None] * np.ones((16, 8, 128))]
-    return np.concatenate(pieces).astype(np.float32), np.concatenate([flat_high, flat_low]), lines
+    return np.concatenate(pieces).astype(np.float32), np.stack([flat_high, flat_low]), lines
 
 
 def kernel(sizes, *refs):
@@ -258,12 +258,6 @@
             packed = jnp.where(where_to // 16 == 2 * k, low, packed)
             packed = jnp.where(where_to // 16 == 2 * k + 1, high, packed)
         slab[comp] = packed.reshape(4, 16, 128)
-
-    pl.semaphore_wait(barrier, len(near))
-
-    tell(0)
-    for d in range(2):
-        push(slab, slab_in.at[d], send.at[0], slab_recv.at[d], neighbours[d])
 
     for copy in loads[1:]:
         copy.wait()
@@ -357,10 +351,17 @@
     def apply(source, comp):
         high, low = split(source[comp])
         parts = jnp.concatenate([high, low], axis=1)
-        product = jnp.dot(flat[...], parts, preferred_element_type=jnp.float32)
-        along = product[:320, :128] + product[:320, 128:] + product[320:, :128]
+        along = jnp.dot(flat[0], parts, preferred_element_type=jnp.float32)
+        along = along[:, :128] + along[:, 128:]
+        along = along + jnp.dot(flat[1], high, preferred_element_type=jnp.float32)
         across_y = jnp.dot(parts, normal[...], preferred_element_type=jnp.float32)
         return along, across_y[:, :128] + across_y[:, 128:]
+
+    def send_face(turn, d, comp):
+        push(
+            face.at[turn, d, comp], face_in.at[turn, d, comp], send.at[2 + turn],
+            recv.at[1 + turn], neighbours[d],
+        )
 
     def operate(source, target, turn):
         for comp in range(3):
@@ -368,10 +369,8 @@
             for d in range(4):
                 rows = slice(256 + 16 * d, 272 + 16 * d)
                 face[turn, d, comp] = along[rows] * joined_y2
-                push(
-                    face.at[turn, d, comp], face_in.at[turn, d, comp], send.at[2 + turn],
-                    recv.at[1 + turn], neighbours[d],
-                )
+                if turn:
+                    send_face(turn, d, comp)
             for i in range(16):
                 rows = slice(16 * i, 16 * i + 16)
                 target[comp, rows] = along[rows] * joined_y2 + across_y[rows] * both(
@@ -379,6 +378,15 @@
                 )
 
     operate(res, one, 0)
+    pl.semaphore_wait(barrier, len(near))
+
+    tell(0)
+    for d in range(2):
+        push(slab, slab_in.at[d], send.at[0], slab_recv.at[d], neighbours[d])
+    for comp in range(3):
+        for d in range(4):
+            send_face(0, d, comp)
+
     def regroup(blocks):
         upper = (lane // 8) % 2 == 1
         result = []

time: 41 us -> 40.4 us (0.985)
  Pallas kernels: 40.2 us -> 39.7 us
    pallas_call x1, Pallas kernels: 39.4 us -> 38.8 us  [body(): pl.pallas_call(functools.partial(kernel, sizes), out_shape=(pltpu.VMEM((3...]
where the time goes in v10:
time: 40.4 us; the launch traced here: 40.3 us
  Pallas kernels  39.7 us (98%)
  between operations  0.64 us (2%)
    pallas_call x1, Pallas kernels, body(): pl.pallas_call(functools.partial(kernel, sizes), out_shape=(pltpu.VMEM((3...  38.8 us
    pallas_call x1, Pallas kernels, body(): pl.pallas_call(combine, out_shape=(jax.ShapeDtypeStruct((3, 16, 16, 128),...  0.86 us

profile of v10, /device:TPU:1, one launch (start us, length us, event | category | flops | bytes accessed | tf_op | source)
XLA Modules:
  0.0 40.3 jit_solution(4854670553904027735)
XLA Ops:
  0.6 38.8 %channel_step.1 = (f32[3,256,128]{2,1,0:T(8,128)S(1)}, f32[3,256,128]{2,1,0:T(8,128)S(1)}, f32[3,256,128]{2,1,0:T(8,128)S(1)}, f32[8,128]{1,0:T(8,128)S(1)}, f32[2,512]{1,0:T(2,128)S(1)}) custom-call(f32[3,16,16,128]{3,2,1,0:T(8,128)} %refs_0_.1, f32[16]{0:T(128)} %refs_1_.1, s32[1,512]{1,0:T(1,128)} %bitcast.3, s32[1,512]{1,0:T(1,128)} %bitcast.4, ...), custom_call_target="tpu_custom_call" | custom-call | tf_op jit(solution)/shard_map/channel_step/pallas_call | solution.py:798
  39.4 0.9 %combine.1 = (f32[3,16,16,128]{3,2,1,0:T(8,128)}, f32[2,512]{1,0:T(2,128)}) custom-call(f32[3,256,128]{2,1,0:T(8,128)S(1)} %get-tuple-element.7.res, f32[3,256,128]{2,1,0:T(8,128)S(1)} %get-tuple-element.8.one, f32[3,256,128]{2,1,0:T(8,128)S(1)} %get-tuple-element.9.two, f32[8,128]{1,0:T(8,128)S(1)} %get-tuple-element.10.scalars, ...), custom_call_target="tpu_custom_call" | custom-call | tf_op jit(solution)/shard_map/combine/pallas_call | solution.py:853

commit v11 on v10

--- a/solution.py
+++ b/solution.py
@@ -349,13 +349,20 @@
         return value[:8] + value[8:]
 
     def apply(source, comp):
-        high, low = split(source[comp])
-        parts = jnp.concatenate([high, low], axis=1)
-        along = jnp.dot(flat[0], parts, preferred_element_type=jnp.float32)
-        along = along[:, :128] + along[:, 128:]
-        along = along + jnp.dot(flat[1], high, preferred_element_type=jnp.float32)
-        across_y = jnp.dot(parts, normal[...], preferred_element_type=jnp.float32)
-        return along, across_y[:, :128] + across_y[:, 128:]
+        return apply_all(source, (comp,))[0]
+
+    def apply_all(source, comps):
+        halves = [split(source[comp]) for comp in comps]
+        highs = jnp.concatenate([high for high, _ in halves], axis=1)
+        small = jnp.dot(flat[1], highs, preferred_element_type=jnp.float32)
+        result = []
+        for n, (high, low) in enumerate(halves):
+            parts = jnp.concatenate([high, low], axis=1)
+            along = jnp.dot(flat[0], parts, preferred_element_type=jnp.float32)
+            along = along[:, :128] + along[:, 128:] + small[:, 128 * n : 128 * n + 128]
+            across_y = jnp.dot(parts, normal[...], preferred_element_type=jnp.float32)
+            result.append((along, across_y[:, :128] + across_y[:, 128:]))
+        return result
 
     def send_face(turn, d, comp):
         push(
@@ -380,12 +387,12 @@
     operate(res, one, 0)
     pl.semaphore_wait(barrier, len(near))
 
-    tell(0)
     for d in range(2):
         push(slab, slab_in.at[d], send.at[0], slab_recv.at[d], neighbours[d])
     for comp in range(3):
         for d in range(4):
             send_face(0, d, comp)
+    tell(0)
 
     def regroup(blocks):
         upper = (lane // 8) % 2 == 1
@@ -542,8 +549,7 @@
         mom[k : k + 1, :] = jnp.sum(value, axis=0, keepdims=True)
 
     def energy(source, index, comps):
-        for comp in comps:
-            along, across_y = apply(source, comp)
+        for comp, (along, across_y) in zip(comps, apply_all(source, comps)):
             inside = jnp.zeros((16, 128), jnp.float32)
             edges = jnp.zeros((16, 128), jnp.float32)
             for i in range(16):

time: 40.4 us -> 40.4 us (level)
  no operation moved by 1% of the time
where the time goes in v11:
time: 40.4 us; the launch traced here: 40.3 us
  Pallas kernels  39.6 us (98%)
  between operations  0.64 us (2%)
    pallas_call x1, Pallas kernels, body(): pl.pallas_call(functools.partial(kernel, sizes), out_shape=(pltpu.VMEM((3...  38.8 us
    pallas_call x1, Pallas kernels, body(): pl.pallas_call(combine, out_shape=(jax.ShapeDtypeStruct((3, 16, 16, 128),...  0.86 us

profile of v11, /device:TPU:1, one launch (start us, length us, event | category | flops | bytes accessed | tf_op | source)
XLA Modules:
  0.0 40.3 jit_solution(17948903854969556294)
XLA Ops:
  0.6 38.8 %channel_step.1 = (f32[3,256,128]{2,1,0:T(8,128)S(1)}, f32[3,256,128]{2,1,0:T(8,128)S(1)}, f32[3,256,128]{2,1,0:T(8,128)S(1)}, f32[8,128]{1,0:T(8,128)S(1)}, f32[2,512]{1,0:T(2,128)S(1)}) custom-call(f32[3,16,16,128]{3,2,1,0:T(8,128)} %refs_0_.1, f32[16]{0:T(128)} %refs_1_.1, s32[1,512]{1,0:T(1,128)} %bitcast.3, s32[1,512]{1,0:T(1,128)} %bitcast.4, ...), custom_call_target="tpu_custom_call" | custom-call | tf_op jit(solution)/shard_map/channel_step/pallas_call | solution.py:804
  39.4 0.9 %combine.1 = (f32[3,16,16,128]{3,2,1,0:T(8,128)}, f32[2,512]{1,0:T(2,128)}) custom-call(f32[3,256,128]{2,1,0:T(8,128)S(1)} %get-tuple-element.7.res, f32[3,256,128]{2,1,0:T(8,128)S(1)} %get-tuple-element.8.one, f32[3,256,128]{2,1,0:T(8,128)S(1)} %get-tuple-element.9.two, f32[8,128]{1,0:T(8,128)S(1)} %get-tuple-element.10.scalars, ...), custom_call_target="tpu_custom_call" | custom-call | tf_op jit(solution)/shard_map/combine/pallas_call | solution.py:859

commit v12 on v10

--- a/solution.py
+++ b/solution.py
@@ -380,9 +380,9 @@
     operate(res, one, 0)
     pl.semaphore_wait(barrier, len(near))
 
-    tell(0)
     for d in range(2):
         push(slab, slab_in.at[d], send.at[0], slab_recv.at[d], neighbours[d])
+    tell(0)
     for comp in range(3):
         for d in range(4):
             send_face(0, d, comp)

time: 40.4 us -> 40.4 us (level)
  no operation moved by 1% of the time
where the time goes in v12:
time: 40.4 us; the launch traced here: 40.3 us
  Pallas kernels  39.6 us (98%)
  between operations  0.64 us (2%)
    pallas_call x1, Pallas kernels, body(): pl.pallas_call(functools.partial(kernel, sizes), out_shape=(pltpu.VMEM((3...  38.8 us
    pallas_call x1, Pallas kernels, body(): pl.pallas_call(combine, out_shape=(jax.ShapeDtypeStruct((3, 16, 16, 128),...  0.86 us

profile of v12, /device:TPU:1, one launch (start us, length us, event | category | flops | bytes accessed | tf_op | source)
XLA Modules:
  0.0 40.3 jit_solution(10445653189927295415)
XLA Ops:
  0.6 38.8 %channel_step.1 = (f32[3,256,128]{2,1,0:T(8,128)S(1)}, f32[3,256,128]{2,1,0:T(8,128)S(1)}, f32[3,256,128]{2,1,0:T(8,128)S(1)}, f32[8,128]{1,0:T(8,128)S(1)}, f32[2,512]{1,0:T(2,128)S(1)}) custom-call(f32[3,16,16,128]{3,2,1,0:T(8,128)} %refs_0_.1, f32[16]{0:T(128)} %refs_1_.1, s32[1,512]{1,0:T(1,128)} %bitcast.3, s32[1,512]{1,0:T(1,128)} %bitcast.4, ...), custom_call_target="tpu_custom_call" | custom-call | tf_op jit(solution)/shard_map/channel_step/pallas_call | solution.py:798
  39.4 0.9 %combine.1 = (f32[3,16,16,128]{3,2,1,0:T(8,128)}, f32[2,512]{1,0:T(2,128)}) custom-call(f32[3,256,128]{2,1,0:T(8,128)S(1)} %get-tuple-element.7.res, f32[3,256,128]{2,1,0:T(8,128)S(1)} %get-tuple-element.8.one, f32[3,256,128]{2,1,0:T(8,128)S(1)} %get-tuple-element.9.two, f32[8,128]{1,0:T(8,128)S(1)} %get-tuple-element.10.scalars, ...), custom_call_target="tpu_custom_call" | custom-call | tf_op jit(solution)/shard_map/combine/pallas_call | solution.py:853
